TPU v7x, 256 devices: a whole 4x4x8 slice. The times are simulated.
256 devices in a mesh: section: 4 (over y), space: 64 (over z, x, core).
Axes of the slice: x: 4, y: 4, z: 8, core: 2. Of those that a mesh axis runs over, the one named last changes fastest.
Arguments:
- start_state: float32 [8, 6, 512, 512], P(None, None, 'space'), may hold values from -6 to 6
- stiffness: float32 [2, 512, 512], P(None, 'space'), may hold values from 0.5 to 4
- contact_a: int32 [8, 64, 8], P('section', 'space'), may hold values from 0 to 31
- contact_b: int32 [8, 64, 8], P('section', 'space'), may hold values from 0 to 39
- pair_count: int32 [8, 64], P('section', 'space'), may hold values from 1 to 8, 260 in all within a row
- cotangent: float32 [8, 6, 512, 512], P(None, None, 'space'), may hold values from -6 to 6
Outputs:
- exit_state: float32 [4, 8, 6, 512, 512], P('section', None, None, 'space')
- incoming_state_gradient: float32 [4, 8, 6, 512, 512], P('section', None, None, 'space')
- stiffness_grad: float32 [2, 512, 512], P(None, 'space')
Inputs may be any that keep to these rules, and one draw needn't show every extreme that they name: Tiles are numbered within one device's band: contact_a over its own 8 rows, contact_b over those rows with one row added above and below, the upper added row first. Slots at or beyond pair_count are ignored; at every step some device has all 8 slots live.
All inputs are finite; a program needn't handle non-finite values.
Results may differ from a plain program's by a relative error of at most 0.0003.
Values sent between devices are 32-bit elements; how exact they have to be, the bound alone decides.
No kernel may reach another device: no remote copies, remote signals or barrier semaphores. Data moves between devices by JAX's collectives and lax.ppermute only.
A program may use at most 64 MiB of HBM per device.

v0:
```python
import math

import jax
import jax.numpy as jnp
from jax import lax
from jax.sharding import PartitionSpec as P

time_step = 0.1
damping = 0.98
rest_length = 1.0
contact_scale = 0.3
kernel_spread = 2.0
gravity = 0.5
tiny_length = 1e-06


def passed_along(value, axis, by):
    size = lax.axis_size(axis)
    pairs = [(i, i + by) for i in range(size) if 0 <= i + by < size]
    return lax.ppermute(value, axis, pairs)


def padded(value, sides, width):
    for axis, dim in sides:
        size, length = (lax.axis_size(axis), value.shape[dim])
        up = [(i, (i + 1) % size) for i in range(size - 1)]
        down = [(j, i) for i, j in up]
        last = lax.slice_in_dim(value, length - width, length, axis=dim)
        first = lax.slice_in_dim(value, 0, width, axis=dim)
        before = lax.ppermute(last, axis, up)
        after = lax.ppermute(first, axis, down)
        value = jnp.concatenate([before, value, after], axis=dim)
    return value


def sent_together(arrays, axis, dim, along):
    widths = [math.prod(a.shape[along:]) for a in arrays]
    both = jnp.concatenate(
        [a.reshape(*a.shape[:along], w) for a, w in zip(arrays, widths)], axis=along
    )
    filled = lax.all_gather(both, axis, axis=dim, tiled=True)
    tiles = jnp.split(filled, [sum(widths[:k]) for k in range(1, len(widths))], axis=along)
    return tuple(
        (b.reshape(*filled.shape[:along], *a.shape[along:]) for a, b in zip(arrays, tiles))
    )


def side_by_side(arrays, axis, split_dim, concat_dim, along):
    both = jnp.concatenate(arrays, axis=along)
    filled, at, finished = (
        lax.all_to_all(both, axis, split_axis=split_dim, concat_axis=concat_dim, tiled=True),
        0,
        [],
    )
    for a in arrays:
        finished.append(lax.slice_in_dim(filled, at, at + a.shape[along], axis=along))
        at += a.shape[along]
    return tuple(finished)


def spring(offset, edge_constant):
    length = jnp.sqrt(jnp.sum(offset * offset, axis=0) + tiny_length)
    return (edge_constant * (length - rest_length) / length)[None] * offset


def contact(points, extended, hits_a, hits_b, active):
    tiles_own = points.reshape(3, -1, 128)
    tiles_all = extended.reshape(3, -1, 128)
    own_points = jnp.einsum("pt,ctk->cpk", hits_a, tiles_own, precision=lax.Precision.HIGHEST)
    other_points = jnp.einsum("pt,ctk->cpk", hits_b, tiles_all, precision=lax.Precision.HIGHEST)
    separation = own_points[:, :, :, None] - other_points[:, :, None, :]
    spring_weights = (
        jnp.exp(-jnp.sum(separation * separation, axis=0) / kernel_spread) * active[:, None, None]
    )
    repulsion = (
        2.0 * contact_scale / kernel_spread * jnp.sum(spring_weights[None] * separation, axis=3)
    )
    placed = jnp.einsum("pt,cpk->ctk", hits_a, repulsion, precision=lax.Precision.HIGHEST)
    return placed.reshape(points.shape)


def local_step(extended, velocity, stiff_row, stiff_column, hits_a, hits_b, active):
    points = extended[:, 1:-1]
    row_width = points.shape[2]
    column_mask = (lax.broadcasted_iota(jnp.int32, (1, row_width), 1) < row_width - 1).astype(
        stiff_row.dtype
    )
    right_edge = stiff_row * column_mask
    left_edge = jnp.pad(right_edge[:, :-1], ((0, 0), (1, 0)))
    right_points = jnp.pad(points[:, :, 1:], ((0, 0), (0, 0), (0, 1)))
    left_points = jnp.pad(points[:, :, :-1], ((0, 0), (0, 0), (1, 0)))
    total_force = spring(right_points - points, right_edge) + spring(
        left_points - points, left_edge
    )
    total_force = total_force + spring(extended[:, :-2] - points, stiff_column[:-1])
    total_force = total_force + spring(extended[:, 2:] - points, stiff_column[1:])
    total_force = total_force + contact(points, extended, hits_a, hits_b, active)
    gravity_pull = jnp.zeros((3, 1, 1), total_force.dtype).at[2].set(-gravity)
    velocity_new = damping * (velocity + time_step * (total_force + gravity_pull))
    points_new = points + time_step * velocity_new
    return jnp.concatenate([points_new, velocity_new], axis=0)


def tables(first_tiles, second_tiles, live_count, tiles_own, tiles_all):
    slot_count = first_tiles.shape[0]
    hits_a = (
        first_tiles[:, None] == lax.broadcasted_iota(jnp.int32, (slot_count, tiles_own), 1)
    ).astype(jnp.float32)
    hits_b = (
        second_tiles[:, None] == lax.broadcasted_iota(jnp.int32, (slot_count, tiles_all), 1)
    ).astype(jnp.float32)
    active = (lax.iota(jnp.int32, slot_count) < live_count).astype(jnp.float32)
    return (hits_a, hits_b, active)


def on_device(start_state, stiffness, contact_a, contact_b, pair_count, cotangent):
    sections = lax.axis_size("section")
    section_index = lax.axis_index("section")
    space_index = lax.axis_index("space")
    micro_count, _, own_rows, row_width = start_state.shape
    steps_section = contact_a.shape[0]
    tiles_own = own_rows * row_width // 128
    tiles_all = (own_rows + 2) * row_width // 128
    total_rows = own_rows * lax.axis_size("space")
    global_rows = space_index * own_rows + lax.iota(jnp.int32, own_rows)
    row_mask = (global_rows < total_rows - 1).astype(jnp.float32)[:, None]
    stiff_row = stiffness[0]
    stiff_own = stiffness[1] * row_mask
    stiff_above = passed_along(stiff_own[-1:], "space", 1)
    stiff_column = jnp.concatenate([stiff_above, stiff_own], axis=0)
    batch_step = jax.vmap(local_step, in_axes=(0, 0, None, None, None, None, None))

    def extend(points):
        return padded(points, (("space", 2),), 1)

    def back_step(table, extended, velocity, adjoint):
        hits_a, hits_b, active = table

        def forward_one(extended_in, velocity_in, row_in, column_in):
            return batch_step(extended_in, velocity_in, row_in, column_in, hits_a, hits_b, active)

        _, pullback = jax.vjp(forward_one, extended, velocity, stiff_row, stiff_column)
        grad_extended, grad_velocity, part_row, part_column = pullback(adjoint)
        edge_rows = jnp.stack([grad_extended[:, :, 0], grad_extended[:, :, -1]], axis=2)
        neighbour = padded(edge_rows, (("space", 2),), 1)
        interior = grad_extended[:, :, 1:-1]
        interior = interior.at[:, :, 0].add(neighbour[:, :, 0]).at[:, :, -1].add(neighbour[:, :, 3])
        return (jnp.concatenate([interior, grad_velocity], axis=1), part_row, part_column)

    first_all, second_all, count_all = sent_together(
        (contact_a, contact_b, pair_count), "section", 0, 2
    )
    share = micro_count // sections
    own_start = lax.dynamic_slice_in_dim(start_state, section_index * share, share, 0)
    own_cotangent = lax.dynamic_slice_in_dim(cotangent, section_index * share, share, 0)
    numbers = jnp.arange(steps_section * sections, dtype=jnp.int32)

    def table_at(section_total):
        return tables(
            first_all[section_total, 0],
            second_all[section_total, 0],
            count_all[section_total, 0],
            tiles_own,
            tiles_all,
        )

    def forward_step(state_now, section_total):
        extended = extend(state_now[:, :3])
        hits_a, hits_b, active = table_at(section_total)
        moved = batch_step(
            extended, state_now[:, 3:], stiff_row, stiff_column, hits_a, hits_b, active
        )
        return (moved, (moved, extended, state_now[:, 3:]))

    _, (after_all, extended_all, velocity_all) = lax.scan(forward_step, own_start, numbers)

    def backward_step(carried, inputs):
        adjoint, grad_row, grad_column = carried
        section_total, extended, velocity = inputs
        adjoint, part_row, part_column = back_step(
            table_at(section_total), extended, velocity, adjoint
        )
        return ((adjoint, grad_row + part_row, grad_column + part_column), adjoint)

    start_carry = (own_cotangent, jnp.zeros_like(stiff_row), jnp.zeros_like(stiff_column))
    (_, grad_row, grad_column), before_all = lax.scan(
        backward_step, start_carry, (numbers, extended_all, velocity_all), reverse=True
    )
    exit_local = after_all[steps_section - 1 :: steps_section]
    adjoint_local = before_all[::steps_section]
    exit_result, resulting_adjoint = side_by_side((exit_local, adjoint_local), "section", 0, 1, 2)
    upper_part = passed_along(grad_column[:1], "space", -1)
    column_own = grad_column[1:].at[-1].add(upper_part[0]) * row_mask
    summed_row, summed_column = lax.psum((grad_row, column_own), "section")
    return (exit_result, resulting_adjoint, jnp.stack([summed_row, summed_column]))


def solution(mesh):
    in_specs = (
        P(None, None, "space", None),
        P(None, "space", None),
        P("section", "space", None),
        P("section", "space", None),
        P("section", "space"),
        P(None, None, "space", None),
    )
    out_specs = (
        P("section", None, None, "space", None),
        P("section", None, None, "space", None),
        P(None, "space", None),
    )
    return jax.shard_map(
        on_device, mesh=mesh, in_specs=in_specs, out_specs=out_specs, check_vma=False
    )
```

profile of v0, /device:TPU:102, one launch (start us, length us, event | category | flops | bytes accessed | tf_op | source)
XLA Modules:
  0.0 388.3 jit_solution(6915735155054566221)
XLA Ops:
  5.6 10.0 %all_gather.3 = s32[8,1,17]{2,1,0:T(1,128)S(1)} all-gather(s32[2,1,17]{2,1,0:T(1,128)S(1)} %pad_add_fusion.2), channel_id=1, replica_groups=mesh['section'=4,'space'=64] {'section'}, dimensions={0}, use_global_device_ids=true | all-gather | bytes 680 | tf_op jit(solution)/shard_map/all_gather | solution.py:41
  17.3 140.9 %while.43 = (s32[]{:T(128)}, f32[2,6,8,512]{3,2,1,0:T(8,128)S(1)}, f32[8,2,6,8,512]{4,3,2,1,0:T(8,128)S(1)}, f32[8,2,3,10,512]{4,3,2,1,0:T(8,128)}, f32[8,512]{1...) while((s32[]{:T(128)}, f32[2,6,8,512]{3,2,1,0:T(8,128)S(1)}, ...), condition=%wide.region_7.8_spmd, body=%wide.region_0.7_spmd.sunk | while | flops 14022485 | bytes 9260103 | solution.py:175
  19.3 3.0 collective-permute-start.1
  34.0 6.4 %collective-permute-start.1 = (f32[2,3,1,512]{3,2,1,0:T(1,128)S(1)}, f32[2,3,1,512]{3,2,1,0:T(1,128)S(1)}, u32[]{:S(2)}, u32[]{:S(2)}) collective-permute-start(f32[2,3,1,512]{3,2,1,0:T(1,128)S(1)} %get-tuple-element.910), channel_id=1, source_target_pairs={{0,1},{1,2},{2,3},{3,4},{4,5},{5,6},{6,7},{7,8},{8,9},{9,10},{10,1... | collective-permute-start | bytes 36872 | tf_op jit(solution)/shard_map/while/body/eval_jaxpr/ppermute | solution.py:30
  51.5 7.0 %collective-permute-start.1 = (f32[2,3,1,512]{3,2,1,0:T(1,128)S(1)}, f32[2,3,1,512]{3,2,1,0:T(1,128)S(1)}, u32[]{:S(2)}, u32[]{:S(2)}) collective-permute-start(f32[2,3,1,512]{3,2,1,0:T(1,128)S(1)} %get-tuple-element.910), channel_id=1, source_target_pairs={{0,1},{1,2},{2,3},{3,4},{4,5},{5,6},{6,7},{7,8},{8,9},{9,10},{10,1... | collective-permute-start | bytes 36872 | tf_op jit(solution)/shard_map/while/body/eval_jaxpr/ppermute | solution.py:30
  69.6 7.0 %collective-permute-start.1 = (f32[2,3,1,512]{3,2,1,0:T(1,128)S(1)}, f32[2,3,1,512]{3,2,1,0:T(1,128)S(1)}, u32[]{:S(2)}, u32[]{:S(2)}) collective-permute-start(f32[2,3,1,512]{3,2,1,0:T(1,128)S(1)} %get-tuple-element.910), channel_id=1, source_target_pairs={{0,1},{1,2},{2,3},{3,4},{4,5},{5,6},{6,7},{7,8},{8,9},{9,10},{10,1... | collective-permute-start | bytes 36872 | tf_op jit(solution)/shard_map/while/body/eval_jaxpr/ppermute | solution.py:30
  87.7 7.0 %collective-permute-start.1 = (f32[2,3,1,512]{3,2,1,0:T(1,128)S(1)}, f32[2,3,1,512]{3,2,1,0:T(1,128)S(1)}, u32[]{:S(2)}, u32[]{:S(2)}) collective-permute-start(f32[2,3,1,512]{3,2,1,0:T(1,128)S(1)} %get-tuple-element.910), channel_id=1, source_target_pairs={{0,1},{1,2},{2,3},{3,4},{4,5},{5,6},{6,7},{7,8},{8,9},{9,10},{10,1... | collective-permute-start | bytes 36872 | tf_op jit(solution)/shard_map/while/body/eval_jaxpr/ppermute | solution.py:30
  105.8 7.0 %collective-permute-start.1 = (f32[2,3,1,512]{3,2,1,0:T(1,128)S(1)}, f32[2,3,1,512]{3,2,1,0:T(1,128)S(1)}, u32[]{:S(2)}, u32[]{:S(2)}) collective-permute-start(f32[2,3,1,512]{3,2,1,0:T(1,128)S(1)} %get-tuple-element.910), channel_id=1, source_target_pairs={{0,1},{1,2},{2,3},{3,4},{4,5},{5,6},{6,7},{7,8},{8,9},{9,10},{10,1... | collective-permute-start | bytes 36872 | tf_op jit(solution)/shard_map/while/body/eval_jaxpr/ppermute | solution.py:30
  123.9 7.0 %collective-permute-start.1 = (f32[2,3,1,512]{3,2,1,0:T(1,128)S(1)}, f32[2,3,1,512]{3,2,1,0:T(1,128)S(1)}, u32[]{:S(2)}, u32[]{:S(2)}) collective-permute-start(f32[2,3,1,512]{3,2,1,0:T(1,128)S(1)} %get-tuple-element.910), channel_id=1, source_target_pairs={{0,1},{1,2},{2,3},{3,4},{4,5},{5,6},{6,7},{7,8},{8,9},{9,10},{10,1... | collective-permute-start | bytes 36872 | tf_op jit(solution)/shard_map/while/body/eval_jaxpr/ppermute | solution.py:30
  142.0 7.0 %collective-permute-start.1 = (f32[2,3,1,512]{3,2,1,0:T(1,128)S(1)}, f32[2,3,1,512]{3,2,1,0:T(1,128)S(1)}, u32[]{:S(2)}, u32[]{:S(2)}) collective-permute-start(f32[2,3,1,512]{3,2,1,0:T(1,128)S(1)} %get-tuple-element.910), channel_id=1, source_target_pairs={{0,1},{1,2},{2,3},{3,4},{4,5},{5,6},{6,7},{7,8},{8,9},{9,10},{10,1... | collective-permute-start | bytes 36872 | tf_op jit(solution)/shard_map/while/body/eval_jaxpr/ppermute | solution.py:30
  159.4 192.2 %while.44 = (s32[]{:T(128)}, f32[2,6,8,512]{3,2,1,0:T(8,128)S(1)}, f32[8,512]{1,0:T(8,128)S(1)}, f32[9,512]{1,0:T(8,128)S(1)}, f32[8,2,6,8,512]{4,3,2,1,0:T(8,12...) while((s32[]{:T(128)}, f32[2,6,8,512]{3,2,1,0:T(8,128)S(1)}, ...), condition=%wide.region_25.26_spmd.clone, body=%wide.region_8.25_spmd.clone.sunk | while | flops 25759636 | bytes 17506628 | solution.py:186
  172.7 7.0 %collective-permute-start.2 = (f32[2,3,1,512]{3,2,1,0:T(1,128)S(1)}, f32[2,3,1,512]{3,2,1,0:T(1,128)S(1)}, u32[]{:S(2)}, u32[]{:S(2)}) collective-permute-start(f32[2,3,1,512]{3,2,1,0:T(1,128)S(1)} %get-tuple-element.973), channel_id=1, source_target_pairs={{0,1},{1,2},{2,3},{3,4},{4,5},{5,6},{6,7},{7,8},{8,9},{9,10},{10,1... | collective-permute-start | bytes 36872 | tf_op jit(solution)/shard_map/while/body/eval_jaxpr/ppermute | solution.py:30
  197.7 7.7 %collective-permute-start.2 = (f32[2,3,1,512]{3,2,1,0:T(1,128)S(1)}, f32[2,3,1,512]{3,2,1,0:T(1,128)S(1)}, u32[]{:S(2)}, u32[]{:S(2)}) collective-permute-start(f32[2,3,1,512]{3,2,1,0:T(1,128)S(1)} %get-tuple-element.973), channel_id=1, source_target_pairs={{0,1},{1,2},{2,3},{3,4},{4,5},{5,6},{6,7},{7,8},{8,9},{9,10},{10,1... | collective-permute-start | bytes 36872 | tf_op jit(solution)/shard_map/while/body/eval_jaxpr/ppermute | solution.py:30
  222.2 7.0 %collective-permute-start.2 = (f32[2,3,1,512]{3,2,1,0:T(1,128)S(1)}, f32[2,3,1,512]{3,2,1,0:T(1,128)S(1)}, u32[]{:S(2)}, u32[]{:S(2)}) collective-permute-start(f32[2,3,1,512]{3,2,1,0:T(1,128)S(1)} %get-tuple-element.973), channel_id=1, source_target_pairs={{0,1},{1,2},{2,3},{3,4},{4,5},{5,6},{6,7},{7,8},{8,9},{9,10},{10,1... | collective-permute-start | bytes 36872 | tf_op jit(solution)/shard_map/while/body/eval_jaxpr/ppermute | solution.py:30
  246.0 7.0 %collective-permute-start.2 = (f32[2,3,1,512]{3,2,1,0:T(1,128)S(1)}, f32[2,3,1,512]{3,2,1,0:T(1,128)S(1)}, u32[]{:S(2)}, u32[]{:S(2)}) collective-permute-start(f32[2,3,1,512]{3,2,1,0:T(1,128)S(1)} %get-tuple-element.973), channel_id=1, source_target_pairs={{0,1},{1,2},{2,3},{3,4},{4,5},{5,6},{6,7},{7,8},{8,9},{9,10},{10,1... | collective-permute-start | bytes 36872 | tf_op jit(solution)/shard_map/while/body/eval_jaxpr/ppermute | solution.py:30
  269.8 7.0 %collective-permute-start.2 = (f32[2,3,1,512]{3,2,1,0:T(1,128)S(1)}, f32[2,3,1,512]{3,2,1,0:T(1,128)S(1)}, u32[]{:S(2)}, u32[]{:S(2)}) collective-permute-start(f32[2,3,1,512]{3,2,1,0:T(1,128)S(1)} %get-tuple-element.973), channel_id=1, source_target_pairs={{0,1},{1,2},{2,3},{3,4},{4,5},{5,6},{6,7},{7,8},{8,9},{9,10},{10,1... | collective-permute-start | bytes 36872 | tf_op jit(solution)/shard_map/while/body/eval_jaxpr/ppermute | solution.py:30
  289.7 2.9 fusion.118
  293.5 7.0 %collective-permute-start.2 = (f32[2,3,1,512]{3,2,1,0:T(1,128)S(1)}, f32[2,3,1,512]{3,2,1,0:T(1,128)S(1)}, u32[]{:S(2)}, u32[]{:S(2)}) collective-permute-start(f32[2,3,1,512]{3,2,1,0:T(1,128)S(1)} %get-tuple-element.973), channel_id=1, source_target_pairs={{0,1},{1,2},{2,3},{3,4},{4,5},{5,6},{6,7},{7,8},{8,9},{9,10},{10,1... | collective-permute-start | bytes 36872 | tf_op jit(solution)/shard_map/while/body/eval_jaxpr/ppermute | solution.py:30
  317.3 7.0 %collective-permute-start.2 = (f32[2,3,1,512]{3,2,1,0:T(1,128)S(1)}, f32[2,3,1,512]{3,2,1,0:T(1,128)S(1)}, u32[]{:S(2)}, u32[]{:S(2)}) collective-permute-start(f32[2,3,1,512]{3,2,1,0:T(1,128)S(1)} %get-tuple-element.973), channel_id=1, source_target_pairs={{0,1},{1,2},{2,3},{3,4},{4,5},{5,6},{6,7},{7,8},{8,9},{9,10},{10,1... | collective-permute-start | bytes 36872 | tf_op jit(solution)/shard_map/while/body/eval_jaxpr/ppermute | solution.py:30
  341.1 7.0 %collective-permute-start.2 = (f32[2,3,1,512]{3,2,1,0:T(1,128)S(1)}, f32[2,3,1,512]{3,2,1,0:T(1,128)S(1)}, u32[]{:S(2)}, u32[]{:S(2)}) collective-permute-start(f32[2,3,1,512]{3,2,1,0:T(1,128)S(1)} %get-tuple-element.973), channel_id=1, source_target_pairs={{0,1},{1,2},{2,3},{3,4},{4,5},{5,6},{6,7},{7,8},{8,9},{9,10},{10,1... | collective-permute-start | bytes 36872 | tf_op jit(solution)/shard_map/while/body/eval_jaxpr/ppermute | solution.py:30
  354.0 3.6 all-to-all-start
  357.5 3.6 collective-permute-start.5
  361.2 4.0 %collective-permute-done.5 = f32[1,512]{1,0:T(1,128)S(1)} collective-permute-done((f32[1,512]{1,0:T(1,128)S(1)}, f32[1,512]{1,0:T(1,128)S(1)}, u32[]{:S(2)}, u32[]{:S(2)}) %collective-permute-start.5) | collective-permute-done | bytes 2080 | tf_op jit(solution)/shard_map/ppermute | solution.py:20
  365.3 21.1 %all-reduce.14 = (f32[1,8,512]{2,1,0:T(8,128)S(1)}, f32[1,8,512]{2,1,0:T(8,128)S(1)}) all-reduce(f32[1,8,512]{2,1,0:T(8,128)S(1)} %multiply_bitcast_fusion, f32[1,8,512]{2,1,0:T(8,128)S(1)} %bitcast.174), channel_id=1, replica_groups=mesh['section'=4,'space'=64] {'section'}, use_global_device_ids=true, to_apply=%region_27.28 | all-reduce | flops 8192 | bytes 65536 | tf_op jit(solution)/shard_map/psum | solution.py:194
  (641 shorter events, 200.0 us)
Async XLA Ops:
  1.5 15.6 %collective-permute-start.4 = (f32[1,512]{1,0:T(1,128)S(1)}, f32[1,512]{1,0:T(1,128)S(1)}, u32[]{:S(2)}, u32[]{:S(2)}) collective-permute-start(f32[1,512]{1,0:T(1,128)S(1)} %slice.367), channel_id=1, source_target_pairs={{0,1},{1,2},{2,3},{3,4},{4,5},{5,6},{6,7},{7,8},{8,9},{9,10},{10,1... | collective-permute-start | bytes 6152 | tf_op jit(solution)/shard_map/ppermute | solution.py:20
  17.3 9.3 %collective-permute-start = (f32[2,3,1,512]{3,2,1,0:T(1,128)S(1)}, f32[2,3,1,512]{3,2,1,0:T(1,128)S(1)}, u32[]{:S(2)}, u32[]{:S(2)}) collective-permute-start(f32[2,3,1,512]{3,2,1,0:T(1,128)S(1)} %get-tuple-element.906), channel_id=1, source_target_pairs={{1,0},{2,1},{3,2},{4,3},{5,4},{6,5},{7,6},{8,7},{9,8},{10,9},{11,1... | collective-permute-start | bytes 36872 | tf_op jit(solution)/shard_map/while/body/eval_jaxpr/ppermute | solution.py:31
  31.5 13.2 %collective-permute-start = (f32[2,3,1,512]{3,2,1,0:T(1,128)S(1)}, f32[2,3,1,512]{3,2,1,0:T(1,128)S(1)}, u32[]{:S(2)}, u32[]{:S(2)}) collective-permute-start(f32[2,3,1,512]{3,2,1,0:T(1,128)S(1)} %get-tuple-element.906), channel_id=1, source_target_pairs={{1,0},{2,1},{3,2},{4,3},{5,4},{6,5},{7,6},{8,7},{9,8},{10,9},{11,1... | collective-permute-start | bytes 36872 | tf_op jit(solution)/shard_map/while/body/eval_jaxpr/ppermute | solution.py:31
  34.0 10.7 %collective-permute-start.1 = (f32[2,3,1,512]{3,2,1,0:T(1,128)S(1)}, f32[2,3,1,512]{3,2,1,0:T(1,128)S(1)}, u32[]{:S(2)}, u32[]{:S(2)}) collective-permute-start(f32[2,3,1,512]{3,2,1,0:T(1,128)S(1)} %get-tuple-element.910), channel_id=1, source_target_pairs={{0,1},{1,2},{2,3},{3,4},{4,5},{5,6},{6,7},{7,8},{8,9},{9,10},{10,1... | collective-permute-start | bytes 36872 | tf_op jit(solution)/shard_map/while/body/eval_jaxpr/ppermute | solution.py:30
  49.6 13.2 %collective-permute-start = (f32[2,3,1,512]{3,2,1,0:T(1,128)S(1)}, f32[2,3,1,512]{3,2,1,0:T(1,128)S(1)}, u32[]{:S(2)}, u32[]{:S(2)}) collective-permute-start(f32[2,3,1,512]{3,2,1,0:T(1,128)S(1)} %get-tuple-element.906), channel_id=1, source_target_pairs={{1,0},{2,1},{3,2},{4,3},{5,4},{6,5},{7,6},{8,7},{9,8},{10,9},{11,1... | collective-permute-start | bytes 36872 | tf_op jit(solution)/shard_map/while/body/eval_jaxpr/ppermute | solution.py:31
  51.5 11.3 %collective-permute-start.1 = (f32[2,3,1,512]{3,2,1,0:T(1,128)S(1)}, f32[2,3,1,512]{3,2,1,0:T(1,128)S(1)}, u32[]{:S(2)}, u32[]{:S(2)}) collective-permute-start(f32[2,3,1,512]{3,2,1,0:T(1,128)S(1)} %get-tuple-element.910), channel_id=1, source_target_pairs={{0,1},{1,2},{2,3},{3,4},{4,5},{5,6},{6,7},{7,8},{8,9},{9,10},{10,1... | collective-permute-start | bytes 36872 | tf_op jit(solution)/shard_map/while/body/eval_jaxpr/ppermute | solution.py:30
  67.7 13.2 %collective-permute-start = (f32[2,3,1,512]{3,2,1,0:T(1,128)S(1)}, f32[2,3,1,512]{3,2,1,0:T(1,128)S(1)}, u32[]{:S(2)}, u32[]{:S(2)}) collective-permute-start(f32[2,3,1,512]{3,2,1,0:T(1,128)S(1)} %get-tuple-element.906), channel_id=1, source_target_pairs={{1,0},{2,1},{3,2},{4,3},{5,4},{6,5},{7,6},{8,7},{9,8},{10,9},{11,1... | collective-permute-start | bytes 36872 | tf_op jit(solution)/shard_map/while/body/eval_jaxpr/ppermute | solution.py:31
  69.6 11.3 %collective-permute-start.1 = (f32[2,3,1,512]{3,2,1,0:T(1,128)S(1)}, f32[2,3,1,512]{3,2,1,0:T(1,128)S(1)}, u32[]{:S(2)}, u32[]{:S(2)}) collective-permute-start(f32[2,3,1,512]{3,2,1,0:T(1,128)S(1)} %get-tuple-element.910), channel_id=1, source_target_pairs={{0,1},{1,2},{2,3},{3,4},{4,5},{5,6},{6,7},{7,8},{8,9},{9,10},{10,1... | collective-permute-start | bytes 36872 | tf_op jit(solution)/shard_map/while/body/eval_jaxpr/ppermute | solution.py:30
  85.8 13.2 %collective-permute-start = (f32[2,3,1,512]{3,2,1,0:T(1,128)S(1)}, f32[2,3,1,512]{3,2,1,0:T(1,128)S(1)}, u32[]{:S(2)}, u32[]{:S(2)}) collective-permute-start(f32[2,3,1,512]{3,2,1,0:T(1,128)S(1)} %get-tuple-element.906), channel_id=1, source_target_pairs={{1,0},{2,1},{3,2},{4,3},{5,4},{6,5},{7,6},{8,7},{9,8},{10,9},{11,1... | collective-permute-start | bytes 36872 | tf_op jit(solution)/shard_map/while/body/eval_jaxpr/ppermute | solution.py:31
  87.7 11.3 %collective-permute-start.1 = (f32[2,3,1,512]{3,2,1,0:T(1,128)S(1)}, f32[2,3,1,512]{3,2,1,0:T(1,128)S(1)}, u32[]{:S(2)}, u32[]{:S(2)}) collective-permute-start(f32[2,3,1,512]{3,2,1,0:T(1,128)S(1)} %get-tuple-element.910), channel_id=1, source_target_pairs={{0,1},{1,2},{2,3},{3,4},{4,5},{5,6},{6,7},{7,8},{8,9},{9,10},{10,1... | collective-permute-start | bytes 36872 | tf_op jit(solution)/shard_map/while/body/eval_jaxpr/ppermute | solution.py:30
  103.9 13.2 %collective-permute-start = (f32[2,3,1,512]{3,2,1,0:T(1,128)S(1)}, f32[2,3,1,512]{3,2,1,0:T(1,128)S(1)}, u32[]{:S(2)}, u32[]{:S(2)}) collective-permute-start(f32[2,3,1,512]{3,2,1,0:T(1,128)S(1)} %get-tuple-element.906), channel_id=1, source_target_pairs={{1,0},{2,1},{3,2},{4,3},{5,4},{6,5},{7,6},{8,7},{9,8},{10,9},{11,1... | collective-permute-start | bytes 36872 | tf_op jit(solution)/shard_map/while/body/eval_jaxpr/ppermute | solution.py:31
  105.8 11.3 %collective-permute-start.1 = (f32[2,3,1,512]{3,2,1,0:T(1,128)S(1)}, f32[2,3,1,512]{3,2,1,0:T(1,128)S(1)}, u32[]{:S(2)}, u32[]{:S(2)}) collective-permute-start(f32[2,3,1,512]{3,2,1,0:T(1,128)S(1)} %get-tuple-element.910), channel_id=1, source_target_pairs={{0,1},{1,2},{2,3},{3,4},{4,5},{5,6},{6,7},{7,8},{8,9},{9,10},{10,1... | collective-permute-start | bytes 36872 | tf_op jit(solution)/shard_map/while/body/eval_jaxpr/ppermute | solution.py:30
  122.0 13.2 %collective-permute-start = (f32[2,3,1,512]{3,2,1,0:T(1,128)S(1)}, f32[2,3,1,512]{3,2,1,0:T(1,128)S(1)}, u32[]{:S(2)}, u32[]{:S(2)}) collective-permute-start(f32[2,3,1,512]{3,2,1,0:T(1,128)S(1)} %get-tuple-element.906), channel_id=1, source_target_pairs={{1,0},{2,1},{3,2},{4,3},{5,4},{6,5},{7,6},{8,7},{9,8},{10,9},{11,1... | collective-permute-start | bytes 36872 | tf_op jit(solution)/shard_map/while/body/eval_jaxpr/ppermute | solution.py:31
  123.9 11.3 %collective-permute-start.1 = (f32[2,3,1,512]{3,2,1,0:T(1,128)S(1)}, f32[2,3,1,512]{3,2,1,0:T(1,128)S(1)}, u32[]{:S(2)}, u32[]{:S(2)}) collective-permute-start(f32[2,3,1,512]{3,2,1,0:T(1,128)S(1)} %get-tuple-element.910), channel_id=1, source_target_pairs={{0,1},{1,2},{2,3},{3,4},{4,5},{5,6},{6,7},{7,8},{8,9},{9,10},{10,1... | collective-permute-start | bytes 36872 | tf_op jit(solution)/shard_map/while/body/eval_jaxpr/ppermute | solution.py:30
  140.1 13.2 %collective-permute-start = (f32[2,3,1,512]{3,2,1,0:T(1,128)S(1)}, f32[2,3,1,512]{3,2,1,0:T(1,128)S(1)}, u32[]{:S(2)}, u32[]{:S(2)}) collective-permute-start(f32[2,3,1,512]{3,2,1,0:T(1,128)S(1)} %get-tuple-element.906), channel_id=1, source_target_pairs={{1,0},{2,1},{3,2},{4,3},{5,4},{6,5},{7,6},{8,7},{9,8},{10,9},{11,1... | collective-permute-start | bytes 36872 | tf_op jit(solution)/shard_map/while/body/eval_jaxpr/ppermute | solution.py:31
  142.0 11.3 %collective-permute-start.1 = (f32[2,3,1,512]{3,2,1,0:T(1,128)S(1)}, f32[2,3,1,512]{3,2,1,0:T(1,128)S(1)}, u32[]{:S(2)}, u32[]{:S(2)}) collective-permute-start(f32[2,3,1,512]{3,2,1,0:T(1,128)S(1)} %get-tuple-element.910), channel_id=1, source_target_pairs={{0,1},{1,2},{2,3},{3,4},{4,5},{5,6},{6,7},{7,8},{8,9},{9,10},{10,1... | collective-permute-start | bytes 36872 | tf_op jit(solution)/shard_map/while/body/eval_jaxpr/ppermute | solution.py:30
  172.7 9.0 %collective-permute-start.2 = (f32[2,3,1,512]{3,2,1,0:T(1,128)S(1)}, f32[2,3,1,512]{3,2,1,0:T(1,128)S(1)}, u32[]{:S(2)}, u32[]{:S(2)}) collective-permute-start(f32[2,3,1,512]{3,2,1,0:T(1,128)S(1)} %get-tuple-element.973), channel_id=1, source_target_pairs={{0,1},{1,2},{2,3},{3,4},{4,5},{5,6},{6,7},{7,8},{8,9},{9,10},{10,1... | collective-permute-start | bytes 36872 | tf_op jit(solution)/shard_map/while/body/eval_jaxpr/ppermute | solution.py:30
  197.7 9.7 %collective-permute-start.2 = (f32[2,3,1,512]{3,2,1,0:T(1,128)S(1)}, f32[2,3,1,512]{3,2,1,0:T(1,128)S(1)}, u32[]{:S(2)}, u32[]{:S(2)}) collective-permute-start(f32[2,3,1,512]{3,2,1,0:T(1,128)S(1)} %get-tuple-element.973), channel_id=1, source_target_pairs={{0,1},{1,2},{2,3},{3,4},{4,5},{5,6},{6,7},{7,8},{8,9},{9,10},{10,1... | collective-permute-start | bytes 36872 | tf_op jit(solution)/shard_map/while/body/eval_jaxpr/ppermute | solution.py:30
  222.2 9.0 %collective-permute-start.2 = (f32[2,3,1,512]{3,2,1,0:T(1,128)S(1)}, f32[2,3,1,512]{3,2,1,0:T(1,128)S(1)}, u32[]{:S(2)}, u32[]{:S(2)}) collective-permute-start(f32[2,3,1,512]{3,2,1,0:T(1,128)S(1)} %get-tuple-element.973), channel_id=1, source_target_pairs={{0,1},{1,2},{2,3},{3,4},{4,5},{5,6},{6,7},{7,8},{8,9},{9,10},{10,1... | collective-permute-start | bytes 36872 | tf_op jit(solution)/shard_map/while/body/eval_jaxpr/ppermute | solution.py:30
  246.0 9.0 %collective-permute-start.2 = (f32[2,3,1,512]{3,2,1,0:T(1,128)S(1)}, f32[2,3,1,512]{3,2,1,0:T(1,128)S(1)}, u32[]{:S(2)}, u32[]{:S(2)}) collective-permute-start(f32[2,3,1,512]{3,2,1,0:T(1,128)S(1)} %get-tuple-element.973), channel_id=1, source_target_pairs={{0,1},{1,2},{2,3},{3,4},{4,5},{5,6},{6,7},{7,8},{8,9},{9,10},{10,1... | collective-permute-start | bytes 36872 | tf_op jit(solution)/shard_map/while/body/eval_jaxpr/ppermute | solution.py:30
  269.8 9.0 %collective-permute-start.2 = (f32[2,3,1,512]{3,2,1,0:T(1,128)S(1)}, f32[2,3,1,512]{3,2,1,0:T(1,128)S(1)}, u32[]{:S(2)}, u32[]{:S(2)}) collective-permute-start(f32[2,3,1,512]{3,2,1,0:T(1,128)S(1)} %get-tuple-element.973), channel_id=1, source_target_pairs={{0,1},{1,2},{2,3},{3,4},{4,5},{5,6},{6,7},{7,8},{8,9},{9,10},{10,1... | collective-permute-start | bytes 36872 | tf_op jit(solution)/shard_map/while/body/eval_jaxpr/ppermute | solution.py:30
  317.3 9.0 %collective-permute-start.2 = (f32[2,3,1,512]{3,2,1,0:T(1,128)S(1)}, f32[2,3,1,512]{3,2,1,0:T(1,128)S(1)}, u32[]{:S(2)}, u32[]{:S(2)}) collective-permute-start(f32[2,3,1,512]{3,2,1,0:T(1,128)S(1)} %get-tuple-element.973), channel_id=1, source_target_pairs={{0,1},{1,2},{2,3},{3,4},{4,5},{5,6},{6,7},{7,8},{8,9},{9,10},{10,1... | collective-permute-start | bytes 36872 | tf_op jit(solution)/shard_map/while/body/eval_jaxpr/ppermute | solution.py:30
  341.1 9.0 %collective-permute-start.2 = (f32[2,3,1,512]{3,2,1,0:T(1,128)S(1)}, f32[2,3,1,512]{3,2,1,0:T(1,128)S(1)}, u32[]{:S(2)}, u32[]{:S(2)}) collective-permute-start(f32[2,3,1,512]{3,2,1,0:T(1,128)S(1)} %get-tuple-element.973), channel_id=1, source_target_pairs={{0,1},{1,2},{2,3},{3,4},{4,5},{5,6},{6,7},{7,8},{8,9},{9,10},{10,1... | collective-permute-start | bytes 36872 | tf_op jit(solution)/shard_map/while/body/eval_jaxpr/ppermute | solution.py:30
  354.0 33.0 %all-to-all-start = ((f32[4,2,12,8,512]{4,3,2,1,0:T(8,128)}), f32[4,2,12,8,512]{4,3,2,1,0:T(8,128)S(1)}, u32[]{:S(2)}, u32[]{:S(2)}) async-start(f32[4,2,12,8,512]{4,3,2,1,0:T(8,128)} %pad_maximum_fusion.5), calls=%async_computation | async-start | bytes 3145728 | tf_op jit(solution)/shard_map/all_to_all | solution.py:51
  (13 other events, 69.6 us)
where the time goes:
time: 391 us; the launch traced here: 388 us
  starting transfers between devices  148 us (38%)
  other arithmetic  96.2 us (25%)
  local copies, waits for them, and re-layouts  47.7 us (12%)
  loops' own time  34.8 us (9%)
  blocking collectives  31 us (8%)
  matrix products  15.6 us (4%)
  waiting for transfers between devices  14.2 us (4%)
    ppermute x16, starting transfers between devices, padded(): before = lax.ppermute(last, axis, up)  108 us
    ppermute x16, starting transfers between devices, padded(): after = lax.ppermute(first, axis, down)  31.3 us
    reduce_sum x16, other arithmetic, contact(): jnp.sum(separation * separation, axis=0)  25 us
    reduce_sum x8, other arithmetic, contact(): separation = own_points[:, :, :, None] - other_points[:, :, None, :]  23.2 us
    psum x1, blocking collectives, on_device(): summed_row, summed_column = lax.psum((grad_row, column_own), 'section')  21.1 us
    another operation x1, loops' own time, on_device(): lax.scan(backward_step, start_carry, (numbers, extended_all, velocity_all...  17.9 us
    another operation x1, loops' own time, on_device(): lax.scan(forward_step, own_start, numbers)  16.9 us
    reduce_sum x8, other arithmetic, contact(): jnp.sum(spring_weights[None] * separation, axis=3)  15.4 us
  transfers between devices with their start and end apart: 35, of which 9 were waited for; matrix products, arithmetic and copies ran while one was open for 6% of the time, Pallas kernels for 0%

commit v1 on v0

v1 whole, which is shorter than its diff:
```python
import functools

import jax
import jax.numpy as jnp
from jax import lax
from jax.experimental import pallas as pl
from jax.experimental.pallas import tpu as pltpu
from jax.sharding import PartitionSpec as P


H = 0.1
DAMP = 0.98
SCALE = 0.3
GRAV = 0.5
TINY = 1e-06
F32 = jnp.float32
BF16 = jnp.bfloat16
GROUP = 2
SLOTS = 8
ROWS = 8
COLS = 512
NB = COLS // 128
EXT = ROWS + 2
META_S, META_C, META_Q = 24, 25, 26


def lists(meta, step):
    section = meta[0, META_S]
    row = lax.rem(section - step // 2 + 4, 4)
    base = 32 * (step % 2)
    return row, base


def tile_start(row, block):
    return pl.multiple_of((block * EXT + row) * 8, 8)


def row_is(r, n=COLS):
    return lax.broadcasted_iota(jnp.int32, (ROWS, n), 0) == r


def fill_tiles(tiles, value_of):
    for t in range(2):
        for c in range(3):
            v = value_of(t, c)
            for b in range(NB):
                tiles[pl.ds((b * EXT + 1) * 8 + 3 * t + c, ROWS, stride=8), :] = v[:, b * 128 : (b + 1) * 128]


def read_tiles(tiles, k):
    return jnp.concatenate([tiles[pl.ds((b * EXT + 1) * 8 + k, ROWS, stride=8), :] for b in range(NB)], axis=1)


def fill_halo(tiles, up, down):
    for b in range(NB):
        tiles[pl.ds(b * EXT * 8, 8), :] = up[:, b * 128 : (b + 1) * 128]
        tiles[pl.ds((b * EXT + EXT - 1) * 8, 8), :] = down[:, b * 128 : (b + 1) * 128]


def selectors():
    row = lax.broadcasted_iota(jnp.int32, (18, 768), 0)
    lane = lax.broadcasted_iota(jnp.int32, (18, 768), 1)
    return (lax.rem(row, 6) == lane // 128).astype(F32).astype(BF16)


def pieces(x):
    high = x.astype(BF16).astype(F32)
    rest = x - high
    middle = rest.astype(BF16).astype(F32)
    return [v[:6] for v in (high, middle, rest - middle)]


def flat(x):
    return jnp.concatenate([x[k : k + 1] for k in range(6)], axis=1)


def spread(left, right):
    return lax.dot_general(left.astype(BF16), right, (((0,), (0,)), ((), ())), preferred_element_type=F32)


def differences(on_lanes, on_sublanes, marks):
    left = jnp.concatenate([-v for v in pieces(on_sublanes)] + [jnp.ones((3, 128), F32)], axis=0)
    right = jnp.concatenate([marks] + [flat(v).astype(BF16) for v in pieces(on_lanes)], axis=0)
    return spread(left, right)


def block(x, j, k):
    return x[8 * j : 8 * j + 8, 128 * k : 128 * k + 128]


def stacked(rows):
    return jnp.concatenate([jnp.sum(v, axis=0, keepdims=True) for v in rows] + [jnp.zeros((2, 128), F32)], axis=0)


def pair_force(xa, xb, marks, scale):
    diff = differences(xa, xb, marks)
    rows = []
    for t in range(2):
        acc = [jnp.zeros((8, 128), F32) for _ in range(3)]
        for j in range(16):
            d = [block(diff, j, 3 * t + c) for c in range(3)]
            w = jnp.exp(-0.5 * (d[0] * d[0] + d[1] * d[1] + d[2] * d[2]))
            acc = [acc[c] + w * d[c] for c in range(3)]
        rows += acc
    return scale * stacked(rows)


def pair_adjoint(xa, xb, ga, marks, scale):
    from_a = differences(xa, xb, marks)
    from_b = differences(xb, xa, marks)
    g_sub = spread(jnp.concatenate(pieces(ga), axis=0), marks)
    rows_a, rows_b = [], []
    for t in range(2):
        g = [ga[3 * t + c : 3 * t + c + 1, :] for c in range(3)]
        sum_a = [jnp.zeros((8, 128), F32) for _ in range(3)]
        sum_b = [jnp.zeros((8, 128), F32) for _ in range(3)]
        for j in range(16):
            sum_a = pair_sum(sum_a, [block(from_a, j, 3 * t + c) for c in range(3)], g)
            sum_b = pair_sum(sum_b, [block(from_b, j, 3 * t + c) for c in range(3)], [block(g_sub, j, 3 * t + c) for c in range(3)])
        rows_a += sum_a
        rows_b += sum_b
    return scale * stacked(rows_a), -scale * stacked(rows_b)


def pair_sum(total, d, g):
    w = jnp.exp(-0.5 * (d[0] * d[0] + d[1] * d[1] + d[2] * d[2]))
    s = g[0] * d[0] + g[1] * d[1] + g[2] * d[2]
    return [v + w * (g[c] - s * d[c]) for c, v in enumerate(total)]


def edge_force(own, other, k):
    d = [o - x for o, x in zip(other, own)]
    coef = k * (1.0 - lax.rsqrt(d[0] * d[0] + d[1] * d[1] + d[2] * d[2] + TINY))
    return [coef * e for e in d]


def edge_adjoint(own, other, k, u):
    d = [o - x for o, x in zip(other, own)]
    y = lax.rsqrt(d[0] * d[0] + d[1] * d[1] + d[2] * d[2] + TINY)
    s = d[0] * u[0] + d[1] * u[1] + d[2] * u[2]
    one = 1.0 - y
    k1, k2 = k * one, k * (y * y * y) * s
    return [k1 * u[c] + k2 * d[c] for c in range(3)], one * s


def start_kernel(meta, state, stiff, send_x, send_p, kk):
    first = meta[0, META_C] == 0
    last = meta[0, META_Q] == 63
    column = lax.broadcasted_iota(jnp.int32, (ROWS, COLS), 1)
    kk[0] = jnp.where(column < COLS - 1, stiff[0], 0.0)
    kc = jnp.where(jnp.logical_and(row_is(ROWS - 1), last), 0.0, stiff[1])
    kk[1] = kc
    write_sends(first, [state[t, c] for t in range(2) for c in range(3)], kc, send_x, send_p)


def write_sends(first, values, kc, send_x, send_p):
    tops = jnp.concatenate([v[0:1] for v in values] + [kc[7:8], kc[7:8]], axis=0)
    lows = jnp.concatenate([v[7:8] for v in values] + [kc[7:8], kc[7:8]], axis=0)
    send_x[...] = jnp.where(first, tops, lows)
    send_p[...] = jnp.where(first, lows, tops)


def side_row(first, v, outer):
    return jnp.where(first, v[0:1], v[7:8]) if outer else jnp.where(first, v[7:8], v[0:1])


def forward_inner(step, meta, state, halo_p, kk, force, tiles, acc):
    first = meta[0, META_C] == 0
    row, base = lists(meta, step)
    fill_tiles(tiles, lambda t, c: state[t, c])
    fill_halo(tiles, halo_p[...], halo_p[...])
    acc[...] = jnp.zeros(acc.shape, F32)
    outer = jnp.where(first, 0, EXT - 1)

    count = meta[row, base + 2 * SLOTS]
    marks = selectors()

    def group(i, carry):
        results = []
        for q in range(GROUP):
            p = i * GROUP + q
            a = meta[row, base + p]
            b = meta[row, base + SLOTS + p]
            b_row = b // NB
            live = jnp.logical_and(p < count, b_row != outer)
            at = tile_start(a // NB + 1, lax.rem(a, NB))
            xa = tiles[pl.ds(at, 8), :]
            xb = tiles[pl.ds(tile_start(b_row, lax.rem(b, NB)), 8), :]
            results.append((at, pair_force(xa, xb, marks, jnp.where(live, SCALE, 0.0))))
        for at, value in results:
            acc[pl.ds(at, 8), :] += value
        return carry

    lax.fori_loop(0, (count + GROUP - 1) // GROUP, group, 0)
    kh, kc = kk[0], kk[1]
    k_up = jnp.where(row_is(0), 0.0, pltpu.roll(kc, 1, 0))
    k_side = jnp.where(first, kc[7:8], halo_p[6:7])
    side = jnp.where(first, ROWS - 1, 0)
    for t in range(2):
        x = [state[t, c] for c in range(3)]
        right = edge_force(x, [pltpu.roll(v, COLS - 1, 1) for v in x], kh)
        up = edge_force(x, [pltpu.roll(v, 1, 0) for v in x], k_up)
        edge = edge_force([side_row(first, v, False) for v in x], [halo_p[3 * t + c : 3 * t + c + 1] for c in range(3)], k_side)
        for c in range(3):
            total = right[c] - pltpu.roll(right[c], 1, 1) + up[c] - pltpu.roll(up[c], 7, 0)
            force[3 * t + c] = total + jnp.where(row_is(side), edge[c], 0.0) + read_tiles(acc, 3 * t + c)


def forward_outer(step, meta, state, halo_x, kk, force, state_out, send_x, send_p, tiles, acc, halo):
    first = meta[0, META_C] == 0
    row, base = lists(meta, step)
    count = meta[row, base + 2 * SLOTS]
    outer = jnp.where(first, 0, EXT - 1)
    hits = [jnp.logical_and(p < count, meta[row, base + SLOTS + p] // NB == outer) for p in range(SLOTS)]
    some = functools.reduce(jnp.logical_or, hits)

    @pl.when(some)
    def _():
        acc[...] = jnp.zeros(acc.shape, F32)
        fill_tiles(tiles, lambda t, c: state[t, c])
        for b in range(NB):
            halo[pl.ds(8 * b, 8), :] = halo_x[:, b * 128 : (b + 1) * 128]
        marks = selectors()

        def slot(p, carry):
            a = meta[row, base + p]
            b = meta[row, base + SLOTS + p]

            @pl.when(b // NB == outer)
            def _():
                at = tile_start(a // NB + 1, lax.rem(a, NB))
                xa = tiles[pl.ds(at, 8), :]
                xb = halo[pl.ds(pl.multiple_of(8 * lax.rem(b, NB), 8), 8), :]
                acc[pl.ds(at, 8), :] += pair_force(xa, xb, marks, SCALE)

            return carry

        lax.fori_loop(0, count, slot, 0)
        for k in range(6):
            force[k] = force[k] + read_tiles(acc, k)

    kc = kk[1]
    k_side = jnp.where(first, halo_x[6:7], kc[7:8])
    side = jnp.where(first, 0, ROWS - 1)
    values = []
    for t in range(2):
        x = [state[t, c] for c in range(3)]
        edge = edge_force([side_row(first, v, True) for v in x], [halo_x[3 * t + c : 3 * t + c + 1] for c in range(3)], k_side)
        for c in range(3):
            f = force[3 * t + c] + jnp.where(row_is(side), edge[c], 0.0)
            if c == 2:
                f = f - GRAV
            v = DAMP * (state[t, 3 + c] + H * f)
            new = x[c] + H * v
            state_out[t, c] = new
            state_out[t, 3 + c] = v
            values.append(new)
    write_sends(first, values, kc, send_x, send_p)


def joined(first, lam, got_x, got_p):
    up = jnp.where(first, got_x[...], got_p[...])
    down = jnp.where(first, got_p[...], got_x[...])
    result = []
    for t in range(2):
        for c in range(3):
            k = 3 * t + c
            result.append(lam[t, c] + jnp.where(row_is(0), up[k : k + 1], 0.0) + jnp.where(row_is(7), down[k : k + 1], 0.0))
    return result, down[6:7]


def backward_outer(step, opening, keep, meta, lam, *refs):
    refs = list(refs)
    got = None if opening else (refs.pop(0), refs.pop(0))
    state, halo_x, halo_p, kk, lam_out, send_x, send_p, kd = refs[:8]
    refs = refs[8:]
    full = refs.pop(0) if keep else None
    tiles, grads, acc, acc_b = refs
    first = meta[0, META_C] == 0
    row, base = lists(meta, step)
    count = meta[row, base + 2 * SLOTS]
    if opening:
        xbar = [lam[t, c] for t in range(2) for c in range(3)]
        got_k = jnp.zeros((1, COLS), F32)
    else:
        xbar, got_k = joined(first, lam, *got)
    force = []
    for t in range(2):
        for c in range(3):
            vbar = lam[t, 3 + c]
            if keep:
                full[t, c] = xbar[3 * t + c]
                full[t, 3 + c] = vbar
            a = DAMP * (vbar + H * xbar[3 * t + c])
            lam_out[t, 3 + c] = a
            force.append(H * a)
    up = jnp.where(first, halo_x[...], halo_p[...])
    down = jnp.where(first, halo_p[...], halo_x[...])
    kc = kk[1]
    up_rows, down_rows = [], []
    up_k = jnp.zeros((1, COLS), F32)
    down_k = got_k
    for t in range(2):
        x = [state[t, c] for c in range(3)]
        g = force[3 * t : 3 * t + 3]
        eu, ku = edge_adjoint([v[0:1] for v in x], [up[3 * t + c : 3 * t + c + 1] for c in range(3)], up[6:7], [v[0:1] for v in g])
        ed, kw = edge_adjoint([v[7:8] for v in x], [down[3 * t + c : 3 * t + c + 1] for c in range(3)], kc[7:8], [v[7:8] for v in g])
        up_rows += eu
        down_rows += ed
        up_k = up_k + ku
        down_k = down_k + kw
        for c in range(3):
            lam_out[t, c] = xbar[3 * t + c] - jnp.where(row_is(0), eu[c], 0.0) - jnp.where(row_is(7), ed[c], 0.0)
    kd[...] = jnp.broadcast_to(down_k, (8, COLS))
    zero = jnp.zeros((1, COLS), F32)
    msg_up = jnp.concatenate(up_rows + [up_k, zero], axis=0)
    msg_down = jnp.concatenate(down_rows + [zero, zero], axis=0)
    send_x[...] = jnp.where(first, msg_up, msg_down)
    send_p[...] = jnp.where(first, msg_down, msg_up)

    def far(b):
        return jnp.logical_or(b < NB, b >= NB * (EXT - 1))

    hits = [jnp.logical_and(p < count, far(meta[row, base + SLOTS + p])) for p in range(SLOTS)]
    some = functools.reduce(jnp.logical_or, hits)

    @pl.when(some)
    def _():
        acc[...] = jnp.zeros(acc.shape, F32)
        acc_b[...] = jnp.zeros(acc_b.shape, F32)
        fill_tiles(tiles, lambda t, c: state[t, c])
        fill_halo(tiles, up, down)
        fill_tiles(grads, lambda t, c: force[3 * t + c])
        marks = selectors()

        def slot(p, carry):
            a = meta[row, base + p]
            b = meta[row, base + SLOTS + p]

            @pl.when(far(b))
            def _():
                at = tile_start(a // NB + 1, lax.rem(a, NB))
                bt = tile_start(b // NB, lax.rem(b, NB))
                con_a, con_b = pair_adjoint(tiles[pl.ds(at, 8), :], tiles[pl.ds(bt, 8), :], grads[pl.ds(at, 8), :], marks, SCALE)
                acc[pl.ds(at, 8), :] += con_a
                out = pl.multiple_of(8 * jnp.where(b < NB, b, b - NB * (EXT - 2)), 8)
                acc_b[pl.ds(out, 8), :] += con_b

            return carry

        lax.fori_loop(0, count, slot, 0)
        for t in range(2):
            for c in range(3):
                lam_out[t, c] = lam_out[t, c] + read_tiles(acc, 3 * t + c)
        more_up = jnp.concatenate([acc_b[8 * b : 8 * b + 8, :] for b in range(NB)], axis=1)
        more_down = jnp.concatenate([acc_b[8 * (NB + b) : 8 * (NB + b) + 8, :] for b in range(NB)], axis=1)
        send_x[...] += jnp.where(first, more_up, more_down)
        send_p[...] += jnp.where(first, more_down, more_up)


def backward_inner(step, opening, meta, lam, state, kk, kd, *refs):
    refs = list(refs)
    old = None if opening else refs.pop(0)
    lam_out, grad, tiles, grads, acc = refs
    row, base = lists(meta, step)
    last = meta[0, META_Q] == 63
    fill_tiles(tiles, lambda t, c: state[t, c])
    fill_tiles(grads, lambda t, c: H * lam[t, 3 + c])
    zero = jnp.zeros((8, COLS), F32)
    fill_halo(tiles, zero, zero)
    acc[...] = jnp.zeros(acc.shape, F32)
    count = meta[row, base + 2 * SLOTS]
    marks = selectors()

    def group(i, carry):
        results = []
        for q in range(GROUP):
            p = i * GROUP + q
            a = meta[row, base + p]
            b = meta[row, base + SLOTS + p]
            live = jnp.logical_and(p < count, jnp.logical_and(b >= NB, b < NB * (EXT - 1)))
            at = tile_start(a // NB + 1, lax.rem(a, NB))
            bt = tile_start(b // NB, lax.rem(b, NB))
            scale = jnp.where(live, SCALE, 0.0)
            results.append((at, bt, *pair_adjoint(tiles[pl.ds(at, 8), :], tiles[pl.ds(bt, 8), :], grads[pl.ds(at, 8), :], marks, scale)))
        for at, bt, con_a, con_b in results:
            acc[pl.ds(at, 8), :] += con_a
            acc[pl.ds(bt, 8), :] += con_b
        return carry

    lax.fori_loop(0, (count + GROUP - 1) // GROUP, group, 0)
    kh, kc = kk[0], kk[1]
    k_up = jnp.where(row_is(0), 0.0, pltpu.roll(kc, 1, 0))
    grad_h = jnp.zeros((ROWS, COLS), F32)
    grad_v = jnp.zeros((ROWS, COLS), F32)
    for t in range(2):
        x = [state[t, c] for c in range(3)]
        g = [H * lam[t, 3 + c] for c in range(3)]
        right, rk = edge_adjoint(x, [pltpu.roll(v, COLS - 1, 1) for v in x], kh, [v - pltpu.roll(v, COLS - 1, 1) for v in g])
        up, uk = edge_adjoint(x, [pltpu.roll(v, 1, 0) for v in x], k_up, [v - pltpu.roll(v, 1, 0) for v in g])
        grad_h = grad_h + rk
        grad_v = grad_v + uk
        for c in range(3):
            total = pltpu.roll(right[c], 1, 1) - right[c] + pltpu.roll(up[c], 7, 0) - up[c]
            lam_out[t, c] = lam[t, c] + total + read_tiles(acc, 3 * t + c)
            lam_out[t, 3 + c] = lam[t, 3 + c]
    column = lax.broadcasted_iota(jnp.int32, (ROWS, COLS), 1)
    grad_h = jnp.where(column < COLS - 1, grad_h, 0.0)
    grad_v = jnp.where(row_is(7), jnp.where(last, 0.0, kd[0:1]), pltpu.roll(grad_v, 7, 0))
    if opening:
        grad[0] = grad_h
        grad[1] = grad_v
    else:
        grad[0] = old[0] + grad_h
        grad[1] = old[1] + grad_v


def end_kernel(meta, lam, got_x, got_p, old, out):
    first = meta[0, META_C] == 0
    last = meta[0, META_Q] == 63
    xbar, got_k = joined(first, lam, got_x, got_p)
    zero = jnp.zeros((2, COLS), F32)
    tops = jnp.concatenate([v[0:1] for v in xbar] + [zero], axis=0)
    lows = jnp.concatenate([v[7:8] for v in xbar] + [zero], axis=0)
    below = old[1] + jnp.where(row_is(7), jnp.where(last, 0.0, got_k), 0.0)
    for s in range(out.shape[0]):
        out[s, 0] = old[0]
        out[s, 1] = below
        out[s, 2] = tops
        out[s, 3] = lows


def output_kernel(meta, swapped, shared, *refs):
    *lams, adjoint, grad = refs
    here = meta[0, META_S] == 0
    for k in range(2):
        grad[k] = shared[0, k] + shared[1, k] + shared[2, k] + shared[3, k]

    @pl.when(here)
    def _():
        for s, lam in enumerate(lams):
            for t in range(2):
                for c in range(3):
                    k = 3 * t + c
                    v = jnp.where(row_is(0), shared[s, 2, k : k + 1], lam[t, c])
                    adjoint[s, t, c] = jnp.where(row_is(7), shared[s, 3, k : k + 1], v)
                    adjoint[s, t, 3 + c] = lam[t, 3 + c]

    @pl.when(jnp.logical_not(here))
    def _():
        adjoint[...] = swapped[...]


STATE = jax.ShapeDtypeStruct((2, 6, ROWS, COLS), F32)
HALO = jax.ShapeDtypeStruct((8, COLS), F32)
GRADS = jax.ShapeDtypeStruct((2, ROWS, COLS), F32)
TILES = pltpu.VMEM((EXT * NB * 8, 128), F32)
SMALL = pltpu.VMEM((NB * 8, 128), F32)


def call(body, outs, operands, scratch=(), flops=0, placed=True):
    spaces = [pltpu.VMEM if k else pltpu.SMEM for k in range(len(operands))]
    if placed:
        operands = [pltpu.with_memory_space_constraint(x, space) for x, space in zip(operands, spaces)]
        outs = [pltpu.VMEM(o.shape, o.dtype) for o in outs]
    return pl.pallas_call(
        body,
        out_shape=outs,
        in_specs=[pl.BlockSpec(memory_space=space) for space in spaces],
        out_specs=[pl.BlockSpec(memory_space=pltpu.VMEM)] * len(outs),
        scratch_shapes=list(scratch),
        cost_estimate=pl.CostEstimate(flops=flops, transcendentals=0, bytes_accessed=1 << 18) if flops else None,
    )(*operands)


def on_device(start_state, stiffness, contact_a, contact_b, pair_count, cotangent):
    section = lax.axis_index("section")
    space = lax.axis_index("space")
    sections = lax.axis_size("section")
    spaces = lax.axis_size("space")
    cross = [(i, i + 1) for i in range(1, spaces - 1, 2)]
    cross = cross + [(b, a) for a, b in cross]
    near = [(i, i ^ 1) for i in range(spaces)]
    steps = contact_a.shape[0] * sections

    facts = jnp.stack([section, lax.rem(space, 2), space]).astype(jnp.int32)
    own_list = jnp.concatenate(
        [
            contact_a[:, 0],
            contact_b[:, 0],
            jnp.broadcast_to(pair_count, (2, 8)),
            jnp.broadcast_to(jnp.pad(facts, (0, 5)), (2, 8)),
        ],
        axis=1,
    ).reshape(1, 64)
    others = [lax.ppermute(own_list, "section", [(i, (i + k) % sections) for i in range(sections)]) for k in range(1, sections)]
    meta = jnp.concatenate([own_list] + others, axis=0)

    state = lax.dynamic_slice_in_dim(start_state, section * 2, 2, 0)
    lam = lax.dynamic_slice_in_dim(cotangent, section * 2, 2, 0)
    send_x, send_p, kk = call(start_kernel, [HALO, HALO, GRADS], [own_list, state, stiffness])

    states, halos, exits = [], [], []
    for step in range(steps):
        halo_x = lax.ppermute(send_x, "space", cross)
        halo_p = lax.ppermute(send_p, "space", near)
        (force,) = call(
            functools.partial(forward_inner, step),
            [jax.ShapeDtypeStruct((6, ROWS, COLS), F32)],
            [meta, state, halo_p, kk],
            [TILES, TILES],
            flops=4000000,
        )
        states.append(state)
        halos.append((halo_x, halo_p))
        state, send_x, send_p = call(
            functools.partial(forward_outer, step), [STATE, HALO, HALO], [meta, state, halo_x, kk, force], [TILES, TILES, SMALL]
        )
        if step % 2 == 1:
            exits.append(state)
    exit_state = lax.all_to_all(jnp.stack(exits), "section", 0, 0, tiled=True)

    grad = None
    got = ()
    fulls = {}
    for step in reversed(range(steps)):
        opening = step == steps - 1
        keep = step % 2 == 1 and not opening
        outs = [STATE, HALO, HALO, HALO] + ([STATE] if keep else [])
        lam, send_x, send_p, kd, *rest = call(
            functools.partial(backward_outer, step, opening, keep),
            outs,
            [meta, lam, *got, states[step], *halos[step], kk],
            [TILES, TILES, TILES, pltpu.VMEM((2 * NB * 8, 128), F32)],
        )
        if keep:
            fulls[(step + 1) // 2] = rest[0]
        got = (lax.ppermute(send_x, "space", cross), lax.ppermute(send_p, "space", near))
        lam, grad = call(
            functools.partial(backward_inner, step, opening),
            [STATE, GRADS],
            [meta, lam, states[step], kk, kd] + ([] if opening else [grad]),
            [TILES, TILES, TILES],
            flops=8000000,
        )
        if step == 1:
            swapped = lax.all_to_all(jnp.stack([fulls[max(s, 1)] for s in range(sections)]), "section", 0, 0, tiled=True)
    lams = [lam]
    for s in range(1, sections):
        lams.append(lax.ppermute(lam, "section", [(s, 0)]))
    (shared,) = call(end_kernel, [jax.ShapeDtypeStruct((sections, 4, ROWS, COLS), F32)], [meta, lam, *got, grad])
    shared = lax.all_to_all(shared, "section", 0, 0, tiled=True)
    adjoint, stiffness_grad = call(
        output_kernel, [jax.ShapeDtypeStruct((sections, 2, 6, ROWS, COLS), F32), GRADS], [meta, swapped, shared, *lams], placed=False
    )
    return (
        exit_state.reshape(1, 8, 6, ROWS, COLS),
        adjoint.reshape(1, 8, 6, ROWS, COLS),
        stiffness_grad,
    )


def solution(mesh):
    in_specs = (
        P(None, None, "space", None),
        P(None, "space", None),
        P("section", "space", None),
        P("section", "space", None),
        P("section", "space"),
        P(None, None, "space", None),
    )
    out_specs = (
        P("section", None, None, "space", None),
        P("section", None, None, "space", None),
        P(None, "space", None),
    )
    return jax.shard_map(on_device, mesh=mesh, in_specs=in_specs, out_specs=out_specs, check_vma=False)
```

time: 391 us -> 220 us (0.56)
  other arithmetic: 96.2 us -> 2.68 us
  Pallas kernels: 0 us -> 51.2 us
  local copies, waits for them, and re-layouts: 47.7 us -> 8.02 us
  loops' own time: 34.8 us -> 0 us
  starting transfers between devices: 148 us -> 114 us
  blocking collectives: 31 us -> 0 us
  waiting for transfers between devices: 14.2 us -> 41.5 us
  matrix products: 15.6 us -> 0 us
    reduce_sum x72 -> x0, other arithmetic: 66.7 us -> none  [the longest x16 25 us: contact(): jnp.sum(separation * separation, axis=0)]
    pallas_call x0 -> x35, Pallas kernels: none -> 51.2 us  [call(): pl.pallas_call(body, out_shape=outs, in_specs=[pl.BlockSpec(memory_space=...]
    ppermute x34 -> x38, starting transfers between devices: 144 us -> 103 us  [the longest x8 35.1 us: on_device(): lax.ppermute(send_p, 'space', near)]
    another operation x2 -> x0, loops' own time: 34.8 us -> none  [the longest x1 17.9 us: on_device(): lax.scan(backward_step, start_carry, (numbers, extended_all, velocity_all...]
    dynamic_slice x41 -> x2, local copies, waits for them, and re-layouts: 27.4 us -> 0.95 us  [the longest x1 0.94 us: on_device(): lam = lax.dynamic_slice_in_dim(cotangent, section * 2, 2, 0)]
    psum x1 -> x0, blocking collectives: 21.1 us -> none  [on_device(): summed_row, summed_column = lax.psum((grad_row, column_own), 'section')]
    all_to_all x1 -> x3, waiting for transfers between devices: 0.01 us -> 15.7 us  [the longest x1 11.6 us: on_device(): exit_state = lax.all_to_all(jnp.stack(exits), 'section', 0, 0, tiled=True)]
    dot_general x64 -> x0, matrix products: 15.6 us -> none  [the longest x24 5.87 us: contact(): jnp.einsum('pt,ctk->cpk', hits_b, tiles_all, precision=lax.Precision.HIGH...]
  transfers between devices with their start and end apart: 35 -> 41, of which waited for: 9 -> 10; matrix products, arithmetic and copies ran while one was open for 6% -> 2% of each run, Pallas kernels for 0% -> 15%
where the time goes in v1:
time: 220 us; the launch traced here: 218 us
  starting transfers between devices  114 us (52%)
  Pallas kernels  51.2 us (23%)
  waiting for transfers between devices  41.5 us (19%)
  local copies, waits for them, and re-layouts  8.02 us (4%)
  other arithmetic  2.68 us (1%)
    pallas_call x35, Pallas kernels, call(): pl.pallas_call(body, out_shape=outs, in_specs=[pl.BlockSpec(memory_space=...  51.2 us
    ppermute x8, starting transfers between devices, on_device(): lax.ppermute(send_p, 'space', near)  35.1 us
    ppermute x8, starting transfers between devices, on_device(): halo_p = lax.ppermute(send_p, 'space', near)  28.8 us
    ppermute x3, waiting for transfers between devices, on_device(): lams.append(lax.ppermute(lam, 'section', [(s, 0)]))  15.9 us
    ppermute x8, starting transfers between devices, on_device(): lax.ppermute(send_x, 'space', cross)  15.4 us
    ppermute x8, starting transfers between devices, on_device(): halo_x = lax.ppermute(send_x, 'space', cross)  15.3 us
    all_to_all x1, waiting for transfers between devices, on_device(): exit_state = lax.all_to_all(jnp.stack(exits), 'section', 0, 0, tiled=True)  11.6 us
    ppermute x8, waiting for transfers between devices, on_device(): halo_x = lax.ppermute(send_x, 'space', cross)  9.56 us
  transfers between devices with their start and end apart: 41, of which 10 were waited for; matrix products, arithmetic and copies ran while one was open for 2% of the time, Pallas kernels for 15%

profile of v1, /device:TPU:102, one launch (start us, length us, event | category | flops | bytes accessed | tf_op | source)
XLA Modules:
  0.0 218.3 jit_solution(11275786426181728350)
XLA Ops:
  2.4 3.0 %collective-permute-start.2 = (s32[1,64]{1,0:T(1,128)S(1)}, s32[1,64]{1,0:T(1,128)S(1)}, u32[]{:S(2)}, u32[]{:S(2)}) collective-permute-start(s32[1,64]{1,0:T(1,128)S(1)} %reshape.15.meta), channel_id=1, source_target_pairs={{0,192},{64,0},{128,64},{192,128},{1,193},{65,1},{129,65},{193,129... | collective-permute-start | bytes 776 | tf_op jit(solution)/shard_map/ppermute | solution.py:496
  10.4 3.2 %collective-permute-start.4 = (f32[8,512]{1,0:T(8,128)S(1)}, f32[8,512]{1,0:T(8,128)S(1)}, u32[]{:S(2)}, u32[]{:S(2)}) collective-permute-start(f32[8,512]{1,0:T(8,128)S(1)} %get-tuple-element.83), channel_id=1, source_target_pairs={{0,1},{1,0},{2,3},{3,2},{4,5},{5,4},{6,7},{7,6},{8,9},{9,8},{10,11... | collective-permute-start | bytes 49160 | tf_op jit(solution)/shard_map/ppermute | solution.py:506
  23.2 3.6 %collective-permute-start.8 = (f32[8,512]{1,0:T(8,128)S(1)}, f32[8,512]{1,0:T(8,128)S(1)}, u32[]{:S(2)}, u32[]{:S(2)}) collective-permute-start(f32[8,512]{1,0:T(8,128)S(1)} %get-tuple-element.89), channel_id=1, source_target_pairs={{0,1},{1,0},{2,3},{3,2},{4,5},{5,4},{6,7},{7,6},{8,9},{9,8},{10,11... | collective-permute-start | bytes 49160 | tf_op jit(solution)/shard_map/ppermute | solution.py:506
  33.1 3.4 %collective-permute-start.10 = (f32[8,512]{1,0:T(8,128)S(1)}, f32[8,512]{1,0:T(8,128)S(1)}, u32[]{:S(2)}, u32[]{:S(2)}) collective-permute-start(f32[8,512]{1,0:T(8,128)S(1)} %get-tuple-element.92), channel_id=1, source_target_pairs={{0,1},{1,0},{2,3},{3,2},{4,5},{5,4},{6,7},{7,6},{8,9},{9,8},{10,11... | collective-permute-start | bytes 49160 | tf_op jit(solution)/shard_map/ppermute | solution.py:506
  42.4 3.4 %collective-permute-start.12 = (f32[8,512]{1,0:T(8,128)S(1)}, f32[8,512]{1,0:T(8,128)S(1)}, u32[]{:S(2)}, u32[]{:S(2)}) collective-permute-start(f32[8,512]{1,0:T(8,128)S(1)} %get-tuple-element.95), channel_id=1, source_target_pairs={{0,1},{1,0},{2,3},{3,2},{4,5},{5,4},{6,7},{7,6},{8,9},{9,8},{10,11... | collective-permute-start | bytes 49160 | tf_op jit(solution)/shard_map/ppermute | solution.py:506
  51.7 3.8 %collective-permute-start.14 = (f32[8,512]{1,0:T(8,128)S(1)}, f32[8,512]{1,0:T(8,128)S(1)}, u32[]{:S(2)}, u32[]{:S(2)}) collective-permute-start(f32[8,512]{1,0:T(8,128)S(1)} %get-tuple-element.98), channel_id=1, source_target_pairs={{0,1},{1,0},{2,3},{3,2},{4,5},{5,4},{6,7},{7,6},{8,9},{9,8},{10,11... | collective-permute-start | bytes 49160 | tf_op jit(solution)/shard_map/ppermute | solution.py:506
  61.4 3.4 %collective-permute-start.16 = (f32[8,512]{1,0:T(8,128)S(1)}, f32[8,512]{1,0:T(8,128)S(1)}, u32[]{:S(2)}, u32[]{:S(2)}) collective-permute-start(f32[8,512]{1,0:T(8,128)S(1)} %get-tuple-element.101), channel_id=1, source_target_pairs={{0,1},{1,0},{2,3},{3,2},{4,5},{5,4},{6,7},{7,6},{8,9},{9,8},{10,11... | collective-permute-start | bytes 49160 | tf_op jit(solution)/shard_map/ppermute | solution.py:506
  72.8 7.4 %collective-permute-start.18 = (f32[8,512]{1,0:T(8,128)S(1)}, f32[8,512]{1,0:T(8,128)S(1)}, u32[]{:S(2)}, u32[]{:S(2)}) collective-permute-start(f32[8,512]{1,0:T(8,128)S(1)} %get-tuple-element.104), channel_id=1, source_target_pairs={{0,1},{1,0},{2,3},{3,2},{4,5},{5,4},{6,7},{7,6},{8,9},{9,8},{10,11... | collective-permute-start | bytes 49160 | tf_op jit(solution)/shard_map/ppermute | solution.py:506
  84.0 6.1 %collective-permute-start.20 = (f32[8,512]{1,0:T(8,128)S(1)}, f32[8,512]{1,0:T(8,128)S(1)}, u32[]{:S(2)}, u32[]{:S(2)}) collective-permute-start(f32[8,512]{1,0:T(8,128)S(1)} %get-tuple-element.110), channel_id=1, source_target_pairs={{0,1},{1,0},{2,3},{3,2},{4,5},{5,4},{6,7},{7,6},{8,9},{9,8},{10,11... | collective-permute-start | bytes 49160 | tf_op jit(solution)/shard_map/ppermute | solution.py:538
  94.8 5.2 %collective-permute-start.22 = (f32[8,512]{1,0:T(8,128)S(1)}, f32[8,512]{1,0:T(8,128)S(1)}, u32[]{:S(2)}, u32[]{:S(2)}) collective-permute-start(f32[8,512]{1,0:T(8,128)S(1)} %get-tuple-element.116), channel_id=1, source_target_pairs={{0,1},{1,0},{2,3},{3,2},{4,5},{5,4},{6,7},{7,6},{8,9},{9,8},{10,11... | collective-permute-start | bytes 49160 | tf_op jit(solution)/shard_map/ppermute | solution.py:538
  106.0 4.0 %collective-permute-start.24 = (f32[8,512]{1,0:T(8,128)S(1)}, f32[8,512]{1,0:T(8,128)S(1)}, u32[]{:S(2)}, u32[]{:S(2)}) collective-permute-start(f32[8,512]{1,0:T(8,128)S(1)} %get-tuple-element.122), channel_id=1, source_target_pairs={{0,1},{1,0},{2,3},{3,2},{4,5},{5,4},{6,7},{7,6},{8,9},{9,8},{10,11... | collective-permute-start | bytes 49160 | tf_op jit(solution)/shard_map/ppermute | solution.py:538
  116.0 3.2 %collective-permute-start.26 = (f32[8,512]{1,0:T(8,128)S(1)}, f32[8,512]{1,0:T(8,128)S(1)}, u32[]{:S(2)}, u32[]{:S(2)}) collective-permute-start(f32[8,512]{1,0:T(8,128)S(1)} %get-tuple-element.128), channel_id=1, source_target_pairs={{0,1},{1,0},{2,3},{3,2},{4,5},{5,4},{6,7},{7,6},{8,9},{9,8},{10,11... | collective-permute-start | bytes 49160 | tf_op jit(solution)/shard_map/ppermute | solution.py:538
  119.2 3.2 %shard_map.109 = (f32[2,6,8,512]{3,2,1,0:T(8,128)S(1)}, f32[2,8,512]{2,1,0:T(8,128)S(1)}) custom-call(s32[4,64]{1,0:T(4,128)} %pad_add_fusion.meta, f32[2,6,8,512]{3,2,1,0:T(8,128)S(1)} %get-tuple-element.123.lam, f32[2,6,8,512]{3,2,1,0:T(8,128)S(1)} %get-tuple-element.93.state.refs_2_, f32[2,8,512]{2,1,0:T(8,128)S(1)} %get-tuple-element.82.kk.refs_3_.refs_5_, ...), custom_call_target="tpu_custom_call" | custom-call | flops 8000000 | bytes 262144 | tf_op jit(solution)/shard_map/pallas_call | solution.py:466
  125.8 2.7 %collective-permute-start.28 = (f32[8,512]{1,0:T(8,128)S(1)}, f32[8,512]{1,0:T(8,128)S(1)}, u32[]{:S(2)}, u32[]{:S(2)}) collective-permute-start(f32[8,512]{1,0:T(8,128)S(1)} %get-tuple-element.134), channel_id=1, source_target_pairs={{0,1},{1,0},{2,3},{3,2},{4,5},{5,4},{6,7},{7,6},{8,9},{9,8},{10,11... | collective-permute-start | bytes 49160 | tf_op jit(solution)/shard_map/ppermute | solution.py:538
  133.6 4.9 %collective-permute-start.30 = (f32[8,512]{1,0:T(8,128)S(1)}, f32[8,512]{1,0:T(8,128)S(1)}, u32[]{:S(2)}, u32[]{:S(2)}) collective-permute-start(f32[8,512]{1,0:T(8,128)S(1)} %get-tuple-element.140), channel_id=1, source_target_pairs={{0,1},{1,0},{2,3},{3,2},{4,5},{5,4},{6,7},{7,6},{8,9},{9,8},{10,11... | collective-permute-start | bytes 49160 | tf_op jit(solution)/shard_map/ppermute | solution.py:538
  143.8 4.8 %collective-permute-start.32 = (f32[8,512]{1,0:T(8,128)S(1)}, f32[8,512]{1,0:T(8,128)S(1)}, u32[]{:S(2)}, u32[]{:S(2)}) collective-permute-start(f32[8,512]{1,0:T(8,128)S(1)} %get-tuple-element.149), channel_id=1, source_target_pairs={{0,1},{1,0},{2,3},{3,2},{4,5},{5,4},{6,7},{7,6},{8,9},{9,8},{10,11... | collective-permute-start | bytes 49160 | tf_op jit(solution)/shard_map/ppermute | solution.py:538
  153.8 4.1 %collective-permute-start.34 = (f32[8,512]{1,0:T(8,128)S(1)}, f32[8,512]{1,0:T(8,128)S(1)}, u32[]{:S(2)}, u32[]{:S(2)}) collective-permute-start(f32[8,512]{1,0:T(8,128)S(1)} %get-tuple-element.155), channel_id=1, source_target_pairs={{0,1},{1,0},{2,3},{3,2},{4,5},{5,4},{6,7},{7,6},{8,9},{9,8},{10,11... | collective-permute-start | bytes 49160 | tf_op jit(solution)/shard_map/ppermute | solution.py:538
  157.9 2.4 %shard_map.117 = (f32[2,6,8,512]{3,2,1,0:T(8,128)S(1)}, f32[2,8,512]{2,1,0:T(8,128)S(1)}) custom-call(s32[4,64]{1,0:T(4,128)} %pad_add_fusion.meta, f32[2,6,8,512]{3,2,1,0:T(8,128)S(1)} %get-tuple-element.150.lam, f32[2,6,8,512]{3,2,1,0:T(8,128)S(1)} %constant_dynamic-slice_fusion.1.state.refs_2_, f32[2,8,512]{2,1,0:T(8,128)S(1)} %get-tuple-element.82.kk.refs_3_.refs_5_, ...), custom_call_target="tpu_custom_call" | custom-call | flops 8000000 | bytes 262144 | tf_op jit(solution)/shard_map/pallas_call | solution.py:466
  161.9 3.5 %all-to-all-start.2 = ((f32[4,4,8,512]{3,2,1,0:T(8,128)}), f32[4,4,8,512]{3,2,1,0:T(8,128)S(1)}, u32[]{:S(2)}, u32[]{:S(2)}) async-start(f32[4,4,8,512]{3,2,1,0:T(8,128)} %shard_map.118), calls=%async_computation.2 | async-start | bytes 524288 | tf_op jit(solution)/shard_map/all_to_all | solution.py:552
  169.1 4.1 %all-to-all-done.2.shared = f32[4,4,8,512]{3,2,1,0:T(8,128)S(1)} async-done(((f32[4,4,8,512]{3,2,1,0:T(8,128)}), f32[4,4,8,512]{3,2,1,0:T(8,128)S(1)}, u32[]{:S(2)}, u32[]{:S(2)}) %all-to-all-start.2) | async-done | bytes 262176 | tf_op jit(solution)/shard_map/all_to_all | solution.py:552
  173.9 3.5 %all-to-all-start = ((f32[4,2,6,8,512]{4,3,2,1,0:T(8,128)}), f32[4,2,6,8,512]{4,3,2,1,0:T(8,128)S(1)}, u32[]{:S(2)}, u32[]{:S(2)}) async-start(f32[4,2,6,8,512]{4,3,2,1,0:T(8,128)} %pad_maximum_fusion), calls=%async_computation | async-start | bytes 1572864 | tf_op jit(solution)/shard_map/all_to_all | solution.py:521
  178.4 11.6 %all-to-all-done = f32[4,2,6,8,512]{4,3,2,1,0:T(8,128)S(1)} async-done(((f32[4,2,6,8,512]{4,3,2,1,0:T(8,128)}), f32[4,2,6,8,512]{4,3,2,1,0:T(8,128)S(1)}, u32[]{:S(2)}, u32[]{:S(2)}) %all-to-all-start) | async-done | bytes 786464 | tf_op jit(solution)/shard_map/all_to_all | solution.py:521
  190.0 3.5 %all-to-all-start.1 = ((f32[4,2,6,8,512]{4,3,2,1,0:T(8,128)}), f32[4,2,6,8,512]{4,3,2,1,0:T(8,128)S(1)}, u32[]{:S(2)}, u32[]{:S(2)}) async-start(f32[4,2,6,8,512]{4,3,2,1,0:T(8,128)} %pad_maximum_fusion.1), calls=%async_computation.1 | async-start | bytes 1572864 | tf_op jit(solution)/shard_map/all_to_all | solution.py:547
  197.4 15.9 %collective-permute-done.37.refs_3_ = f32[2,6,8,512]{3,2,1,0:T(8,128)S(1)} collective-permute-done((f32[2,6,8,512]{3,2,1,0:T(8,128)S(1)}, f32[2,6,8,512]{3,2,1,0:T(8,128)S(1)}, u32[]{:S(2)}, u32[]{:S(2)}) %collective-permute-start.37) | collective-permute-done | bytes 196640 | tf_op jit(solution)/shard_map/ppermute | solution.py:550
  (154 shorter events, 102.6 us)
Async XLA Ops:
  2.4 11.2 %collective-permute-start.2 = (s32[1,64]{1,0:T(1,128)S(1)}, s32[1,64]{1,0:T(1,128)S(1)}, u32[]{:S(2)}, u32[]{:S(2)}) collective-permute-start(s32[1,64]{1,0:T(1,128)S(1)} %reshape.15.meta), channel_id=1, source_target_pairs={{0,192},{64,0},{128,64},{192,128},{1,193},{65,1},{129,65},{193,129... | collective-permute-start | bytes 776 | tf_op jit(solution)/shard_map/ppermute | solution.py:496
  5.4 8.2 %collective-permute-start.1 = (s32[1,64]{1,0:T(1,128)S(1)}, s32[1,64]{1,0:T(1,128)S(1)}, u32[]{:S(2)}, u32[]{:S(2)}) collective-permute-start(s32[1,64]{1,0:T(1,128)S(1)} %reshape.15.meta), channel_id=1, source_target_pairs={{0,128},{64,192},{128,0},{192,64},{1,129},{65,193},{129,1},{193,65... | collective-permute-start | bytes 776 | tf_op jit(solution)/shard_map/ppermute | solution.py:496
  6.0 7.6 %collective-permute-start = (s32[1,64]{1,0:T(1,128)S(1)}, s32[1,64]{1,0:T(1,128)S(1)}, u32[]{:S(2)}, u32[]{:S(2)}) collective-permute-start(s32[1,64]{1,0:T(1,128)S(1)} %reshape.15.meta), channel_id=1, source_target_pairs={{0,64},{64,128},{128,192},{192,0},{1,65},{65,129},{129,193},{193,1... | collective-permute-start | bytes 776 | tf_op jit(solution)/shard_map/ppermute | solution.py:496
  8.5 7.6 %collective-permute-start.3 = (f32[8,512]{1,0:T(8,128)S(1)}, f32[8,512]{1,0:T(8,128)S(1)}, u32[]{:S(2)}, u32[]{:S(2)}) collective-permute-start(f32[8,512]{1,0:T(8,128)S(1)} %get-tuple-element.81), channel_id=1, source_target_pairs={{1,2},{3,4},{5,6},{7,8},{9,10},{11,12},{13,14},{15,16},{17,18},{19... | collective-permute-start | bytes 49160 | tf_op jit(solution)/shard_map/ppermute | solution.py:505
  70.9 10.3 %collective-permute-start.17 = (f32[8,512]{1,0:T(8,128)S(1)}, f32[8,512]{1,0:T(8,128)S(1)}, u32[]{:S(2)}, u32[]{:S(2)}) collective-permute-start(f32[8,512]{1,0:T(8,128)S(1)} %get-tuple-element.103), channel_id=1, source_target_pairs={{1,2},{3,4},{5,6},{7,8},{9,10},{11,12},{13,14},{15,16},{17,18},{19... | collective-permute-start | bytes 49160 | tf_op jit(solution)/shard_map/ppermute | solution.py:505
  72.8 8.4 %collective-permute-start.18 = (f32[8,512]{1,0:T(8,128)S(1)}, f32[8,512]{1,0:T(8,128)S(1)}, u32[]{:S(2)}, u32[]{:S(2)}) collective-permute-start(f32[8,512]{1,0:T(8,128)S(1)} %get-tuple-element.104), channel_id=1, source_target_pairs={{0,1},{1,0},{2,3},{3,2},{4,5},{5,4},{6,7},{7,6},{8,9},{9,8},{10,11... | collective-permute-start | bytes 49160 | tf_op jit(solution)/shard_map/ppermute | solution.py:506
  82.1 9.9 %collective-permute-start.19 = (f32[8,512]{1,0:T(8,128)S(1)}, f32[8,512]{1,0:T(8,128)S(1)}, u32[]{:S(2)}, u32[]{:S(2)}) collective-permute-start(f32[8,512]{1,0:T(8,128)S(1)} %get-tuple-element.109), channel_id=1, source_target_pairs={{1,2},{3,4},{5,6},{7,8},{9,10},{11,12},{13,14},{15,16},{17,18},{19... | collective-permute-start | bytes 49160 | tf_op jit(solution)/shard_map/ppermute | solution.py:538
  84.0 8.0 %collective-permute-start.20 = (f32[8,512]{1,0:T(8,128)S(1)}, f32[8,512]{1,0:T(8,128)S(1)}, u32[]{:S(2)}, u32[]{:S(2)}) collective-permute-start(f32[8,512]{1,0:T(8,128)S(1)} %get-tuple-element.110), channel_id=1, source_target_pairs={{0,1},{1,0},{2,3},{3,2},{4,5},{5,4},{6,7},{7,6},{8,9},{9,8},{10,11... | collective-permute-start | bytes 49160 | tf_op jit(solution)/shard_map/ppermute | solution.py:538
  92.9 9.0 %collective-permute-start.21 = (f32[8,512]{1,0:T(8,128)S(1)}, f32[8,512]{1,0:T(8,128)S(1)}, u32[]{:S(2)}, u32[]{:S(2)}) collective-permute-start(f32[8,512]{1,0:T(8,128)S(1)} %get-tuple-element.115), channel_id=1, source_target_pairs={{1,2},{3,4},{5,6},{7,8},{9,10},{11,12},{13,14},{15,16},{17,18},{19... | collective-permute-start | bytes 49160 | tf_op jit(solution)/shard_map/ppermute | solution.py:538
  94.8 7.1 %collective-permute-start.22 = (f32[8,512]{1,0:T(8,128)S(1)}, f32[8,512]{1,0:T(8,128)S(1)}, u32[]{:S(2)}, u32[]{:S(2)}) collective-permute-start(f32[8,512]{1,0:T(8,128)S(1)} %get-tuple-element.116), channel_id=1, source_target_pairs={{0,1},{1,0},{2,3},{3,2},{4,5},{5,4},{6,7},{7,6},{8,9},{9,8},{10,11... | collective-permute-start | bytes 49160 | tf_op jit(solution)/shard_map/ppermute | solution.py:538
  104.1 9.1 %collective-permute-start.23 = (f32[8,512]{1,0:T(8,128)S(1)}, f32[8,512]{1,0:T(8,128)S(1)}, u32[]{:S(2)}, u32[]{:S(2)}) collective-permute-start(f32[8,512]{1,0:T(8,128)S(1)} %get-tuple-element.121), channel_id=1, source_target_pairs={{1,2},{3,4},{5,6},{7,8},{9,10},{11,12},{13,14},{15,16},{17,18},{19... | collective-permute-start | bytes 49160 | tf_op jit(solution)/shard_map/ppermute | solution.py:538
  106.0 7.2 %collective-permute-start.24 = (f32[8,512]{1,0:T(8,128)S(1)}, f32[8,512]{1,0:T(8,128)S(1)}, u32[]{:S(2)}, u32[]{:S(2)}) collective-permute-start(f32[8,512]{1,0:T(8,128)S(1)} %get-tuple-element.122), channel_id=1, source_target_pairs={{0,1},{1,0},{2,3},{3,2},{4,5},{5,4},{6,7},{7,6},{8,9},{9,8},{10,11... | collective-permute-start | bytes 49160 | tf_op jit(solution)/shard_map/ppermute | solution.py:538
  114.1 8.3 %collective-permute-start.25 = (f32[8,512]{1,0:T(8,128)S(1)}, f32[8,512]{1,0:T(8,128)S(1)}, u32[]{:S(2)}, u32[]{:S(2)}) collective-permute-start(f32[8,512]{1,0:T(8,128)S(1)} %get-tuple-element.127), channel_id=1, source_target_pairs={{1,2},{3,4},{5,6},{7,8},{9,10},{11,12},{13,14},{15,16},{17,18},{19... | collective-permute-start | bytes 49160 | tf_op jit(solution)/shard_map/ppermute | solution.py:538
  131.7 9.3 %collective-permute-start.29 = (f32[8,512]{1,0:T(8,128)S(1)}, f32[8,512]{1,0:T(8,128)S(1)}, u32[]{:S(2)}, u32[]{:S(2)}) collective-permute-start(f32[8,512]{1,0:T(8,128)S(1)} %get-tuple-element.139), channel_id=1, source_target_pairs={{1,2},{3,4},{5,6},{7,8},{9,10},{11,12},{13,14},{15,16},{17,18},{19... | collective-permute-start | bytes 49160 | tf_op jit(solution)/shard_map/ppermute | solution.py:538
  133.6 7.4 %collective-permute-start.30 = (f32[8,512]{1,0:T(8,128)S(1)}, f32[8,512]{1,0:T(8,128)S(1)}, u32[]{:S(2)}, u32[]{:S(2)}) collective-permute-start(f32[8,512]{1,0:T(8,128)S(1)} %get-tuple-element.140), channel_id=1, source_target_pairs={{0,1},{1,0},{2,3},{3,2},{4,5},{5,4},{6,7},{7,6},{8,9},{9,8},{10,11... | collective-permute-start | bytes 49160 | tf_op jit(solution)/shard_map/ppermute | solution.py:538
  141.9 8.5 %collective-permute-start.31 = (f32[8,512]{1,0:T(8,128)S(1)}, f32[8,512]{1,0:T(8,128)S(1)}, u32[]{:S(2)}, u32[]{:S(2)}) collective-permute-start(f32[8,512]{1,0:T(8,128)S(1)} %get-tuple-element.148), channel_id=1, source_target_pairs={{1,2},{3,4},{5,6},{7,8},{9,10},{11,12},{13,14},{15,16},{17,18},{19... | collective-permute-start | bytes 49160 | tf_op jit(solution)/shard_map/ppermute | solution.py:538
  151.9 8.5 %collective-permute-start.33 = (f32[8,512]{1,0:T(8,128)S(1)}, f32[8,512]{1,0:T(8,128)S(1)}, u32[]{:S(2)}, u32[]{:S(2)}) collective-permute-start(f32[8,512]{1,0:T(8,128)S(1)} %get-tuple-element.154), channel_id=1, source_target_pairs={{1,2},{3,4},{5,6},{7,8},{9,10},{11,12},{13,14},{15,16},{17,18},{19... | collective-permute-start | bytes 49160 | tf_op jit(solution)/shard_map/ppermute | solution.py:538
  153.8 6.6 %collective-permute-start.34 = (f32[8,512]{1,0:T(8,128)S(1)}, f32[8,512]{1,0:T(8,128)S(1)}, u32[]{:S(2)}, u32[]{:S(2)}) collective-permute-start(f32[8,512]{1,0:T(8,128)S(1)} %get-tuple-element.155), channel_id=1, source_target_pairs={{0,1},{1,0},{2,3},{3,2},{4,5},{5,4},{6,7},{7,6},{8,9},{9,8},{10,11... | collective-permute-start | bytes 49160 | tf_op jit(solution)/shard_map/ppermute | solution.py:538
  161.9 11.4 %all-to-all-start.2 = ((f32[4,4,8,512]{3,2,1,0:T(8,128)}), f32[4,4,8,512]{3,2,1,0:T(8,128)S(1)}, u32[]{:S(2)}, u32[]{:S(2)}) async-start(f32[4,4,8,512]{3,2,1,0:T(8,128)} %shard_map.118), calls=%async_computation.2 | async-start | bytes 524288 | tf_op jit(solution)/shard_map/all_to_all | solution.py:552
  173.9 16.0 %all-to-all-start = ((f32[4,2,6,8,512]{4,3,2,1,0:T(8,128)}), f32[4,2,6,8,512]{4,3,2,1,0:T(8,128)S(1)}, u32[]{:S(2)}, u32[]{:S(2)}) async-start(f32[4,2,6,8,512]{4,3,2,1,0:T(8,128)} %pad_maximum_fusion), calls=%async_computation | async-start | bytes 1572864 | tf_op jit(solution)/shard_map/all_to_all | solution.py:521
  190.0 23.4 %all-to-all-start.1 = ((f32[4,2,6,8,512]{4,3,2,1,0:T(8,128)}), f32[4,2,6,8,512]{4,3,2,1,0:T(8,128)S(1)}, u32[]{:S(2)}, u32[]{:S(2)}) async-start(f32[4,2,6,8,512]{4,3,2,1,0:T(8,128)} %pad_maximum_fusion.1), calls=%async_computation.1 | async-start | bytes 1572864 | tf_op jit(solution)/shard_map/all_to_all | solution.py:547
  193.5 19.8 %collective-permute-start.37 = (f32[2,6,8,512]{3,2,1,0:T(8,128)S(1)}, f32[2,6,8,512]{3,2,1,0:T(8,128)S(1)}, u32[]{:S(2)}, u32[]{:S(2)}) collective-permute-start(f32[2,6,8,512]{3,2,1,0:T(8,128)S(1)} %get-tuple-element.153.lam.refs_0_), channel_id=1, source_target_pairs={{192,0},{193,1},{194,2},{195,3},{196,4},{197,5},{198,6},{199,7},{2... | collective-permute-start | bytes 589832 | tf_op jit(solution)/shard_map/ppermute | solution.py:550
  194.8 18.5 %collective-permute-start.36 = (f32[2,6,8,512]{3,2,1,0:T(8,128)S(1)}, f32[2,6,8,512]{3,2,1,0:T(8,128)S(1)}, u32[]{:S(2)}, u32[]{:S(2)}) collective-permute-start(f32[2,6,8,512]{3,2,1,0:T(8,128)S(1)} %get-tuple-element.153.lam.refs_0_), channel_id=1, source_target_pairs={{128,0},{129,1},{130,2},{131,3},{132,4},{133,5},{134,6},{135,7},{1... | collective-permute-start | bytes 589832 | tf_op jit(solution)/shard_map/ppermute | solution.py:550
  196.1 17.2 %collective-permute-start.35 = (f32[2,6,8,512]{3,2,1,0:T(8,128)S(1)}, f32[2,6,8,512]{3,2,1,0:T(8,128)S(1)}, u32[]{:S(2)}, u32[]{:S(2)}) collective-permute-start(f32[2,6,8,512]{3,2,1,0:T(8,128)S(1)} %get-tuple-element.153.lam.refs_0_), channel_id=1, source_target_pairs={{64,0},{65,1},{66,2},{67,3},{68,4},{69,5},{70,6},{71,7},{72,8},{73... | collective-permute-start | bytes 589832 | tf_op jit(solution)/shard_map/ppermute | solution.py:550
  (42 other events, 170.0 us)

commit v2 on v1

--- a/solution.py
+++ b/solution.py
@@ -15,6 +15,7 @@
 TINY = 1e-06
 F32 = jnp.float32
 BF16 = jnp.bfloat16
+COPY_STEP = 3
 GROUP = 2
 SLOTS = 8
 ROWS = 8
@@ -105,8 +106,8 @@
     return scale * stacked(rows)
 
 
-def pair_adjoint(xa, xb, ga, marks, scale):
-    from_a = differences(xa, xb, marks)
+def pair_adjoint(xa, xb, ga, marks, scale_a, scale_b):
+    from_a = differences(xa, xb, marks) if scale_a is not None else None
     from_b = differences(xb, xa, marks)
     g_sub = spread(jnp.concatenate(pieces(ga), axis=0), marks)
     rows_a, rows_b = [], []
@@ -115,11 +116,13 @@
         sum_a = [jnp.zeros((8, 128), F32) for _ in range(3)]
         sum_b = [jnp.zeros((8, 128), F32) for _ in range(3)]
         for j in range(16):
-            sum_a = pair_sum(sum_a, [block(from_a, j, 3 * t + c) for c in range(3)], g)
+            if scale_a is not None:
+                sum_a = pair_sum(sum_a, [block(from_a, j, 3 * t + c) for c in range(3)], g)
             sum_b = pair_sum(sum_b, [block(from_b, j, 3 * t + c) for c in range(3)], [block(g_sub, j, 3 * t + c) for c in range(3)])
         rows_a += sum_a
         rows_b += sum_b
-    return scale * stacked(rows_a), -scale * stacked(rows_b)
+    con_a = scale_a * stacked(rows_a) if scale_a is not None else None
+    return con_a, -scale_b * stacked(rows_b)
 
 
 def pair_sum(total, d, g):
@@ -275,7 +278,7 @@
     state, halo_x, halo_p, kk, lam_out, send_x, send_p, kd = refs[:8]
     refs = refs[8:]
     full = refs.pop(0) if keep else None
-    tiles, grads, acc, acc_b = refs
+    tiles, grads, acc_b = refs
     first = meta[0, META_C] == 0
     row, base = lists(meta, step)
     count = meta[row, base + 2 * SLOTS]
@@ -326,7 +329,6 @@
 
     @pl.when(some)
     def _():
-        acc[...] = jnp.zeros(acc.shape, F32)
         acc_b[...] = jnp.zeros(acc_b.shape, F32)
         fill_tiles(tiles, lambda t, c: state[t, c])
         fill_halo(tiles, up, down)
@@ -341,33 +343,35 @@
             def _():
                 at = tile_start(a // NB + 1, lax.rem(a, NB))
                 bt = tile_start(b // NB, lax.rem(b, NB))
-                con_a, con_b = pair_adjoint(tiles[pl.ds(at, 8), :], tiles[pl.ds(bt, 8), :], grads[pl.ds(at, 8), :], marks, SCALE)
-                acc[pl.ds(at, 8), :] += con_a
+                _, con_b = pair_adjoint(tiles[pl.ds(at, 8), :], tiles[pl.ds(bt, 8), :], grads[pl.ds(at, 8), :], marks, None, SCALE)
                 out = pl.multiple_of(8 * jnp.where(b < NB, b, b - NB * (EXT - 2)), 8)
                 acc_b[pl.ds(out, 8), :] += con_b
 
             return carry
 
         lax.fori_loop(0, count, slot, 0)
-        for t in range(2):
-            for c in range(3):
-                lam_out[t, c] = lam_out[t, c] + read_tiles(acc, 3 * t + c)
         more_up = jnp.concatenate([acc_b[8 * b : 8 * b + 8, :] for b in range(NB)], axis=1)
         more_down = jnp.concatenate([acc_b[8 * (NB + b) : 8 * (NB + b) + 8, :] for b in range(NB)], axis=1)
         send_x[...] += jnp.where(first, more_up, more_down)
         send_p[...] += jnp.where(first, more_down, more_up)
 
 
-def backward_inner(step, opening, meta, lam, state, kk, kd, *refs):
+def backward_inner(step, opening, meta, lam, state, halo_x, halo_p, kk, kd, *refs):
     refs = list(refs)
     old = None if opening else refs.pop(0)
+    copies = []
+    if step == COPY_STEP:
+        source, target, sems = refs.pop(0), refs.pop(2), refs.pop()
+        copies = [pltpu.make_async_copy(source.at[s], target.at[s], sems.at[s]) for s in range(4)]
+        for copy in copies:
+            copy.start()
     lam_out, grad, tiles, grads, acc = refs
     row, base = lists(meta, step)
     last = meta[0, META_Q] == 63
     fill_tiles(tiles, lambda t, c: state[t, c])
     fill_tiles(grads, lambda t, c: H * lam[t, 3 + c])
-    zero = jnp.zeros((8, COLS), F32)
-    fill_halo(tiles, zero, zero)
+    first = meta[0, META_C] == 0
+    fill_halo(tiles, jnp.where(first, halo_x[...], halo_p[...]), jnp.where(first, halo_p[...], halo_x[...]))
     acc[...] = jnp.zeros(acc.shape, F32)
     count = meta[row, base + 2 * SLOTS]
     marks = selectors()
@@ -378,11 +382,12 @@
             p = i * GROUP + q
             a = meta[row, base + p]
             b = meta[row, base + SLOTS + p]
-            live = jnp.logical_and(p < count, jnp.logical_and(b >= NB, b < NB * (EXT - 1)))
+            live = p < count
+            inside = jnp.logical_and(live, jnp.logical_and(b >= NB, b < NB * (EXT - 1)))
             at = tile_start(a // NB + 1, lax.rem(a, NB))
             bt = tile_start(b // NB, lax.rem(b, NB))
-            scale = jnp.where(live, SCALE, 0.0)
-            results.append((at, bt, *pair_adjoint(tiles[pl.ds(at, 8), :], tiles[pl.ds(bt, 8), :], grads[pl.ds(at, 8), :], marks, scale)))
+            scales = [jnp.where(on, SCALE, 0.0) for on in (live, inside)]
+            results.append((at, bt, *pair_adjoint(tiles[pl.ds(at, 8), :], tiles[pl.ds(bt, 8), :], grads[pl.ds(at, 8), :], marks, *scales)))
         for at, bt, con_a, con_b in results:
             acc[pl.ds(at, 8), :] += con_a
             acc[pl.ds(bt, 8), :] += con_b
@@ -413,6 +418,8 @@
     else:
         grad[0] = old[0] + grad_h
         grad[1] = old[1] + grad_v
+    for copy in copies:
+        copy.wait()
 
 
 def end_kernel(meta, lam, got_x, got_p, old, out):
@@ -420,54 +427,68 @@
     last = meta[0, META_Q] == 63
     xbar, got_k = joined(first, lam, got_x, got_p)
     zero = jnp.zeros((2, COLS), F32)
-    tops = jnp.concatenate([v[0:1] for v in xbar] + [zero], axis=0)
-    lows = jnp.concatenate([v[7:8] for v in xbar] + [zero], axis=0)
-    below = old[1] + jnp.where(row_is(7), jnp.where(last, 0.0, got_k), 0.0)
-    for s in range(out.shape[0]):
-        out[s, 0] = old[0]
-        out[s, 1] = below
-        out[s, 2] = tops
-        out[s, 3] = lows
-
-
-def output_kernel(meta, swapped, shared, *refs):
-    *lams, adjoint, grad = refs
+    out[0] = old[0]
+    out[1] = old[1] + jnp.where(row_is(7), jnp.where(last, 0.0, got_k), 0.0)
+    out[2] = jnp.concatenate([v[0:1] for v in xbar] + [zero], axis=0)
+    out[3] = jnp.concatenate([v[7:8] for v in xbar] + [zero], axis=0)
+
+
+def output_kernel(sections, meta, swapped, *refs):
+    shared, lams = refs[:sections], refs[sections : 2 * sections]
+    adjoint, grad, buffer, total, sems = refs[2 * sections :]
     here = meta[0, META_S] == 0
-    for k in range(2):
-        grad[k] = shared[0, k] + shared[1, k] + shared[2, k] + shared[3, k]
+
+    @pl.when(jnp.logical_not(here))
+    def _():
+        for s in range(sections):
+            pltpu.make_async_copy(swapped.at[s], adjoint.at[s], sems.at[s]).start()
 
     @pl.when(here)
     def _():
         for s, lam in enumerate(lams):
+            part = shared[-s % sections]
             for t in range(2):
                 for c in range(3):
                     k = 3 * t + c
-                    v = jnp.where(row_is(0), shared[s, 2, k : k + 1], lam[t, c])
-                    adjoint[s, t, c] = jnp.where(row_is(7), shared[s, 3, k : k + 1], v)
-                    adjoint[s, t, 3 + c] = lam[t, 3 + c]
-
-    @pl.when(jnp.logical_not(here))
-    def _():
-        adjoint[...] = swapped[...]
+                    v = jnp.where(row_is(0), part[2, k : k + 1], lam[t, c])
+                    buffer[s, t, c] = jnp.where(row_is(7), part[3, k : k + 1], v)
+                    buffer[s, t, 3 + c] = lam[t, 3 + c]
+            pltpu.make_async_copy(buffer.at[s], adjoint.at[s], sems.at[s]).start()
+
+    for own in range(sections):
+
+        @pl.when(meta[0, META_S] == own)
+        def _(own=own):
+            for k in range(2):
+                value = shared[own % sections][k]
+                for s in range(1, sections):
+                    value = value + shared[(own - s) % sections][k]
+                total[k] = value
+
+    last = pltpu.make_async_copy(total, grad, sems.at[sections])
+    last.start()
+    for s in range(sections):
+        pltpu.make_async_copy(buffer.at[s], adjoint.at[s], sems.at[s]).wait()
+    last.wait()
 
 
 STATE = jax.ShapeDtypeStruct((2, 6, ROWS, COLS), F32)
 HALO = jax.ShapeDtypeStruct((8, COLS), F32)
+CHUNKS = jax.ShapeDtypeStruct((4, 2, 6, ROWS, COLS), F32)
 GRADS = jax.ShapeDtypeStruct((2, ROWS, COLS), F32)
 TILES = pltpu.VMEM((EXT * NB * 8, 128), F32)
 SMALL = pltpu.VMEM((NB * 8, 128), F32)
 
 
-def call(body, outs, operands, scratch=(), flops=0, placed=True):
+def call(body, outs, operands, scratch=(), flops=0, hbm_out=()):
     spaces = [pltpu.VMEM if k else pltpu.SMEM for k in range(len(operands))]
-    if placed:
-        operands = [pltpu.with_memory_space_constraint(x, space) for x, space in zip(operands, spaces)]
-        outs = [pltpu.VMEM(o.shape, o.dtype) for o in outs]
+    operands = [pltpu.with_memory_space_constraint(x, space) for x, space in zip(operands, spaces)]
+    out_spaces = [pltpu.HBM if k in hbm_out else pltpu.VMEM for k in range(len(outs))]
     return pl.pallas_call(
         body,
-        out_shape=outs,
+        out_shape=[space(o.shape, o.dtype) for space, o in zip(out_spaces, outs)],
         in_specs=[pl.BlockSpec(memory_space=space) for space in spaces],
-        out_specs=[pl.BlockSpec(memory_space=pltpu.VMEM)] * len(outs),
+        out_specs=[pl.BlockSpec(memory_space=space) for space in out_spaces],
         scratch_shapes=list(scratch),
         cost_estimate=pl.CostEstimate(flops=flops, transcendentals=0, bytes_accessed=1 << 18) if flops else None,
     )(*operands)
@@ -500,10 +521,14 @@
     lam = lax.dynamic_slice_in_dim(cotangent, section * 2, 2, 0)
     send_x, send_p, kk = call(start_kernel, [HALO, HALO, GRADS], [own_list, state, stiffness])
 
+    def exchange(send_x, send_p):
+        got_x = lax.ppermute(send_x, "space", cross)
+        got_p = lax.ppermute(send_p, "space", near)
+        return got_x, got_p
+
     states, halos, exits = [], [], []
     for step in range(steps):
-        halo_x = lax.ppermute(send_x, "space", cross)
-        halo_p = lax.ppermute(send_p, "space", near)
+        halo_x, halo_p = exchange(send_x, send_p)
         (force,) = call(
             functools.partial(forward_inner, step),
             [jax.ShapeDtypeStruct((6, ROWS, COLS), F32)],
@@ -522,36 +547,43 @@
 
     grad = None
     got = ()
-    fulls = {}
+    fulls = []
     for step in reversed(range(steps)):
         opening = step == steps - 1
         keep = step % 2 == 1 and not opening
-        outs = [STATE, HALO, HALO, HALO] + ([STATE] if keep else [])
         lam, send_x, send_p, kd, *rest = call(
             functools.partial(backward_outer, step, opening, keep),
-            outs,
+            [STATE, HALO, HALO, HALO] + [STATE] * keep,
             [meta, lam, *got, states[step], *halos[step], kk],
-            [TILES, TILES, TILES, pltpu.VMEM((2 * NB * 8, 128), F32)],
+            [TILES, TILES, pltpu.VMEM((2 * NB * 8, 128), F32)],
         )
-        if keep:
-            fulls[(step + 1) // 2] = rest[0]
-        got = (lax.ppermute(send_x, "space", cross), lax.ppermute(send_p, "space", near))
-        lam, grad = call(
+        fulls = rest + fulls
+        got = exchange(send_x, send_p)
+        copying = step == COPY_STEP
+        operands = [meta, lam, states[step], *halos[step], kk, kd] + ([] if opening else [grad])
+        lam, grad, *rest = call(
             functools.partial(backward_inner, step, opening),
-            [STATE, GRADS],
-            [meta, lam, states[step], kk, kd] + ([] if opening else [grad]),
-            [TILES, TILES, TILES],
+            [STATE, GRADS] + [CHUNKS] * copying,
+            operands + [exit_state] * copying,
+            [TILES, TILES, TILES] + [pltpu.SemaphoreType.DMA((4,))] * copying,
             flops=8000000,
+            hbm_out=(2,),
         )
+        if copying:
+            (exit_state,) = rest
         if step == 1:
-            swapped = lax.all_to_all(jnp.stack([fulls[max(s, 1)] for s in range(sections)]), "section", 0, 0, tiled=True)
+            swapped = lax.all_to_all(jnp.stack([fulls[0], *fulls]), "section", 0, 0, tiled=True)
     lams = [lam]
     for s in range(1, sections):
         lams.append(lax.ppermute(lam, "section", [(s, 0)]))
-    (shared,) = call(end_kernel, [jax.ShapeDtypeStruct((sections, 4, ROWS, COLS), F32)], [meta, lam, *got, grad])
-    shared = lax.all_to_all(shared, "section", 0, 0, tiled=True)
+    (shared,) = call(end_kernel, [jax.ShapeDtypeStruct((4, ROWS, COLS), F32)], [meta, lam, *got, grad])
+    parts = [shared] + [lax.ppermute(shared, "section", [(i, (i + k) % sections) for i in range(sections)]) for k in range(1, sections)]
     adjoint, stiffness_grad = call(
-        output_kernel, [jax.ShapeDtypeStruct((sections, 2, 6, ROWS, COLS), F32), GRADS], [meta, swapped, shared, *lams], placed=False
+        functools.partial(output_kernel, sections),
+        [CHUNKS, GRADS],
+        [meta, swapped, *parts, *lams],
+        [pltpu.VMEM((4, 2, 6, ROWS, COLS), F32), pltpu.VMEM((2, ROWS, COLS), F32), pltpu.SemaphoreType.DMA((5,))],
+        hbm_out=(0, 1),
     )
     return (
         exit_state.reshape(1, 8, 6, ROWS, COLS),

time: 220 us -> 197 us (0.90)
  waiting for transfers between devices: 41.5 us -> 16.4 us
  starting transfers between devices: 114 us -> 117 us
    ppermute x3, waiting for transfers between devices: 15.9 us -> 0.01 us  [on_device(): lams.append(lax.ppermute(lam, 'section', [(s, 0)]))]
    all_to_all x1, waiting for transfers between devices: 11.6 us -> 0.01 us  [on_device(): exit_state = lax.all_to_all(jnp.stack(exits), 'section', 0, 0, tiled=True)]
    ppermute x32 -> x35, waiting for transfers between devices: 9.84 us -> 16.3 us  [the longest x16 11.5 us: exchange(): got_x = lax.ppermute(send_x, 'space', cross)]
    ppermute x32 -> x35, starting transfers between devices: 94.5 us -> 99.2 us  [the longest x16 60.9 us: exchange(): got_p = lax.ppermute(send_p, 'space', near)]
    all_to_all x2 -> x1, waiting for transfers between devices: 4.13 us -> 0.01 us  [on_device(): lax.all_to_all(jnp.stack([fulls[0], *fulls]), 'section', 0, 0, tiled=True)]
    unnamed x51 -> x22, local copies, waits for them, and re-layouts: 6.83 us -> 4.35 us
    all_to_all x2 -> x1, starting transfers between devices: 7.03 us -> 4.87 us  [on_device(): lax.all_to_all(jnp.stack([fulls[0], *fulls]), 'section', 0, 0, tiled=True)]
  transfers between devices with their start and end apart: 41 -> 43, of which waited for: 10 -> 11; matrix products, arithmetic and copies ran while one was open for 2% -> 1% of each run, Pallas kernels for 15% -> 20%
where the time goes in v2:
time: 197 us; the launch traced here: 194 us
  starting transfers between devices  117 us (59%)
  Pallas kernels  49.5 us (25%)
  waiting for transfers between devices  16.4 us (8%)
  local copies, waits for them, and re-layouts  6.05 us (3%)
  other arithmetic  3.32 us (2%)
    ppermute x16, starting transfers between devices, exchange(): got_p = lax.ppermute(send_p, 'space', near)  60.9 us
    pallas_call x35, Pallas kernels, call(): pl.pallas_call(body, out_shape=[space(o.shape, o.dtype) for space, o in z...  49.5 us
    ppermute x16, starting transfers between devices, exchange(): got_x = lax.ppermute(send_x, 'space', cross)  31.4 us
    ppermute x16, waiting for transfers between devices, exchange(): got_x = lax.ppermute(send_x, 'space', cross)  11.5 us
    ppermute x3, starting transfers between devices, on_device(): lax.ppermute(shared, 'section', [(i, (i + k) % sections) for i in range(s...  6.96 us
    all_to_all x1, starting transfers between devices, on_device(): lax.all_to_all(jnp.stack([fulls[0], *fulls]), 'section', 0, 0, tiled=True)  4.87 us
    ppermute x3, starting transfers between devices, on_device(): lax.ppermute(own_list, 'section', [(i, (i + k) % sections) for i in range...  4.61 us
    unnamed x22, local copies, waits for them, and re-layouts  4.35 us
  transfers between devices with their start and end apart: 43, of which 11 were waited for; matrix products, arithmetic and copies ran while one was open for 1% of the time, Pallas kernels for 20%

profile of v2, /device:TPU:102, one launch (start us, length us, event | category | flops | bytes accessed | tf_op | source)
XLA Modules:
  0.0 193.5 jit_solution(4961792905766782237)
XLA Ops:
  2.9 3.0 %collective-permute-start.2 = (s32[1,64]{1,0:T(1,128)}, s32[1,64]{1,0:T(1,128)S(1)}, u32[]{:S(2)}, u32[]{:S(2)}) collective-permute-start(s32[1,64]{1,0:T(1,128)} %reshape.15.meta), channel_id=1, source_target_pairs={{0,192},{64,0},{128,64},{192,128},{1,193},{65,1},{129,65},{193,129... | collective-permute-start | bytes 776 | tf_op jit(solution)/shard_map/ppermute | solution.py:517
  10.9 3.2 %collective-permute-start.4 = (f32[8,512]{1,0:T(8,128)S(1)}, f32[8,512]{1,0:T(8,128)S(1)}, u32[]{:S(2)}, u32[]{:S(2)}) collective-permute-start(f32[8,512]{1,0:T(8,128)S(1)} %get-tuple-element.84), channel_id=1, source_target_pairs={{0,1},{1,0},{2,3},{3,2},{4,5},{5,4},{6,7},{7,6},{8,9},{9,8},{10,11... | collective-permute-start | bytes 49160 | tf_op jit(solution)/shard_map/ppermute | solution.py:526
  23.8 3.9 %collective-permute-start.8 = (f32[8,512]{1,0:T(8,128)S(1)}, f32[8,512]{1,0:T(8,128)S(1)}, u32[]{:S(2)}, u32[]{:S(2)}) collective-permute-start(f32[8,512]{1,0:T(8,128)S(1)} %get-tuple-element.90), channel_id=1, source_target_pairs={{0,1},{1,0},{2,3},{3,2},{4,5},{5,4},{6,7},{7,6},{8,9},{9,8},{10,11... | collective-permute-start | bytes 49160 | tf_op jit(solution)/shard_map/ppermute | solution.py:526
  34.0 3.4 %collective-permute-start.10 = (f32[8,512]{1,0:T(8,128)S(1)}, f32[8,512]{1,0:T(8,128)S(1)}, u32[]{:S(2)}, u32[]{:S(2)}) collective-permute-start(f32[8,512]{1,0:T(8,128)S(1)} %get-tuple-element.93), channel_id=1, source_target_pairs={{0,1},{1,0},{2,3},{3,2},{4,5},{5,4},{6,7},{7,6},{8,9},{9,8},{10,11... | collective-permute-start | bytes 49160 | tf_op jit(solution)/shard_map/ppermute | solution.py:526
  43.3 3.4 %collective-permute-start.12 = (f32[8,512]{1,0:T(8,128)S(1)}, f32[8,512]{1,0:T(8,128)S(1)}, u32[]{:S(2)}, u32[]{:S(2)}) collective-permute-start(f32[8,512]{1,0:T(8,128)S(1)} %get-tuple-element.96), channel_id=1, source_target_pairs={{0,1},{1,0},{2,3},{3,2},{4,5},{5,4},{6,7},{7,6},{8,9},{9,8},{10,11... | collective-permute-start | bytes 49160 | tf_op jit(solution)/shard_map/ppermute | solution.py:526
  52.6 3.8 %collective-permute-start.14 = (f32[8,512]{1,0:T(8,128)S(1)}, f32[8,512]{1,0:T(8,128)S(1)}, u32[]{:S(2)}, u32[]{:S(2)}) collective-permute-start(f32[8,512]{1,0:T(8,128)S(1)} %get-tuple-element.99), channel_id=1, source_target_pairs={{0,1},{1,0},{2,3},{3,2},{4,5},{5,4},{6,7},{7,6},{8,9},{9,8},{10,11... | collective-permute-start | bytes 49160 | tf_op jit(solution)/shard_map/ppermute | solution.py:526
  62.3 3.4 %collective-permute-start.16 = (f32[8,512]{1,0:T(8,128)S(1)}, f32[8,512]{1,0:T(8,128)S(1)}, u32[]{:S(2)}, u32[]{:S(2)}) collective-permute-start(f32[8,512]{1,0:T(8,128)S(1)} %get-tuple-element.102), channel_id=1, source_target_pairs={{0,1},{1,0},{2,3},{3,2},{4,5},{5,4},{6,7},{7,6},{8,9},{9,8},{10,11... | collective-permute-start | bytes 49160 | tf_op jit(solution)/shard_map/ppermute | solution.py:526
  71.8 4.1 %collective-permute-start.18 = (f32[8,512]{1,0:T(8,128)S(1)}, f32[8,512]{1,0:T(8,128)S(1)}, u32[]{:S(2)}, u32[]{:S(2)}) collective-permute-start(f32[8,512]{1,0:T(8,128)S(1)} %get-tuple-element.105), channel_id=1, source_target_pairs={{0,1},{1,0},{2,3},{3,2},{4,5},{5,4},{6,7},{7,6},{8,9},{9,8},{10,11... | collective-permute-start | bytes 49160 | tf_op jit(solution)/shard_map/ppermute | solution.py:526
  83.4 4.2 %all-to-all-start = ((f32[4,2,6,8,512]{4,3,2,1,0:T(8,128)}), f32[4,2,6,8,512]{4,3,2,1,0:T(8,128)}, u32[]{:S(2)}, u32[]{:S(2)}) async-start(f32[4,2,6,8,512]{4,3,2,1,0:T(8,128)} %pad_maximum_fusion), calls=%async_computation | async-start | bytes 1572864 | tf_op jit(solution)/shard_map/all_to_all | solution.py:546
  90.1 2.5 %collective-permute-start.19 = (f32[8,512]{1,0:T(8,128)S(1)}, f32[8,512]{1,0:T(8,128)S(1)}, u32[]{:S(2)}, u32[]{:S(2)}) collective-permute-start(f32[8,512]{1,0:T(8,128)S(1)} %get-tuple-element.109), channel_id=1, source_target_pairs={{1,2},{3,4},{5,6},{7,8},{9,10},{11,12},{13,14},{15,16},{17,18},{19... | collective-permute-start | bytes 49160 | tf_op jit(solution)/shard_map/ppermute | solution.py:525
  92.6 6.1 %collective-permute-start.20 = (f32[8,512]{1,0:T(8,128)S(1)}, f32[8,512]{1,0:T(8,128)S(1)}, u32[]{:S(2)}, u32[]{:S(2)}) collective-permute-start(f32[8,512]{1,0:T(8,128)S(1)} %get-tuple-element.110), channel_id=1, source_target_pairs={{0,1},{1,0},{2,3},{3,2},{4,5},{5,4},{6,7},{7,6},{8,9},{9,8},{10,11... | collective-permute-start | bytes 49160 | tf_op jit(solution)/shard_map/ppermute | solution.py:526
  104.2 4.3 %collective-permute-start.22 = (f32[8,512]{1,0:T(8,128)S(1)}, f32[8,512]{1,0:T(8,128)S(1)}, u32[]{:S(2)}, u32[]{:S(2)}) collective-permute-start(f32[8,512]{1,0:T(8,128)S(1)} %get-tuple-element.116), channel_id=1, source_target_pairs={{0,1},{1,0},{2,3},{3,2},{4,5},{5,4},{6,7},{7,6},{8,9},{9,8},{10,11... | collective-permute-start | bytes 49160 | tf_op jit(solution)/shard_map/ppermute | solution.py:526
  113.5 4.3 %collective-permute-start.24 = (f32[8,512]{1,0:T(8,128)S(1)}, f32[8,512]{1,0:T(8,128)S(1)}, u32[]{:S(2)}, u32[]{:S(2)}) collective-permute-start(f32[8,512]{1,0:T(8,128)S(1)} %get-tuple-element.122), channel_id=1, source_target_pairs={{0,1},{1,0},{2,3},{3,2},{4,5},{5,4},{6,7},{7,6},{8,9},{9,8},{10,11... | collective-permute-start | bytes 49160 | tf_op jit(solution)/shard_map/ppermute | solution.py:526
  117.8 2.4 %shard_map.105 = (f32[2,6,8,512]{3,2,1,0:T(8,128)S(1)}, f32[2,8,512]{2,1,0:T(8,128)S(1)}) custom-call(s32[4,64]{1,0:T(4,128)} %pad_add_fusion.meta, f32[2,6,8,512]{3,2,1,0:T(8,128)S(1)} %get-tuple-element.117.lam, f32[2,6,8,512]{3,2,1,0:T(8,128)S(1)} %get-tuple-element.97.state.refs_2_, f32[8,512]{1,0:T(8,128)S(1)} %collective-permute-done.13.halo_x.refs_3_, ...), custom_call_target="tpu_custom_call" | custom-call | flops 8000000 | bytes 262144 | tf_op jit(solution)/shard_map/pallas_call | solution.py:487
  123.1 4.0 %collective-permute-start.26 = (f32[8,512]{1,0:T(8,128)S(1)}, f32[8,512]{1,0:T(8,128)S(1)}, u32[]{:S(2)}, u32[]{:S(2)}) collective-permute-start(f32[8,512]{1,0:T(8,128)S(1)} %get-tuple-element.128), channel_id=1, source_target_pairs={{0,1},{1,0},{2,3},{3,2},{4,5},{5,4},{6,7},{7,6},{8,9},{9,8},{10,11... | collective-permute-start | bytes 49160 | tf_op jit(solution)/shard_map/ppermute | solution.py:526
  127.1 3.2 %shard_map.107 = (f32[2,6,8,512]{3,2,1,0:T(8,128)S(1)}, f32[2,8,512]{2,1,0:T(8,128)S(1)}) custom-call(s32[4,64]{1,0:T(4,128)} %pad_add_fusion.meta, f32[2,6,8,512]{3,2,1,0:T(8,128)S(1)} %get-tuple-element.123.lam, f32[2,6,8,512]{3,2,1,0:T(8,128)S(1)} %get-tuple-element.94.state.refs_2_, f32[8,512]{1,0:T(8,128)S(1)} %collective-permute-done.11.halo_x.refs_3_, ...), custom_call_target="tpu_custom_call" | custom-call | flops 8000000 | bytes 262144 | tf_op jit(solution)/shard_map/pallas_call | solution.py:487
  134.2 2.8 %collective-permute-start.28 = (f32[8,512]{1,0:T(8,128)S(1)}, f32[8,512]{1,0:T(8,128)S(1)}, u32[]{:S(2)}, u32[]{:S(2)}) collective-permute-start(f32[8,512]{1,0:T(8,128)S(1)} %get-tuple-element.136), channel_id=1, source_target_pairs={{0,1},{1,0},{2,3},{3,2},{4,5},{5,4},{6,7},{7,6},{8,9},{9,8},{10,11... | collective-permute-start | bytes 49160 | tf_op jit(solution)/shard_map/ppermute | solution.py:526
  142.5 4.4 %collective-permute-start.30 = (f32[8,512]{1,0:T(8,128)S(1)}, f32[8,512]{1,0:T(8,128)S(1)}, u32[]{:S(2)}, u32[]{:S(2)}) collective-permute-start(f32[8,512]{1,0:T(8,128)S(1)} %get-tuple-element.142), channel_id=1, source_target_pairs={{0,1},{1,0},{2,3},{3,2},{4,5},{5,4},{6,7},{7,6},{8,9},{9,8},{10,11... | collective-permute-start | bytes 49160 | tf_op jit(solution)/shard_map/ppermute | solution.py:526
  146.9 2.4 %shard_map.113 = (f32[2,6,8,512]{3,2,1,0:T(8,128)S(1)}, f32[2,8,512]{2,1,0:T(8,128)S(1)}) custom-call(s32[4,64]{1,0:T(4,128)} %pad_add_fusion.meta, f32[2,6,8,512]{3,2,1,0:T(8,128)S(1)} %get-tuple-element.137.lam, f32[2,6,8,512]{3,2,1,0:T(8,128)S(1)} %get-tuple-element.88.state.refs_2_, f32[8,512]{1,0:T(8,128)S(1)} %collective-permute-done.7.halo_x.refs_3_, ...), custom_call_target="tpu_custom_call" | custom-call | flops 8000000 | bytes 262144 | tf_op jit(solution)/shard_map/pallas_call | solution.py:487
  151.4 4.9 %all-to-all-start.1 = ((f32[4,2,6,8,512]{4,3,2,1,0:T(8,128)}), f32[4,2,6,8,512]{4,3,2,1,0:T(8,128)S(1)}, u32[]{:S(2)}, u32[]{:S(2)}) async-start(f32[4,2,6,8,512]{4,3,2,1,0:T(8,128)} %pad_maximum_fusion.1), calls=%async_computation.1 | async-start | bytes 1572864 | tf_op jit(solution)/shard_map/all_to_all | solution.py:575
  158.2 4.6 %collective-permute-start.32 = (f32[8,512]{1,0:T(8,128)S(1)}, f32[8,512]{1,0:T(8,128)S(1)}, u32[]{:S(2)}, u32[]{:S(2)}) collective-permute-start(f32[8,512]{1,0:T(8,128)S(1)} %get-tuple-element.151), channel_id=1, source_target_pairs={{0,1},{1,0},{2,3},{3,2},{4,5},{5,4},{6,7},{7,6},{8,9},{9,8},{10,11... | collective-permute-start | bytes 49160 | tf_op jit(solution)/shard_map/ppermute | solution.py:526
  165.9 2.5 %shard_map.117 = (f32[2,6,8,512]{3,2,1,0:T(8,128)S(1)}, f32[2,8,512]{2,1,0:T(8,128)S(1)}) custom-call(s32[4,64]{1,0:T(4,128)} %pad_add_fusion.meta, f32[2,6,8,512]{3,2,1,0:T(8,128)S(1)} %get-tuple-element.152.lam, f32[2,6,8,512]{3,2,1,0:T(8,128)S(1)} %constant_dynamic-slice_fusion.state.refs_2_, f32[8,512]{1,0:T(8,128)S(1)} %collective-permute-done.3.halo_x.refs_3_, ...), custom_call_target="tpu_custom_call" | custom-call | flops 8000000 | bytes 262144 | tf_op jit(solution)/shard_map/pallas_call | solution.py:487
  174.4 4.8 %collective-permute-start.34 = (f32[8,512]{1,0:T(8,128)S(1)}, f32[8,512]{1,0:T(8,128)S(1)}, u32[]{:S(2)}, u32[]{:S(2)}) collective-permute-start(f32[8,512]{1,0:T(8,128)S(1)} %get-tuple-element.157), channel_id=1, source_target_pairs={{0,1},{1,0},{2,3},{3,2},{4,5},{5,4},{6,7},{7,6},{8,9},{9,8},{10,11... | collective-permute-start | bytes 49160 | tf_op jit(solution)/shard_map/ppermute | solution.py:526
  180.7 2.7 %collective-permute-start.37 = (f32[4,8,512]{2,1,0:T(8,128)S(1)}, f32[4,8,512]{2,1,0:T(8,128)S(1)}, u32[]{:S(2)}, u32[]{:S(2)}) collective-permute-start(f32[4,8,512]{2,1,0:T(8,128)S(1)} %shard_map.118.refs_0_), channel_id=1, source_target_pairs={{0,192},{64,0},{128,64},{192,128},{1,193},{65,1},{129,65},{193,129... | collective-permute-start | bytes 196616 | tf_op jit(solution)/shard_map/ppermute | solution.py:580
  (129 shorter events, 103.5 us)
Async XLA Ops:
  2.9 11.2 %collective-permute-start.2 = (s32[1,64]{1,0:T(1,128)}, s32[1,64]{1,0:T(1,128)S(1)}, u32[]{:S(2)}, u32[]{:S(2)}) collective-permute-start(s32[1,64]{1,0:T(1,128)} %reshape.15.meta), channel_id=1, source_target_pairs={{0,192},{64,0},{128,64},{192,128},{1,193},{65,1},{129,65},{193,129... | collective-permute-start | bytes 776 | tf_op jit(solution)/shard_map/ppermute | solution.py:517
  5.9 8.2 %collective-permute-start.1 = (s32[1,64]{1,0:T(1,128)}, s32[1,64]{1,0:T(1,128)S(1)}, u32[]{:S(2)}, u32[]{:S(2)}) collective-permute-start(s32[1,64]{1,0:T(1,128)} %reshape.15.meta), channel_id=1, source_target_pairs={{0,128},{64,192},{128,0},{192,64},{1,129},{65,193},{129,1},{193,65... | collective-permute-start | bytes 776 | tf_op jit(solution)/shard_map/ppermute | solution.py:517
  6.5 7.6 %collective-permute-start = (s32[1,64]{1,0:T(1,128)}, s32[1,64]{1,0:T(1,128)S(1)}, u32[]{:S(2)}, u32[]{:S(2)}) collective-permute-start(s32[1,64]{1,0:T(1,128)} %reshape.15.meta), channel_id=1, source_target_pairs={{0,64},{64,128},{128,192},{192,0},{1,65},{65,129},{129,193},{193,1... | collective-permute-start | bytes 776 | tf_op jit(solution)/shard_map/ppermute | solution.py:517
  8.9 8.0 %collective-permute-start.3 = (f32[8,512]{1,0:T(8,128)S(1)}, f32[8,512]{1,0:T(8,128)S(1)}, u32[]{:S(2)}, u32[]{:S(2)}) collective-permute-start(f32[8,512]{1,0:T(8,128)S(1)} %get-tuple-element.82), channel_id=1, source_target_pairs={{1,2},{3,4},{5,6},{7,8},{9,10},{11,12},{13,14},{15,16},{17,18},{19... | collective-permute-start | bytes 49160 | tf_op jit(solution)/shard_map/ppermute | solution.py:525
  71.8 6.1 %collective-permute-start.18 = (f32[8,512]{1,0:T(8,128)S(1)}, f32[8,512]{1,0:T(8,128)S(1)}, u32[]{:S(2)}, u32[]{:S(2)}) collective-permute-start(f32[8,512]{1,0:T(8,128)S(1)} %get-tuple-element.105), channel_id=1, source_target_pairs={{0,1},{1,0},{2,3},{3,2},{4,5},{5,4},{6,7},{7,6},{8,9},{9,8},{10,11... | collective-permute-start | bytes 49160 | tf_op jit(solution)/shard_map/ppermute | solution.py:526
  83.4 53.6 %all-to-all-start = ((f32[4,2,6,8,512]{4,3,2,1,0:T(8,128)}), f32[4,2,6,8,512]{4,3,2,1,0:T(8,128)}, u32[]{:S(2)}, u32[]{:S(2)}) async-start(f32[4,2,6,8,512]{4,3,2,1,0:T(8,128)} %pad_maximum_fusion), calls=%async_computation | async-start | bytes 1572864 | tf_op jit(solution)/shard_map/all_to_all | solution.py:546
  90.1 11.3 %collective-permute-start.19 = (f32[8,512]{1,0:T(8,128)S(1)}, f32[8,512]{1,0:T(8,128)S(1)}, u32[]{:S(2)}, u32[]{:S(2)}) collective-permute-start(f32[8,512]{1,0:T(8,128)S(1)} %get-tuple-element.109), channel_id=1, source_target_pairs={{1,2},{3,4},{5,6},{7,8},{9,10},{11,12},{13,14},{15,16},{17,18},{19... | collective-permute-start | bytes 49160 | tf_op jit(solution)/shard_map/ppermute | solution.py:525
  92.6 8.8 %collective-permute-start.20 = (f32[8,512]{1,0:T(8,128)S(1)}, f32[8,512]{1,0:T(8,128)S(1)}, u32[]{:S(2)}, u32[]{:S(2)}) collective-permute-start(f32[8,512]{1,0:T(8,128)S(1)} %get-tuple-element.110), channel_id=1, source_target_pairs={{0,1},{1,0},{2,3},{3,2},{4,5},{5,4},{6,7},{7,6},{8,9},{9,8},{10,11... | collective-permute-start | bytes 49160 | tf_op jit(solution)/shard_map/ppermute | solution.py:526
  102.3 7.9 %collective-permute-start.21 = (f32[8,512]{1,0:T(8,128)S(1)}, f32[8,512]{1,0:T(8,128)S(1)}, u32[]{:S(2)}, u32[]{:S(2)}) collective-permute-start(f32[8,512]{1,0:T(8,128)S(1)} %get-tuple-element.115), channel_id=1, source_target_pairs={{1,2},{3,4},{5,6},{7,8},{9,10},{11,12},{13,14},{15,16},{17,18},{19... | collective-permute-start | bytes 49160 | tf_op jit(solution)/shard_map/ppermute | solution.py:525
  111.6 8.7 %collective-permute-start.23 = (f32[8,512]{1,0:T(8,128)S(1)}, f32[8,512]{1,0:T(8,128)S(1)}, u32[]{:S(2)}, u32[]{:S(2)}) collective-permute-start(f32[8,512]{1,0:T(8,128)S(1)} %get-tuple-element.121), channel_id=1, source_target_pairs={{1,2},{3,4},{5,6},{7,8},{9,10},{11,12},{13,14},{15,16},{17,18},{19... | collective-permute-start | bytes 49160 | tf_op jit(solution)/shard_map/ppermute | solution.py:525
  113.5 6.8 %collective-permute-start.24 = (f32[8,512]{1,0:T(8,128)S(1)}, f32[8,512]{1,0:T(8,128)S(1)}, u32[]{:S(2)}, u32[]{:S(2)}) collective-permute-start(f32[8,512]{1,0:T(8,128)S(1)} %get-tuple-element.122), channel_id=1, source_target_pairs={{0,1},{1,0},{2,3},{3,2},{4,5},{5,4},{6,7},{7,6},{8,9},{9,8},{10,11... | collective-permute-start | bytes 49160 | tf_op jit(solution)/shard_map/ppermute | solution.py:526
  121.2 9.1 %collective-permute-start.25 = (f32[8,512]{1,0:T(8,128)S(1)}, f32[8,512]{1,0:T(8,128)S(1)}, u32[]{:S(2)}, u32[]{:S(2)}) collective-permute-start(f32[8,512]{1,0:T(8,128)S(1)} %get-tuple-element.127), channel_id=1, source_target_pairs={{1,2},{3,4},{5,6},{7,8},{9,10},{11,12},{13,14},{15,16},{17,18},{19... | collective-permute-start | bytes 49160 | tf_op jit(solution)/shard_map/ppermute | solution.py:525
  123.1 7.2 %collective-permute-start.26 = (f32[8,512]{1,0:T(8,128)S(1)}, f32[8,512]{1,0:T(8,128)S(1)}, u32[]{:S(2)}, u32[]{:S(2)}) collective-permute-start(f32[8,512]{1,0:T(8,128)S(1)} %get-tuple-element.128), channel_id=1, source_target_pairs={{0,1},{1,0},{2,3},{3,2},{4,5},{5,4},{6,7},{7,6},{8,9},{9,8},{10,11... | collective-permute-start | bytes 49160 | tf_op jit(solution)/shard_map/ppermute | solution.py:526
  132.2 7.0 %collective-permute-start.27 = (f32[8,512]{1,0:T(8,128)S(1)}, f32[8,512]{1,0:T(8,128)S(1)}, u32[]{:S(2)}, u32[]{:S(2)}) collective-permute-start(f32[8,512]{1,0:T(8,128)S(1)} %get-tuple-element.135), channel_id=1, source_target_pairs={{1,2},{3,4},{5,6},{7,8},{9,10},{11,12},{13,14},{15,16},{17,18},{19... | collective-permute-start | bytes 49160 | tf_op jit(solution)/shard_map/ppermute | solution.py:525
  140.6 8.8 %collective-permute-start.29 = (f32[8,512]{1,0:T(8,128)S(1)}, f32[8,512]{1,0:T(8,128)S(1)}, u32[]{:S(2)}, u32[]{:S(2)}) collective-permute-start(f32[8,512]{1,0:T(8,128)S(1)} %get-tuple-element.141), channel_id=1, source_target_pairs={{1,2},{3,4},{5,6},{7,8},{9,10},{11,12},{13,14},{15,16},{17,18},{19... | collective-permute-start | bytes 49160 | tf_op jit(solution)/shard_map/ppermute | solution.py:525
  142.5 6.9 %collective-permute-start.30 = (f32[8,512]{1,0:T(8,128)S(1)}, f32[8,512]{1,0:T(8,128)S(1)}, u32[]{:S(2)}, u32[]{:S(2)}) collective-permute-start(f32[8,512]{1,0:T(8,128)S(1)} %get-tuple-element.142), channel_id=1, source_target_pairs={{0,1},{1,0},{2,3},{3,2},{4,5},{5,4},{6,7},{7,6},{8,9},{9,8},{10,11... | collective-permute-start | bytes 49160 | tf_op jit(solution)/shard_map/ppermute | solution.py:526
  151.4 40.3 %all-to-all-start.1 = ((f32[4,2,6,8,512]{4,3,2,1,0:T(8,128)}), f32[4,2,6,8,512]{4,3,2,1,0:T(8,128)S(1)}, u32[]{:S(2)}, u32[]{:S(2)}) async-start(f32[4,2,6,8,512]{4,3,2,1,0:T(8,128)} %pad_maximum_fusion.1), calls=%async_computation.1 | async-start | bytes 1572864 | tf_op jit(solution)/shard_map/all_to_all | solution.py:575
  156.3 8.2 %collective-permute-start.31 = (f32[8,512]{1,0:T(8,128)S(1)}, f32[8,512]{1,0:T(8,128)S(1)}, u32[]{:S(2)}, u32[]{:S(2)}) collective-permute-start(f32[8,512]{1,0:T(8,128)S(1)} %get-tuple-element.150), channel_id=1, source_target_pairs={{1,2},{3,4},{5,6},{7,8},{9,10},{11,12},{13,14},{15,16},{17,18},{19... | collective-permute-start | bytes 49160 | tf_op jit(solution)/shard_map/ppermute | solution.py:525
  158.2 6.3 %collective-permute-start.32 = (f32[8,512]{1,0:T(8,128)S(1)}, f32[8,512]{1,0:T(8,128)S(1)}, u32[]{:S(2)}, u32[]{:S(2)}) collective-permute-start(f32[8,512]{1,0:T(8,128)S(1)} %get-tuple-element.151), channel_id=1, source_target_pairs={{0,1},{1,0},{2,3},{3,2},{4,5},{5,4},{6,7},{7,6},{8,9},{9,8},{10,11... | collective-permute-start | bytes 49160 | tf_op jit(solution)/shard_map/ppermute | solution.py:526
  168.3 23.4 %collective-permute-start.40 = (f32[2,6,8,512]{3,2,1,0:T(8,128)S(1)}, f32[2,6,8,512]{3,2,1,0:T(8,128)S(1)}, u32[]{:S(2)}, u32[]{:S(2)}) collective-permute-start(f32[2,6,8,512]{3,2,1,0:T(8,128)S(1)} %get-tuple-element.155.lam.refs_4_), channel_id=1, source_target_pairs={{192,0},{193,1},{194,2},{195,3},{196,4},{197,5},{198,6},{199,7},{2... | collective-permute-start | bytes 589832 | tf_op jit(solution)/shard_map/ppermute | solution.py:578
  169.6 22.1 %collective-permute-start.39 = (f32[2,6,8,512]{3,2,1,0:T(8,128)S(1)}, f32[2,6,8,512]{3,2,1,0:T(8,128)S(1)}, u32[]{:S(2)}, u32[]{:S(2)}) collective-permute-start(f32[2,6,8,512]{3,2,1,0:T(8,128)S(1)} %get-tuple-element.155.lam.refs_4_), channel_id=1, source_target_pairs={{128,0},{129,1},{130,2},{131,3},{132,4},{133,5},{134,6},{135,7},{1... | collective-permute-start | bytes 589832 | tf_op jit(solution)/shard_map/ppermute | solution.py:578
  170.9 20.8 %collective-permute-start.38 = (f32[2,6,8,512]{3,2,1,0:T(8,128)S(1)}, f32[2,6,8,512]{3,2,1,0:T(8,128)S(1)}, u32[]{:S(2)}, u32[]{:S(2)}) collective-permute-start(f32[2,6,8,512]{3,2,1,0:T(8,128)S(1)} %get-tuple-element.155.lam.refs_4_), channel_id=1, source_target_pairs={{64,0},{65,1},{66,2},{67,3},{68,4},{69,5},{70,6},{71,7},{72,8},{73... | collective-permute-start | bytes 589832 | tf_op jit(solution)/shard_map/ppermute | solution.py:578
  172.2 6.9 %collective-permute-start.33 = (f32[8,512]{1,0:T(8,128)S(1)}, f32[8,512]{1,0:T(8,128)S(1)}, u32[]{:S(2)}, u32[]{:S(2)}) collective-permute-start(f32[8,512]{1,0:T(8,128)S(1)} %get-tuple-element.156), channel_id=1, source_target_pairs={{1,2},{3,4},{5,6},{7,8},{9,10},{11,12},{13,14},{15,16},{17,18},{19... | collective-permute-start | bytes 49160 | tf_op jit(solution)/shard_map/ppermute | solution.py:525
  183.4 6.2 %collective-permute-start.36 = (f32[4,8,512]{2,1,0:T(8,128)S(1)}, f32[4,8,512]{2,1,0:T(8,128)S(1)}, u32[]{:S(2)}, u32[]{:S(2)}) collective-permute-start(f32[4,8,512]{2,1,0:T(8,128)S(1)} %shard_map.118.refs_0_), channel_id=1, source_target_pairs={{0,128},{64,192},{128,0},{192,64},{1,129},{65,193},{129,1},{193,65... | collective-permute-start | bytes 196616 | tf_op jit(solution)/shard_map/ppermute | solution.py:580
  (30 other events, 253.2 us)

commit v3 on v2

--- a/solution.py
+++ b/solution.py
@@ -17,6 +17,7 @@
 BF16 = jnp.bfloat16
 COPY_STEP = 3
 GROUP = 2
+GROUP_BACK = 2
 SLOTS = 8
 ROWS = 8
 COLS = 512
@@ -107,22 +108,47 @@
 
 
 def pair_adjoint(xa, xb, ga, marks, scale_a, scale_b):
-    from_a = differences(xa, xb, marks) if scale_a is not None else None
+    from_a = differences(xa, xb, marks)
     from_b = differences(xb, xa, marks)
     g_sub = spread(jnp.concatenate(pieces(ga), axis=0), marks)
+    zero = jnp.zeros((8, 128), F32)
     rows_a, rows_b = [], []
     for t in range(2):
         g = [ga[3 * t + c : 3 * t + c + 1, :] for c in range(3)]
-        sum_a = [jnp.zeros((8, 128), F32) for _ in range(3)]
-        sum_b = [jnp.zeros((8, 128), F32) for _ in range(3)]
+        weights, products = [], []
+        sum_w = zero
+        sum_a = [zero] * 3
         for j in range(16):
-            if scale_a is not None:
-                sum_a = pair_sum(sum_a, [block(from_a, j, 3 * t + c) for c in range(3)], g)
-            sum_b = pair_sum(sum_b, [block(from_b, j, 3 * t + c) for c in range(3)], [block(g_sub, j, 3 * t + c) for c in range(3)])
-        rows_a += sum_a
-        rows_b += sum_b
-    con_a = scale_a * stacked(rows_a) if scale_a is not None else None
-    return con_a, -scale_b * stacked(rows_b)
+            d = [block(from_a, j, 3 * t + c) for c in range(3)]
+            w = jnp.exp(-0.5 * (d[0] * d[0] + d[1] * d[1] + d[2] * d[2]))
+            u = w * (g[0] * d[0] + g[1] * d[1] + g[2] * d[2])
+            weights.append(w)
+            products.append(u)
+            sum_w = sum_w + w
+            sum_a = [sum_a[c] + u * d[c] for c in range(3)]
+        total = jnp.sum(sum_w, axis=0, keepdims=True)
+        rows_a += [g[c] * total - jnp.sum(sum_a[c], axis=0, keepdims=True) for c in range(3)]
+        w_back = jnp.transpose(jnp.concatenate(weights, axis=0))
+        u_back = jnp.transpose(jnp.concatenate(products, axis=0))
+        sum_b = [zero] * 3
+        for j in range(16):
+            w, u = w_back[8 * j : 8 * j + 8], u_back[8 * j : 8 * j + 8]
+            sum_b = [sum_b[c] + (w * block(g_sub, j, 3 * t + c) + u * block(from_b, j, 3 * t + c)) for c in range(3)]
+        rows_b += [jnp.sum(v, axis=0, keepdims=True) for v in sum_b]
+    rest = [jnp.zeros((2, 128), F32)]
+    return scale_a * jnp.concatenate(rows_a + rest, axis=0), -scale_b * jnp.concatenate(rows_b + rest, axis=0)
+
+
+def pair_adjoint_far(xa, xb, ga, marks):
+    from_b = differences(xb, xa, marks)
+    g_sub = spread(jnp.concatenate(pieces(ga), axis=0), marks)
+    rows = []
+    for t in range(2):
+        total = [jnp.zeros((8, 128), F32) for _ in range(3)]
+        for j in range(16):
+            total = pair_sum(total, [block(from_b, j, 3 * t + c) for c in range(3)], [block(g_sub, j, 3 * t + c) for c in range(3)])
+        rows += total
+    return -SCALE * stacked(rows)
 
 
 def pair_sum(total, d, g):
@@ -343,7 +369,7 @@
             def _():
                 at = tile_start(a // NB + 1, lax.rem(a, NB))
                 bt = tile_start(b // NB, lax.rem(b, NB))
-                _, con_b = pair_adjoint(tiles[pl.ds(at, 8), :], tiles[pl.ds(bt, 8), :], grads[pl.ds(at, 8), :], marks, None, SCALE)
+                con_b = pair_adjoint_far(tiles[pl.ds(at, 8), :], tiles[pl.ds(bt, 8), :], grads[pl.ds(at, 8), :], marks)
                 out = pl.multiple_of(8 * jnp.where(b < NB, b, b - NB * (EXT - 2)), 8)
                 acc_b[pl.ds(out, 8), :] += con_b
 
@@ -359,12 +385,11 @@
 def backward_inner(step, opening, meta, lam, state, halo_x, halo_p, kk, kd, *refs):
     refs = list(refs)
     old = None if opening else refs.pop(0)
-    copies = []
     if step == COPY_STEP:
-        source, target, sems = refs.pop(0), refs.pop(2), refs.pop()
-        copies = [pltpu.make_async_copy(source.at[s], target.at[s], sems.at[s]) for s in range(4)]
-        for copy in copies:
-            copy.start()
+        source, target, sems, buffer = refs.pop(0), refs.pop(2), refs.pop(), refs.pop()
+        fetch = pltpu.make_async_copy(source, buffer, sems.at[0])
+        store = pltpu.make_async_copy(buffer, target, sems.at[1])
+        fetch.start()
     lam_out, grad, tiles, grads, acc = refs
     row, base = lists(meta, step)
     last = meta[0, META_Q] == 63
@@ -378,11 +403,12 @@
 
     def group(i, carry):
         results = []
-        for q in range(GROUP):
-            p = i * GROUP + q
+        for q in range(GROUP_BACK):
+            n = i * GROUP_BACK + q
+            p = jnp.minimum(n, SLOTS - 1)
             a = meta[row, base + p]
             b = meta[row, base + SLOTS + p]
-            live = p < count
+            live = n < count
             inside = jnp.logical_and(live, jnp.logical_and(b >= NB, b < NB * (EXT - 1)))
             at = tile_start(a // NB + 1, lax.rem(a, NB))
             bt = tile_start(b // NB, lax.rem(b, NB))
@@ -393,7 +419,10 @@
             acc[pl.ds(bt, 8), :] += con_b
         return carry
 
-    lax.fori_loop(0, (count + GROUP - 1) // GROUP, group, 0)
+    lax.fori_loop(0, (count + GROUP_BACK - 1) // GROUP_BACK, group, 0)
+    if step == COPY_STEP:
+        fetch.wait()
+        store.start()
     kh, kc = kk[0], kk[1]
     k_up = jnp.where(row_is(0), 0.0, pltpu.roll(kc, 1, 0))
     grad_h = jnp.zeros((ROWS, COLS), F32)
@@ -418,8 +447,8 @@
     else:
         grad[0] = old[0] + grad_h
         grad[1] = old[1] + grad_v
-    for copy in copies:
-        copy.wait()
+    if step == COPY_STEP:
+        store.wait()
 
 
 def end_kernel(meta, lam, got_x, got_p, old, out):
@@ -480,8 +509,8 @@
 SMALL = pltpu.VMEM((NB * 8, 128), F32)
 
 
-def call(body, outs, operands, scratch=(), flops=0, hbm_out=()):
-    spaces = [pltpu.VMEM if k else pltpu.SMEM for k in range(len(operands))]
+def call(body, outs, operands, scratch=(), flops=0, hbm=(), hbm_out=()):
+    spaces = [pltpu.HBM if k in hbm else pltpu.VMEM if k else pltpu.SMEM for k in range(len(operands))]
     operands = [pltpu.with_memory_space_constraint(x, space) for x, space in zip(operands, spaces)]
     out_spaces = [pltpu.HBM if k in hbm_out else pltpu.VMEM for k in range(len(outs))]
     return pl.pallas_call(
@@ -504,22 +533,18 @@
     near = [(i, i ^ 1) for i in range(spaces)]
     steps = contact_a.shape[0] * sections
 
-    facts = jnp.stack([section, lax.rem(space, 2), space]).astype(jnp.int32)
-    own_list = jnp.concatenate(
-        [
-            contact_a[:, 0],
-            contact_b[:, 0],
-            jnp.broadcast_to(pair_count, (2, 8)),
-            jnp.broadcast_to(jnp.pad(facts, (0, 5)), (2, 8)),
-        ],
-        axis=1,
+    facts = jnp.pad(jnp.stack([section, lax.rem(space, 2), space]).astype(jnp.int32), (META_S, 64 - META_S - 3))[None]
+    own_list = facts + jnp.pad(
+        jnp.concatenate([contact_a[:, 0], contact_b[:, 0], pair_count], axis=1), ((0, 0), (0, 31 - 2 * SLOTS))
     ).reshape(1, 64)
-    others = [lax.ppermute(own_list, "section", [(i, (i + k) % sections) for i in range(sections)]) for k in range(1, sections)]
+    others = []
+    for k in range(1, sections):
+        others.append(lax.ppermute(own_list, "section", [(i, (i + k) % sections) for i in range(sections)]))
     meta = jnp.concatenate([own_list] + others, axis=0)
 
     state = lax.dynamic_slice_in_dim(start_state, section * 2, 2, 0)
     lam = lax.dynamic_slice_in_dim(cotangent, section * 2, 2, 0)
-    send_x, send_p, kk = call(start_kernel, [HALO, HALO, GRADS], [own_list, state, stiffness])
+    send_x, send_p, kk = call(start_kernel, [HALO, HALO, GRADS], [facts, state, stiffness])
 
     def exchange(send_x, send_p):
         got_x = lax.ppermute(send_x, "space", cross)
@@ -565,8 +590,9 @@
             functools.partial(backward_inner, step, opening),
             [STATE, GRADS] + [CHUNKS] * copying,
             operands + [exit_state] * copying,
-            [TILES, TILES, TILES] + [pltpu.SemaphoreType.DMA((4,))] * copying,
+            [TILES, TILES, TILES] + ([pltpu.VMEM(CHUNKS.shape, F32), pltpu.SemaphoreType.DMA((2,))] if copying else []),
             flops=8000000,
+            hbm=(len(operands),),
             hbm_out=(2,),
         )
         if copying:

time: 197 us -> 196 us (level)
    unnamed x22 -> x19, local copies, waits for them, and re-layouts: 4.35 us -> 3.86 us
  transfers between devices with their start and end apart: 43 -> 43, of which waited for: 11 -> 12; matrix products, arithmetic and copies ran while one was open for 1% -> 1% of each run, Pallas kernels for 20% -> 19%
where the time goes in v3:
time: 196 us; the launch traced here: 192 us
  starting transfers between devices  118 us (60%)
  Pallas kernels  48.4 us (25%)
  waiting for transfers between devices  16.5 us (8%)
  local copies, waits for them, and re-layouts  4.91 us (3%)
  other arithmetic  3.28 us (2%)
    ppermute x16, starting transfers between devices, exchange(): got_p = lax.ppermute(send_p, 'space', near)  62 us
    pallas_call x35, Pallas kernels, call(): pl.pallas_call(body, out_shape=[space(o.shape, o.dtype) for space, o in z...  48.4 us
    ppermute x16, starting transfers between devices, exchange(): got_x = lax.ppermute(send_x, 'space', cross)  31.2 us
    ppermute x16, waiting for transfers between devices, exchange(): got_x = lax.ppermute(send_x, 'space', cross)  11.5 us
    ppermute x3, starting transfers between devices, on_device(): lax.ppermute(shared, 'section', [(i, (i + k) % sections) for i in range(s...  7.07 us
    all_to_all x1, starting transfers between devices, on_device(): lax.all_to_all(jnp.stack([fulls[0], *fulls]), 'section', 0, 0, tiled=True)  4.87 us
    ppermute x3, starting transfers between devices, on_device(): lax.ppermute(own_list, 'section', [(i, (i + k) % sections) for i in range...  4.61 us
    all_to_all x1, starting transfers between devices, on_device(): exit_state = lax.all_to_all(jnp.stack(exits), 'section', 0, 0, tiled=True)  4.21 us
  transfers between devices with their start and end apart: 43, of which 12 were waited for; matrix products, arithmetic and copies ran while one was open for 1% of the time, Pallas kernels for 19%

profile of v3, /device:TPU:102, one launch (start us, length us, event | category | flops | bytes accessed | tf_op | source)
XLA Modules:
  0.0 192.4 jit_solution(16756349752411523224)
XLA Ops:
  3.0 3.0 %collective-permute-start.2 = (s32[1,64]{1,0:T(1,128)S(1)}, s32[1,64]{1,0:T(1,128)S(1)}, u32[]{:S(2)}, u32[]{:S(2)}) collective-permute-start(s32[1,64]{1,0:T(1,128)S(1)} %get-tuple-element.162), channel_id=1, source_target_pairs={{0,192},{64,0},{128,64},{192,128},{1,193},{65,1},{129,65},{193,129... | collective-permute-start | bytes 776 | tf_op jit(solution)/shard_map/ppermute | solution.py:542
  11.0 3.2 %collective-permute-start.4 = (f32[8,512]{1,0:T(8,128)S(1)}, f32[8,512]{1,0:T(8,128)S(1)}, u32[]{:S(2)}, u32[]{:S(2)}) collective-permute-start(f32[8,512]{1,0:T(8,128)S(1)} %get-tuple-element.84), channel_id=1, source_target_pairs={{0,1},{1,0},{2,3},{3,2},{4,5},{5,4},{6,7},{7,6},{8,9},{9,8},{10,11... | collective-permute-start | bytes 49160 | tf_op jit(solution)/shard_map/ppermute | solution.py:551
  23.9 3.6 %collective-permute-start.8 = (f32[8,512]{1,0:T(8,128)S(1)}, f32[8,512]{1,0:T(8,128)S(1)}, u32[]{:S(2)}, u32[]{:S(2)}) collective-permute-start(f32[8,512]{1,0:T(8,128)S(1)} %get-tuple-element.90), channel_id=1, source_target_pairs={{0,1},{1,0},{2,3},{3,2},{4,5},{5,4},{6,7},{7,6},{8,9},{9,8},{10,11... | collective-permute-start | bytes 49160 | tf_op jit(solution)/shard_map/ppermute | solution.py:551
  33.7 3.4 %collective-permute-start.10 = (f32[8,512]{1,0:T(8,128)S(1)}, f32[8,512]{1,0:T(8,128)S(1)}, u32[]{:S(2)}, u32[]{:S(2)}) collective-permute-start(f32[8,512]{1,0:T(8,128)S(1)} %get-tuple-element.93), channel_id=1, source_target_pairs={{0,1},{1,0},{2,3},{3,2},{4,5},{5,4},{6,7},{7,6},{8,9},{9,8},{10,11... | collective-permute-start | bytes 49160 | tf_op jit(solution)/shard_map/ppermute | solution.py:551
  43.0 3.4 %collective-permute-start.12 = (f32[8,512]{1,0:T(8,128)S(1)}, f32[8,512]{1,0:T(8,128)S(1)}, u32[]{:S(2)}, u32[]{:S(2)}) collective-permute-start(f32[8,512]{1,0:T(8,128)S(1)} %get-tuple-element.96), channel_id=1, source_target_pairs={{0,1},{1,0},{2,3},{3,2},{4,5},{5,4},{6,7},{7,6},{8,9},{9,8},{10,11... | collective-permute-start | bytes 49160 | tf_op jit(solution)/shard_map/ppermute | solution.py:551
  52.3 3.8 %collective-permute-start.14 = (f32[8,512]{1,0:T(8,128)S(1)}, f32[8,512]{1,0:T(8,128)S(1)}, u32[]{:S(2)}, u32[]{:S(2)}) collective-permute-start(f32[8,512]{1,0:T(8,128)S(1)} %get-tuple-element.99), channel_id=1, source_target_pairs={{0,1},{1,0},{2,3},{3,2},{4,5},{5,4},{6,7},{7,6},{8,9},{9,8},{10,11... | collective-permute-start | bytes 49160 | tf_op jit(solution)/shard_map/ppermute | solution.py:551
  62.0 3.4 %collective-permute-start.16 = (f32[8,512]{1,0:T(8,128)S(1)}, f32[8,512]{1,0:T(8,128)S(1)}, u32[]{:S(2)}, u32[]{:S(2)}) collective-permute-start(f32[8,512]{1,0:T(8,128)S(1)} %get-tuple-element.102), channel_id=1, source_target_pairs={{0,1},{1,0},{2,3},{3,2},{4,5},{5,4},{6,7},{7,6},{8,9},{9,8},{10,11... | collective-permute-start | bytes 49160 | tf_op jit(solution)/shard_map/ppermute | solution.py:551
  71.5 4.1 %collective-permute-start.18 = (f32[8,512]{1,0:T(8,128)S(1)}, f32[8,512]{1,0:T(8,128)S(1)}, u32[]{:S(2)}, u32[]{:S(2)}) collective-permute-start(f32[8,512]{1,0:T(8,128)S(1)} %get-tuple-element.105), channel_id=1, source_target_pairs={{0,1},{1,0},{2,3},{3,2},{4,5},{5,4},{6,7},{7,6},{8,9},{9,8},{10,11... | collective-permute-start | bytes 49160 | tf_op jit(solution)/shard_map/ppermute | solution.py:551
  83.1 4.2 %all-to-all-start = ((f32[4,2,6,8,512]{4,3,2,1,0:T(8,128)}), f32[4,2,6,8,512]{4,3,2,1,0:T(8,128)}, u32[]{:S(2)}, u32[]{:S(2)}) async-start(f32[4,2,6,8,512]{4,3,2,1,0:T(8,128)} %pad_maximum_fusion), calls=%async_computation | async-start | bytes 1572864 | tf_op jit(solution)/shard_map/all_to_all | solution.py:571
  89.8 2.5 %collective-permute-start.19 = (f32[8,512]{1,0:T(8,128)S(1)}, f32[8,512]{1,0:T(8,128)S(1)}, u32[]{:S(2)}, u32[]{:S(2)}) collective-permute-start(f32[8,512]{1,0:T(8,128)S(1)} %get-tuple-element.109), channel_id=1, source_target_pairs={{1,2},{3,4},{5,6},{7,8},{9,10},{11,12},{13,14},{15,16},{17,18},{19... | collective-permute-start | bytes 49160 | tf_op jit(solution)/shard_map/ppermute | solution.py:550
  92.3 6.6 %collective-permute-start.20 = (f32[8,512]{1,0:T(8,128)S(1)}, f32[8,512]{1,0:T(8,128)S(1)}, u32[]{:S(2)}, u32[]{:S(2)}) collective-permute-start(f32[8,512]{1,0:T(8,128)S(1)} %get-tuple-element.110), channel_id=1, source_target_pairs={{0,1},{1,0},{2,3},{3,2},{4,5},{5,4},{6,7},{7,6},{8,9},{9,8},{10,11... | collective-permute-start | bytes 49160 | tf_op jit(solution)/shard_map/ppermute | solution.py:551
  104.2 4.4 %collective-permute-start.22 = (f32[8,512]{1,0:T(8,128)S(1)}, f32[8,512]{1,0:T(8,128)S(1)}, u32[]{:S(2)}, u32[]{:S(2)}) collective-permute-start(f32[8,512]{1,0:T(8,128)S(1)} %get-tuple-element.116), channel_id=1, source_target_pairs={{0,1},{1,0},{2,3},{3,2},{4,5},{5,4},{6,7},{7,6},{8,9},{9,8},{10,11... | collective-permute-start | bytes 49160 | tf_op jit(solution)/shard_map/ppermute | solution.py:551
  113.5 4.4 %collective-permute-start.24 = (f32[8,512]{1,0:T(8,128)S(1)}, f32[8,512]{1,0:T(8,128)S(1)}, u32[]{:S(2)}, u32[]{:S(2)}) collective-permute-start(f32[8,512]{1,0:T(8,128)S(1)} %get-tuple-element.122), channel_id=1, source_target_pairs={{0,1},{1,0},{2,3},{3,2},{4,5},{5,4},{6,7},{7,6},{8,9},{9,8},{10,11... | collective-permute-start | bytes 49160 | tf_op jit(solution)/shard_map/ppermute | solution.py:551
  122.9 4.3 %collective-permute-start.26 = (f32[8,512]{1,0:T(8,128)S(1)}, f32[8,512]{1,0:T(8,128)S(1)}, u32[]{:S(2)}, u32[]{:S(2)}) collective-permute-start(f32[8,512]{1,0:T(8,128)S(1)} %get-tuple-element.128), channel_id=1, source_target_pairs={{0,1},{1,0},{2,3},{3,2},{4,5},{5,4},{6,7},{7,6},{8,9},{9,8},{10,11... | collective-permute-start | bytes 49160 | tf_op jit(solution)/shard_map/ppermute | solution.py:551
  127.2 2.8 %shard_map.107 = (f32[2,6,8,512]{3,2,1,0:T(8,128)S(1)}, f32[2,8,512]{2,1,0:T(8,128)S(1)}) custom-call(s32[4,64]{1,0:T(4,128)} %pad_add_fusion.meta, f32[2,6,8,512]{3,2,1,0:T(8,128)S(1)} %get-tuple-element.123.lam, f32[2,6,8,512]{3,2,1,0:T(8,128)S(1)} %get-tuple-element.94.state.refs_2_, f32[8,512]{1,0:T(8,128)S(1)} %collective-permute-done.11.halo_x.refs_3_, ...), custom_call_target="tpu_custom_call" | custom-call | flops 8000000 | bytes 262144 | tf_op jit(solution)/shard_map/pallas_call | solution.py:516
  133.2 3.3 %collective-permute-start.28 = (f32[8,512]{1,0:T(8,128)S(1)}, f32[8,512]{1,0:T(8,128)S(1)}, u32[]{:S(2)}, u32[]{:S(2)}) collective-permute-start(f32[8,512]{1,0:T(8,128)S(1)} %get-tuple-element.136), channel_id=1, source_target_pairs={{0,1},{1,0},{2,3},{3,2},{4,5},{5,4},{6,7},{7,6},{8,9},{9,8},{10,11... | collective-permute-start | bytes 49160 | tf_op jit(solution)/shard_map/ppermute | solution.py:551
  136.5 2.7 %shard_map.111 = (f32[2,6,8,512]{3,2,1,0:T(8,128)S(1)}, f32[2,8,512]{2,1,0:T(8,128)S(1)}, f32[4,2,6,8,512]{4,3,2,1,0:T(8,128)}) custom-call(s32[4,64]{1,0:T(4,128)} %pad_add_fusion.meta, f32[2,6,8,512]{3,2,1,0:T(8,128)S(1)} %get-tuple-element.129.lam, f32[2,6,8,512]{3,2,1,0:T(8,128)S(1)} %get-tuple-element.91.state.refs_2_, ...), custom_call_target="tpu_custom_call" | custom-call | flops 8000000 | bytes 262144 | tf_op jit(solution)/shard_map/pallas_call | solution.py:516
  142.5 3.7 %collective-permute-start.30 = (f32[8,512]{1,0:T(8,128)S(1)}, f32[8,512]{1,0:T(8,128)S(1)}, u32[]{:S(2)}, u32[]{:S(2)}) collective-permute-start(f32[8,512]{1,0:T(8,128)S(1)} %get-tuple-element.142), channel_id=1, source_target_pairs={{0,1},{1,0},{2,3},{3,2},{4,5},{5,4},{6,7},{7,6},{8,9},{9,8},{10,11... | collective-permute-start | bytes 49160 | tf_op jit(solution)/shard_map/ppermute | solution.py:551
  146.1 2.4 %shard_map.113 = (f32[2,6,8,512]{3,2,1,0:T(8,128)S(1)}, f32[2,8,512]{2,1,0:T(8,128)S(1)}) custom-call(s32[4,64]{1,0:T(4,128)} %pad_add_fusion.meta, f32[2,6,8,512]{3,2,1,0:T(8,128)S(1)} %get-tuple-element.137.lam, f32[2,6,8,512]{3,2,1,0:T(8,128)S(1)} %get-tuple-element.88.state.refs_2_, f32[8,512]{1,0:T(8,128)S(1)} %collective-permute-done.7.halo_x.refs_3_, ...), custom_call_target="tpu_custom_call" | custom-call | flops 8000000 | bytes 262144 | tf_op jit(solution)/shard_map/pallas_call | solution.py:516
  150.4 4.9 %all-to-all-start.1 = ((f32[4,2,6,8,512]{4,3,2,1,0:T(8,128)}), f32[4,2,6,8,512]{4,3,2,1,0:T(8,128)S(1)}, u32[]{:S(2)}, u32[]{:S(2)}) async-start(f32[4,2,6,8,512]{4,3,2,1,0:T(8,128)} %pad_maximum_fusion.1), calls=%async_computation.1 | async-start | bytes 1572864 | tf_op jit(solution)/shard_map/all_to_all | solution.py:601
  157.2 4.9 %collective-permute-start.32 = (f32[8,512]{1,0:T(8,128)S(1)}, f32[8,512]{1,0:T(8,128)S(1)}, u32[]{:S(2)}, u32[]{:S(2)}) collective-permute-start(f32[8,512]{1,0:T(8,128)S(1)} %get-tuple-element.151), channel_id=1, source_target_pairs={{0,1},{1,0},{2,3},{3,2},{4,5},{5,4},{6,7},{7,6},{8,9},{9,8},{10,11... | collective-permute-start | bytes 49160 | tf_op jit(solution)/shard_map/ppermute | solution.py:551
  173.0 5.0 %collective-permute-start.34 = (f32[8,512]{1,0:T(8,128)S(1)}, f32[8,512]{1,0:T(8,128)S(1)}, u32[]{:S(2)}, u32[]{:S(2)}) collective-permute-start(f32[8,512]{1,0:T(8,128)S(1)} %get-tuple-element.157), channel_id=1, source_target_pairs={{0,1},{1,0},{2,3},{3,2},{4,5},{5,4},{6,7},{7,6},{8,9},{9,8},{10,11... | collective-permute-start | bytes 49160 | tf_op jit(solution)/shard_map/ppermute | solution.py:551
  179.6 2.7 %collective-permute-start.37 = (f32[4,8,512]{2,1,0:T(8,128)S(1)}, f32[4,8,512]{2,1,0:T(8,128)S(1)}, u32[]{:S(2)}, u32[]{:S(2)}) collective-permute-start(f32[4,8,512]{2,1,0:T(8,128)S(1)} %shard_map.118.refs_0_), channel_id=1, source_target_pairs={{0,192},{64,0},{128,64},{192,128},{1,193},{65,1},{129,65},{193,129... | collective-permute-start | bytes 196616 | tf_op jit(solution)/shard_map/ppermute | solution.py:606
  184.6 2.3 %collective-permute-start.35 = (f32[4,8,512]{2,1,0:T(8,128)S(1)}, f32[4,8,512]{2,1,0:T(8,128)S(1)}, u32[]{:S(2)}, u32[]{:S(2)}) collective-permute-start(f32[4,8,512]{2,1,0:T(8,128)S(1)} %shard_map.118.refs_0_), channel_id=1, source_target_pairs={{0,64},{64,128},{128,192},{192,0},{1,65},{65,129},{129,193},{193,1... | collective-permute-start | bytes 196616 | tf_op jit(solution)/shard_map/ppermute | solution.py:606
  (126 shorter events, 101.9 us)
Async XLA Ops:
  3.0 11.2 %collective-permute-start.2 = (s32[1,64]{1,0:T(1,128)S(1)}, s32[1,64]{1,0:T(1,128)S(1)}, u32[]{:S(2)}, u32[]{:S(2)}) collective-permute-start(s32[1,64]{1,0:T(1,128)S(1)} %get-tuple-element.162), channel_id=1, source_target_pairs={{0,192},{64,0},{128,64},{192,128},{1,193},{65,1},{129,65},{193,129... | collective-permute-start | bytes 776 | tf_op jit(solution)/shard_map/ppermute | solution.py:542
  6.0 8.2 %collective-permute-start.1 = (s32[1,64]{1,0:T(1,128)S(1)}, s32[1,64]{1,0:T(1,128)S(1)}, u32[]{:S(2)}, u32[]{:S(2)}) collective-permute-start(s32[1,64]{1,0:T(1,128)S(1)} %get-tuple-element.162), channel_id=1, source_target_pairs={{0,128},{64,192},{128,0},{192,64},{1,129},{65,193},{129,1},{193,65... | collective-permute-start | bytes 776 | tf_op jit(solution)/shard_map/ppermute | solution.py:542
  6.6 7.6 %collective-permute-start = (s32[1,64]{1,0:T(1,128)S(1)}, s32[1,64]{1,0:T(1,128)S(1)}, u32[]{:S(2)}, u32[]{:S(2)}) collective-permute-start(s32[1,64]{1,0:T(1,128)S(1)} %get-tuple-element.162), channel_id=1, source_target_pairs={{0,64},{64,128},{128,192},{192,0},{1,65},{65,129},{129,193},{193,1... | collective-permute-start | bytes 776 | tf_op jit(solution)/shard_map/ppermute | solution.py:542
  9.1 7.6 %collective-permute-start.3 = (f32[8,512]{1,0:T(8,128)S(1)}, f32[8,512]{1,0:T(8,128)S(1)}, u32[]{:S(2)}, u32[]{:S(2)}) collective-permute-start(f32[8,512]{1,0:T(8,128)S(1)} %get-tuple-element.82), channel_id=1, source_target_pairs={{1,2},{3,4},{5,6},{7,8},{9,10},{11,12},{13,14},{15,16},{17,18},{19... | collective-permute-start | bytes 49160 | tf_op jit(solution)/shard_map/ppermute | solution.py:550
  71.5 6.1 %collective-permute-start.18 = (f32[8,512]{1,0:T(8,128)S(1)}, f32[8,512]{1,0:T(8,128)S(1)}, u32[]{:S(2)}, u32[]{:S(2)}) collective-permute-start(f32[8,512]{1,0:T(8,128)S(1)} %get-tuple-element.105), channel_id=1, source_target_pairs={{0,1},{1,0},{2,3},{3,2},{4,5},{5,4},{6,7},{7,6},{8,9},{9,8},{10,11... | collective-permute-start | bytes 49160 | tf_op jit(solution)/shard_map/ppermute | solution.py:551
  83.1 53.4 %all-to-all-start = ((f32[4,2,6,8,512]{4,3,2,1,0:T(8,128)}), f32[4,2,6,8,512]{4,3,2,1,0:T(8,128)}, u32[]{:S(2)}, u32[]{:S(2)}) async-start(f32[4,2,6,8,512]{4,3,2,1,0:T(8,128)} %pad_maximum_fusion), calls=%async_computation | async-start | bytes 1572864 | tf_op jit(solution)/shard_map/all_to_all | solution.py:571
  89.8 11.6 %collective-permute-start.19 = (f32[8,512]{1,0:T(8,128)S(1)}, f32[8,512]{1,0:T(8,128)S(1)}, u32[]{:S(2)}, u32[]{:S(2)}) collective-permute-start(f32[8,512]{1,0:T(8,128)S(1)} %get-tuple-element.109), channel_id=1, source_target_pairs={{1,2},{3,4},{5,6},{7,8},{9,10},{11,12},{13,14},{15,16},{17,18},{19... | collective-permute-start | bytes 49160 | tf_op jit(solution)/shard_map/ppermute | solution.py:550
  92.3 9.1 %collective-permute-start.20 = (f32[8,512]{1,0:T(8,128)S(1)}, f32[8,512]{1,0:T(8,128)S(1)}, u32[]{:S(2)}, u32[]{:S(2)}) collective-permute-start(f32[8,512]{1,0:T(8,128)S(1)} %get-tuple-element.110), channel_id=1, source_target_pairs={{0,1},{1,0},{2,3},{3,2},{4,5},{5,4},{6,7},{7,6},{8,9},{9,8},{10,11... | collective-permute-start | bytes 49160 | tf_op jit(solution)/shard_map/ppermute | solution.py:551
  102.3 7.9 %collective-permute-start.21 = (f32[8,512]{1,0:T(8,128)S(1)}, f32[8,512]{1,0:T(8,128)S(1)}, u32[]{:S(2)}, u32[]{:S(2)}) collective-permute-start(f32[8,512]{1,0:T(8,128)S(1)} %get-tuple-element.115), channel_id=1, source_target_pairs={{1,2},{3,4},{5,6},{7,8},{9,10},{11,12},{13,14},{15,16},{17,18},{19... | collective-permute-start | bytes 49160 | tf_op jit(solution)/shard_map/ppermute | solution.py:550
  111.6 8.5 %collective-permute-start.23 = (f32[8,512]{1,0:T(8,128)S(1)}, f32[8,512]{1,0:T(8,128)S(1)}, u32[]{:S(2)}, u32[]{:S(2)}) collective-permute-start(f32[8,512]{1,0:T(8,128)S(1)} %get-tuple-element.121), channel_id=1, source_target_pairs={{1,2},{3,4},{5,6},{7,8},{9,10},{11,12},{13,14},{15,16},{17,18},{19... | collective-permute-start | bytes 49160 | tf_op jit(solution)/shard_map/ppermute | solution.py:550
  113.5 6.6 %collective-permute-start.24 = (f32[8,512]{1,0:T(8,128)S(1)}, f32[8,512]{1,0:T(8,128)S(1)}, u32[]{:S(2)}, u32[]{:S(2)}) collective-permute-start(f32[8,512]{1,0:T(8,128)S(1)} %get-tuple-element.122), channel_id=1, source_target_pairs={{0,1},{1,0},{2,3},{3,2},{4,5},{5,4},{6,7},{7,6},{8,9},{9,8},{10,11... | collective-permute-start | bytes 49160 | tf_op jit(solution)/shard_map/ppermute | solution.py:551
  121.0 9.0 %collective-permute-start.25 = (f32[8,512]{1,0:T(8,128)S(1)}, f32[8,512]{1,0:T(8,128)S(1)}, u32[]{:S(2)}, u32[]{:S(2)}) collective-permute-start(f32[8,512]{1,0:T(8,128)S(1)} %get-tuple-element.127), channel_id=1, source_target_pairs={{1,2},{3,4},{5,6},{7,8},{9,10},{11,12},{13,14},{15,16},{17,18},{19... | collective-permute-start | bytes 49160 | tf_op jit(solution)/shard_map/ppermute | solution.py:550
  122.9 7.0 %collective-permute-start.26 = (f32[8,512]{1,0:T(8,128)S(1)}, f32[8,512]{1,0:T(8,128)S(1)}, u32[]{:S(2)}, u32[]{:S(2)}) collective-permute-start(f32[8,512]{1,0:T(8,128)S(1)} %get-tuple-element.128), channel_id=1, source_target_pairs={{0,1},{1,0},{2,3},{3,2},{4,5},{5,4},{6,7},{7,6},{8,9},{9,8},{10,11... | collective-permute-start | bytes 49160 | tf_op jit(solution)/shard_map/ppermute | solution.py:551
  131.3 7.9 %collective-permute-start.27 = (f32[8,512]{1,0:T(8,128)S(1)}, f32[8,512]{1,0:T(8,128)S(1)}, u32[]{:S(2)}, u32[]{:S(2)}) collective-permute-start(f32[8,512]{1,0:T(8,128)S(1)} %get-tuple-element.135), channel_id=1, source_target_pairs={{1,2},{3,4},{5,6},{7,8},{9,10},{11,12},{13,14},{15,16},{17,18},{19... | collective-permute-start | bytes 49160 | tf_op jit(solution)/shard_map/ppermute | solution.py:550
  140.5 8.0 %collective-permute-start.29 = (f32[8,512]{1,0:T(8,128)S(1)}, f32[8,512]{1,0:T(8,128)S(1)}, u32[]{:S(2)}, u32[]{:S(2)}) collective-permute-start(f32[8,512]{1,0:T(8,128)S(1)} %get-tuple-element.141), channel_id=1, source_target_pairs={{1,2},{3,4},{5,6},{7,8},{9,10},{11,12},{13,14},{15,16},{17,18},{19... | collective-permute-start | bytes 49160 | tf_op jit(solution)/shard_map/ppermute | solution.py:550
  142.5 6.1 %collective-permute-start.30 = (f32[8,512]{1,0:T(8,128)S(1)}, f32[8,512]{1,0:T(8,128)S(1)}, u32[]{:S(2)}, u32[]{:S(2)}) collective-permute-start(f32[8,512]{1,0:T(8,128)S(1)} %get-tuple-element.142), channel_id=1, source_target_pairs={{0,1},{1,0},{2,3},{3,2},{4,5},{5,4},{6,7},{7,6},{8,9},{9,8},{10,11... | collective-permute-start | bytes 49160 | tf_op jit(solution)/shard_map/ppermute | solution.py:551
  150.4 40.2 %all-to-all-start.1 = ((f32[4,2,6,8,512]{4,3,2,1,0:T(8,128)}), f32[4,2,6,8,512]{4,3,2,1,0:T(8,128)S(1)}, u32[]{:S(2)}, u32[]{:S(2)}) async-start(f32[4,2,6,8,512]{4,3,2,1,0:T(8,128)} %pad_maximum_fusion.1), calls=%async_computation.1 | async-start | bytes 1572864 | tf_op jit(solution)/shard_map/all_to_all | solution.py:601
  155.3 8.4 %collective-permute-start.31 = (f32[8,512]{1,0:T(8,128)S(1)}, f32[8,512]{1,0:T(8,128)S(1)}, u32[]{:S(2)}, u32[]{:S(2)}) collective-permute-start(f32[8,512]{1,0:T(8,128)S(1)} %get-tuple-element.150), channel_id=1, source_target_pairs={{1,2},{3,4},{5,6},{7,8},{9,10},{11,12},{13,14},{15,16},{17,18},{19... | collective-permute-start | bytes 49160 | tf_op jit(solution)/shard_map/ppermute | solution.py:550
  157.2 6.5 %collective-permute-start.32 = (f32[8,512]{1,0:T(8,128)S(1)}, f32[8,512]{1,0:T(8,128)S(1)}, u32[]{:S(2)}, u32[]{:S(2)}) collective-permute-start(f32[8,512]{1,0:T(8,128)S(1)} %get-tuple-element.151), channel_id=1, source_target_pairs={{0,1},{1,0},{2,3},{3,2},{4,5},{5,4},{6,7},{7,6},{8,9},{9,8},{10,11... | collective-permute-start | bytes 49160 | tf_op jit(solution)/shard_map/ppermute | solution.py:551
  167.2 23.4 %collective-permute-start.40 = (f32[2,6,8,512]{3,2,1,0:T(8,128)S(1)}, f32[2,6,8,512]{3,2,1,0:T(8,128)S(1)}, u32[]{:S(2)}, u32[]{:S(2)}) collective-permute-start(f32[2,6,8,512]{3,2,1,0:T(8,128)S(1)} %get-tuple-element.155.lam.refs_4_), channel_id=1, source_target_pairs={{192,0},{193,1},{194,2},{195,3},{196,4},{197,5},{198,6},{199,7},{2... | collective-permute-start | bytes 589832 | tf_op jit(solution)/shard_map/ppermute | solution.py:604
  168.5 22.1 %collective-permute-start.39 = (f32[2,6,8,512]{3,2,1,0:T(8,128)S(1)}, f32[2,6,8,512]{3,2,1,0:T(8,128)S(1)}, u32[]{:S(2)}, u32[]{:S(2)}) collective-permute-start(f32[2,6,8,512]{3,2,1,0:T(8,128)S(1)} %get-tuple-element.155.lam.refs_4_), channel_id=1, source_target_pairs={{128,0},{129,1},{130,2},{131,3},{132,4},{133,5},{134,6},{135,7},{1... | collective-permute-start | bytes 589832 | tf_op jit(solution)/shard_map/ppermute | solution.py:604
  169.8 20.8 %collective-permute-start.38 = (f32[2,6,8,512]{3,2,1,0:T(8,128)S(1)}, f32[2,6,8,512]{3,2,1,0:T(8,128)S(1)}, u32[]{:S(2)}, u32[]{:S(2)}) collective-permute-start(f32[2,6,8,512]{3,2,1,0:T(8,128)S(1)} %get-tuple-element.155.lam.refs_4_), channel_id=1, source_target_pairs={{64,0},{65,1},{66,2},{67,3},{68,4},{69,5},{70,6},{71,7},{72,8},{73... | collective-permute-start | bytes 589832 | tf_op jit(solution)/shard_map/ppermute | solution.py:604
  171.1 6.9 %collective-permute-start.33 = (f32[8,512]{1,0:T(8,128)S(1)}, f32[8,512]{1,0:T(8,128)S(1)}, u32[]{:S(2)}, u32[]{:S(2)}) collective-permute-start(f32[8,512]{1,0:T(8,128)S(1)} %get-tuple-element.156), channel_id=1, source_target_pairs={{1,2},{3,4},{5,6},{7,8},{9,10},{11,12},{13,14},{15,16},{17,18},{19... | collective-permute-start | bytes 49160 | tf_op jit(solution)/shard_map/ppermute | solution.py:550
  182.3 6.3 %collective-permute-start.36 = (f32[4,8,512]{2,1,0:T(8,128)S(1)}, f32[4,8,512]{2,1,0:T(8,128)S(1)}, u32[]{:S(2)}, u32[]{:S(2)}) collective-permute-start(f32[4,8,512]{2,1,0:T(8,128)S(1)} %shard_map.118.refs_0_), channel_id=1, source_target_pairs={{0,128},{64,192},{128,0},{192,64},{1,129},{65,193},{129,1},{193,65... | collective-permute-start | bytes 196616 | tf_op jit(solution)/shard_map/ppermute | solution.py:606
  (28 other events, 252.0 us)

commit v4 on v3

--- a/solution.py
+++ b/solution.py
@@ -139,7 +139,7 @@
     return scale_a * jnp.concatenate(rows_a + rest, axis=0), -scale_b * jnp.concatenate(rows_b + rest, axis=0)
 
 
-def pair_adjoint_far(xa, xb, ga, marks):
+def pair_adjoint_far(xa, xb, ga, marks, scale):
     from_b = differences(xb, xa, marks)
     g_sub = spread(jnp.concatenate(pieces(ga), axis=0), marks)
     rows = []
@@ -148,7 +148,7 @@
         for j in range(16):
             total = pair_sum(total, [block(from_b, j, 3 * t + c) for c in range(3)], [block(g_sub, j, 3 * t + c) for c in range(3)])
         rows += total
-    return -SCALE * stacked(rows)
+    return -scale * stacked(rows)
 
 
 def pair_sum(total, d, g):
@@ -304,7 +304,7 @@
     state, halo_x, halo_p, kk, lam_out, send_x, send_p, kd = refs[:8]
     refs = refs[8:]
     full = refs.pop(0) if keep else None
-    tiles, grads, acc_b = refs
+    tiles, grads, acc_b, packed = refs
     first = meta[0, META_C] == 0
     row, base = lists(meta, step)
     count = meta[row, base + 2 * SLOTS]
@@ -350,10 +350,12 @@
     def far(b):
         return jnp.logical_or(b < NB, b >= NB * (EXT - 1))
 
-    hits = [jnp.logical_and(p < count, far(meta[row, base + SLOTS + p])) for p in range(SLOTS)]
-    some = functools.reduce(jnp.logical_or, hits)
-
-    @pl.when(some)
+    found = jnp.int32(0)
+    for p in range(SLOTS):
+        packed[found] = p
+        found = found + jnp.logical_and(p < count, far(meta[row, base + SLOTS + p])).astype(jnp.int32)
+
+    @pl.when(found > 0)
     def _():
         acc_b[...] = jnp.zeros(acc_b.shape, F32)
         fill_tiles(tiles, lambda t, c: state[t, c])
@@ -361,21 +363,23 @@
         fill_tiles(grads, lambda t, c: force[3 * t + c])
         marks = selectors()
 
-        def slot(p, carry):
-            a = meta[row, base + p]
-            b = meta[row, base + SLOTS + p]
-
-            @pl.when(far(b))
-            def _():
+        def group(i, carry):
+            results = []
+            for q in range(2):
+                n = 2 * i + q
+                p = packed[jnp.minimum(n, found - 1)]
+                a = meta[row, base + p]
+                b = meta[row, base + SLOTS + p]
                 at = tile_start(a // NB + 1, lax.rem(a, NB))
                 bt = tile_start(b // NB, lax.rem(b, NB))
-                con_b = pair_adjoint_far(tiles[pl.ds(at, 8), :], tiles[pl.ds(bt, 8), :], grads[pl.ds(at, 8), :], marks)
                 out = pl.multiple_of(8 * jnp.where(b < NB, b, b - NB * (EXT - 2)), 8)
-                acc_b[pl.ds(out, 8), :] += con_b
-
+                scale = jnp.where(n < found, SCALE, 0.0)
+                results.append((out, pair_adjoint_far(tiles[pl.ds(at, 8), :], tiles[pl.ds(bt, 8), :], grads[pl.ds(at, 8), :], marks, scale)))
+            for out, value in results:
+                acc_b[pl.ds(out, 8), :] += value
             return carry
 
-        lax.fori_loop(0, count, slot, 0)
+        lax.fori_loop(0, (found + 1) // 2, group, 0)
         more_up = jnp.concatenate([acc_b[8 * b : 8 * b + 8, :] for b in range(NB)], axis=1)
         more_down = jnp.concatenate([acc_b[8 * (NB + b) : 8 * (NB + b) + 8, :] for b in range(NB)], axis=1)
         send_x[...] += jnp.where(first, more_up, more_down)
@@ -580,7 +584,7 @@
             functools.partial(backward_outer, step, opening, keep),
             [STATE, HALO, HALO, HALO] + [STATE] * keep,
             [meta, lam, *got, states[step], *halos[step], kk],
-            [TILES, TILES, pltpu.VMEM((2 * NB * 8, 128), F32)],
+            [TILES, TILES, pltpu.VMEM((2 * NB * 8, 128), F32), pltpu.SMEM((SLOTS + 1,), jnp.int32)],
         )
         fulls = rest + fulls
         got = exchange(send_x, send_p)

time: 196 us -> 196 us (level)
  no operation moved by 1% of the time
where the time goes in v4:
time: 196 us; the launch traced here: 193 us
  starting transfers between devices  118 us (60%)
  Pallas kernels  48.8 us (25%)
  waiting for transfers between devices  16.6 us (8%)
  local copies, waits for them, and re-layouts  4.91 us (3%)
  other arithmetic  3.28 us (2%)
    ppermute x16, starting transfers between devices, exchange(): got_p = lax.ppermute(send_p, 'space', near)  61.7 us
    pallas_call x35, Pallas kernels, call(): pl.pallas_call(body, out_shape=[space(o.shape, o.dtype) for space, o in z...  48.8 us
    ppermute x16, starting transfers between devices, exchange(): got_x = lax.ppermute(send_x, 'space', cross)  31.2 us
    ppermute x16, waiting for transfers between devices, exchange(): got_x = lax.ppermute(send_x, 'space', cross)  11.5 us
    ppermute x3, starting transfers between devices, on_device(): lax.ppermute(shared, 'section', [(i, (i + k) % sections) for i in range(s...  7.09 us
    all_to_all x1, starting transfers between devices, on_device(): lax.all_to_all(jnp.stack([fulls[0], *fulls]), 'section', 0, 0, tiled=True)  4.88 us
    ppermute x3, starting transfers between devices, on_device(): lax.ppermute(own_list, 'section', [(i, (i + k) % sections) for i in range...  4.61 us
    all_to_all x1, starting transfers between devices, on_device(): exit_state = lax.all_to_all(jnp.stack(exits), 'section', 0, 0, tiled=True)  4.21 us
  transfers between devices with their start and end apart: 43, of which 12 were waited for; matrix products, arithmetic and copies ran while one was open for 1% of the time, Pallas kernels for 19%

profile of v4, /device:TPU:102, one launch (start us, length us, event | category | flops | bytes accessed | tf_op | source)
XLA Modules:
  0.0 192.6 jit_solution(1328095583377693365)
XLA Ops:
  3.0 3.0 %collective-permute-start.2 = (s32[1,64]{1,0:T(1,128)S(1)}, s32[1,64]{1,0:T(1,128)S(1)}, u32[]{:S(2)}, u32[]{:S(2)}) collective-permute-start(s32[1,64]{1,0:T(1,128)S(1)} %get-tuple-element.162), channel_id=1, source_target_pairs={{0,192},{64,0},{128,64},{192,128},{1,193},{65,1},{129,65},{193,129... | collective-permute-start | bytes 776 | tf_op jit(solution)/shard_map/ppermute | solution.py:546
  11.0 3.2 %collective-permute-start.4 = (f32[8,512]{1,0:T(8,128)S(1)}, f32[8,512]{1,0:T(8,128)S(1)}, u32[]{:S(2)}, u32[]{:S(2)}) collective-permute-start(f32[8,512]{1,0:T(8,128)S(1)} %get-tuple-element.84), channel_id=1, source_target_pairs={{0,1},{1,0},{2,3},{3,2},{4,5},{5,4},{6,7},{7,6},{8,9},{9,8},{10,11... | collective-permute-start | bytes 49160 | tf_op jit(solution)/shard_map/ppermute | solution.py:555
  23.9 3.6 %collective-permute-start.8 = (f32[8,512]{1,0:T(8,128)S(1)}, f32[8,512]{1,0:T(8,128)S(1)}, u32[]{:S(2)}, u32[]{:S(2)}) collective-permute-start(f32[8,512]{1,0:T(8,128)S(1)} %get-tuple-element.90), channel_id=1, source_target_pairs={{0,1},{1,0},{2,3},{3,2},{4,5},{5,4},{6,7},{7,6},{8,9},{9,8},{10,11... | collective-permute-start | bytes 49160 | tf_op jit(solution)/shard_map/ppermute | solution.py:555
  33.7 3.4 %collective-permute-start.10 = (f32[8,512]{1,0:T(8,128)S(1)}, f32[8,512]{1,0:T(8,128)S(1)}, u32[]{:S(2)}, u32[]{:S(2)}) collective-permute-start(f32[8,512]{1,0:T(8,128)S(1)} %get-tuple-element.93), channel_id=1, source_target_pairs={{0,1},{1,0},{2,3},{3,2},{4,5},{5,4},{6,7},{7,6},{8,9},{9,8},{10,11... | collective-permute-start | bytes 49160 | tf_op jit(solution)/shard_map/ppermute | solution.py:555
  43.0 3.4 %collective-permute-start.12 = (f32[8,512]{1,0:T(8,128)S(1)}, f32[8,512]{1,0:T(8,128)S(1)}, u32[]{:S(2)}, u32[]{:S(2)}) collective-permute-start(f32[8,512]{1,0:T(8,128)S(1)} %get-tuple-element.96), channel_id=1, source_target_pairs={{0,1},{1,0},{2,3},{3,2},{4,5},{5,4},{6,7},{7,6},{8,9},{9,8},{10,11... | collective-permute-start | bytes 49160 | tf_op jit(solution)/shard_map/ppermute | solution.py:555
  52.3 3.8 %collective-permute-start.14 = (f32[8,512]{1,0:T(8,128)S(1)}, f32[8,512]{1,0:T(8,128)S(1)}, u32[]{:S(2)}, u32[]{:S(2)}) collective-permute-start(f32[8,512]{1,0:T(8,128)S(1)} %get-tuple-element.99), channel_id=1, source_target_pairs={{0,1},{1,0},{2,3},{3,2},{4,5},{5,4},{6,7},{7,6},{8,9},{9,8},{10,11... | collective-permute-start | bytes 49160 | tf_op jit(solution)/shard_map/ppermute | solution.py:555
  62.0 3.4 %collective-permute-start.16 = (f32[8,512]{1,0:T(8,128)S(1)}, f32[8,512]{1,0:T(8,128)S(1)}, u32[]{:S(2)}, u32[]{:S(2)}) collective-permute-start(f32[8,512]{1,0:T(8,128)S(1)} %get-tuple-element.102), channel_id=1, source_target_pairs={{0,1},{1,0},{2,3},{3,2},{4,5},{5,4},{6,7},{7,6},{8,9},{9,8},{10,11... | collective-permute-start | bytes 49160 | tf_op jit(solution)/shard_map/ppermute | solution.py:555
  71.5 4.1 %collective-permute-start.18 = (f32[8,512]{1,0:T(8,128)S(1)}, f32[8,512]{1,0:T(8,128)S(1)}, u32[]{:S(2)}, u32[]{:S(2)}) collective-permute-start(f32[8,512]{1,0:T(8,128)S(1)} %get-tuple-element.105), channel_id=1, source_target_pairs={{0,1},{1,0},{2,3},{3,2},{4,5},{5,4},{6,7},{7,6},{8,9},{9,8},{10,11... | collective-permute-start | bytes 49160 | tf_op jit(solution)/shard_map/ppermute | solution.py:555
  83.1 4.2 %all-to-all-start = ((f32[4,2,6,8,512]{4,3,2,1,0:T(8,128)}), f32[4,2,6,8,512]{4,3,2,1,0:T(8,128)}, u32[]{:S(2)}, u32[]{:S(2)}) async-start(f32[4,2,6,8,512]{4,3,2,1,0:T(8,128)} %pad_maximum_fusion), calls=%async_computation | async-start | bytes 1572864 | tf_op jit(solution)/shard_map/all_to_all | solution.py:575
  89.8 2.5 %collective-permute-start.19 = (f32[8,512]{1,0:T(8,128)S(1)}, f32[8,512]{1,0:T(8,128)S(1)}, u32[]{:S(2)}, u32[]{:S(2)}) collective-permute-start(f32[8,512]{1,0:T(8,128)S(1)} %get-tuple-element.109), channel_id=1, source_target_pairs={{1,2},{3,4},{5,6},{7,8},{9,10},{11,12},{13,14},{15,16},{17,18},{19... | collective-permute-start | bytes 49160 | tf_op jit(solution)/shard_map/ppermute | solution.py:554
  92.3 6.6 %collective-permute-start.20 = (f32[8,512]{1,0:T(8,128)S(1)}, f32[8,512]{1,0:T(8,128)S(1)}, u32[]{:S(2)}, u32[]{:S(2)}) collective-permute-start(f32[8,512]{1,0:T(8,128)S(1)} %get-tuple-element.110), channel_id=1, source_target_pairs={{0,1},{1,0},{2,3},{3,2},{4,5},{5,4},{6,7},{7,6},{8,9},{9,8},{10,11... | collective-permute-start | bytes 49160 | tf_op jit(solution)/shard_map/ppermute | solution.py:555
  104.3 4.5 %collective-permute-start.22 = (f32[8,512]{1,0:T(8,128)S(1)}, f32[8,512]{1,0:T(8,128)S(1)}, u32[]{:S(2)}, u32[]{:S(2)}) collective-permute-start(f32[8,512]{1,0:T(8,128)S(1)} %get-tuple-element.116), channel_id=1, source_target_pairs={{0,1},{1,0},{2,3},{3,2},{4,5},{5,4},{6,7},{7,6},{8,9},{9,8},{10,11... | collective-permute-start | bytes 49160 | tf_op jit(solution)/shard_map/ppermute | solution.py:555
  113.7 4.3 %collective-permute-start.24 = (f32[8,512]{1,0:T(8,128)S(1)}, f32[8,512]{1,0:T(8,128)S(1)}, u32[]{:S(2)}, u32[]{:S(2)}) collective-permute-start(f32[8,512]{1,0:T(8,128)S(1)} %get-tuple-element.122), channel_id=1, source_target_pairs={{0,1},{1,0},{2,3},{3,2},{4,5},{5,4},{6,7},{7,6},{8,9},{9,8},{10,11... | collective-permute-start | bytes 49160 | tf_op jit(solution)/shard_map/ppermute | solution.py:555
  118.0 2.2 %shard_map.105 = (f32[2,6,8,512]{3,2,1,0:T(8,128)S(1)}, f32[2,8,512]{2,1,0:T(8,128)S(1)}) custom-call(s32[4,64]{1,0:T(4,128)} %pad_add_fusion.meta, f32[2,6,8,512]{3,2,1,0:T(8,128)S(1)} %get-tuple-element.117.lam, f32[2,6,8,512]{3,2,1,0:T(8,128)S(1)} %get-tuple-element.97.state.refs_2_, f32[8,512]{1,0:T(8,128)S(1)} %collective-permute-done.13.halo_x.refs_3_, ...), custom_call_target="tpu_custom_call" | custom-call | flops 8000000 | bytes 262144 | tf_op jit(solution)/shard_map/pallas_call | solution.py:520
  123.0 4.3 %collective-permute-start.26 = (f32[8,512]{1,0:T(8,128)S(1)}, f32[8,512]{1,0:T(8,128)S(1)}, u32[]{:S(2)}, u32[]{:S(2)}) collective-permute-start(f32[8,512]{1,0:T(8,128)S(1)} %get-tuple-element.128), channel_id=1, source_target_pairs={{0,1},{1,0},{2,3},{3,2},{4,5},{5,4},{6,7},{7,6},{8,9},{9,8},{10,11... | collective-permute-start | bytes 49160 | tf_op jit(solution)/shard_map/ppermute | solution.py:555
  127.3 2.8 %shard_map.107 = (f32[2,6,8,512]{3,2,1,0:T(8,128)S(1)}, f32[2,8,512]{2,1,0:T(8,128)S(1)}) custom-call(s32[4,64]{1,0:T(4,128)} %pad_add_fusion.meta, f32[2,6,8,512]{3,2,1,0:T(8,128)S(1)} %get-tuple-element.123.lam, f32[2,6,8,512]{3,2,1,0:T(8,128)S(1)} %get-tuple-element.94.state.refs_2_, f32[8,512]{1,0:T(8,128)S(1)} %collective-permute-done.11.halo_x.refs_3_, ...), custom_call_target="tpu_custom_call" | custom-call | flops 8000000 | bytes 262144 | tf_op jit(solution)/shard_map/pallas_call | solution.py:520
  133.4 3.1 %collective-permute-start.28 = (f32[8,512]{1,0:T(8,128)S(1)}, f32[8,512]{1,0:T(8,128)S(1)}, u32[]{:S(2)}, u32[]{:S(2)}) collective-permute-start(f32[8,512]{1,0:T(8,128)S(1)} %get-tuple-element.136), channel_id=1, source_target_pairs={{0,1},{1,0},{2,3},{3,2},{4,5},{5,4},{6,7},{7,6},{8,9},{9,8},{10,11... | collective-permute-start | bytes 49160 | tf_op jit(solution)/shard_map/ppermute | solution.py:555
  136.5 2.7 %shard_map.111 = (f32[2,6,8,512]{3,2,1,0:T(8,128)S(1)}, f32[2,8,512]{2,1,0:T(8,128)S(1)}, f32[4,2,6,8,512]{4,3,2,1,0:T(8,128)}) custom-call(s32[4,64]{1,0:T(4,128)} %pad_add_fusion.meta, f32[2,6,8,512]{3,2,1,0:T(8,128)S(1)} %get-tuple-element.129.lam, f32[2,6,8,512]{3,2,1,0:T(8,128)S(1)} %get-tuple-element.91.state.refs_2_, ...), custom_call_target="tpu_custom_call" | custom-call | flops 8000000 | bytes 262144 | tf_op jit(solution)/shard_map/pallas_call | solution.py:520
  142.8 3.7 %collective-permute-start.30 = (f32[8,512]{1,0:T(8,128)S(1)}, f32[8,512]{1,0:T(8,128)S(1)}, u32[]{:S(2)}, u32[]{:S(2)}) collective-permute-start(f32[8,512]{1,0:T(8,128)S(1)} %get-tuple-element.142), channel_id=1, source_target_pairs={{0,1},{1,0},{2,3},{3,2},{4,5},{5,4},{6,7},{7,6},{8,9},{9,8},{10,11... | collective-permute-start | bytes 49160 | tf_op jit(solution)/shard_map/ppermute | solution.py:555
  150.6 4.9 %all-to-all-start.1 = ((f32[4,2,6,8,512]{4,3,2,1,0:T(8,128)}), f32[4,2,6,8,512]{4,3,2,1,0:T(8,128)S(1)}, u32[]{:S(2)}, u32[]{:S(2)}) async-start(f32[4,2,6,8,512]{4,3,2,1,0:T(8,128)} %pad_maximum_fusion.1), calls=%async_computation.1 | async-start | bytes 1572864 | tf_op jit(solution)/shard_map/all_to_all | solution.py:605
  157.4 4.8 %collective-permute-start.32 = (f32[8,512]{1,0:T(8,128)S(1)}, f32[8,512]{1,0:T(8,128)S(1)}, u32[]{:S(2)}, u32[]{:S(2)}) collective-permute-start(f32[8,512]{1,0:T(8,128)S(1)} %get-tuple-element.151), channel_id=1, source_target_pairs={{0,1},{1,0},{2,3},{3,2},{4,5},{5,4},{6,7},{7,6},{8,9},{9,8},{10,11... | collective-permute-start | bytes 49160 | tf_op jit(solution)/shard_map/ppermute | solution.py:555
  173.2 4.9 %collective-permute-start.34 = (f32[8,512]{1,0:T(8,128)S(1)}, f32[8,512]{1,0:T(8,128)S(1)}, u32[]{:S(2)}, u32[]{:S(2)}) collective-permute-start(f32[8,512]{1,0:T(8,128)S(1)} %get-tuple-element.157), channel_id=1, source_target_pairs={{0,1},{1,0},{2,3},{3,2},{4,5},{5,4},{6,7},{7,6},{8,9},{9,8},{10,11... | collective-permute-start | bytes 49160 | tf_op jit(solution)/shard_map/ppermute | solution.py:555
  179.7 2.7 %collective-permute-start.37 = (f32[4,8,512]{2,1,0:T(8,128)S(1)}, f32[4,8,512]{2,1,0:T(8,128)S(1)}, u32[]{:S(2)}, u32[]{:S(2)}) collective-permute-start(f32[4,8,512]{2,1,0:T(8,128)S(1)} %shard_map.118.refs_0_), channel_id=1, source_target_pairs={{0,192},{64,0},{128,64},{192,128},{1,193},{65,1},{129,65},{193,129... | collective-permute-start | bytes 196616 | tf_op jit(solution)/shard_map/ppermute | solution.py:610
  184.9 2.3 %collective-permute-start.35 = (f32[4,8,512]{2,1,0:T(8,128)S(1)}, f32[4,8,512]{2,1,0:T(8,128)S(1)}, u32[]{:S(2)}, u32[]{:S(2)}) collective-permute-start(f32[4,8,512]{2,1,0:T(8,128)S(1)} %shard_map.118.refs_0_), channel_id=1, source_target_pairs={{0,64},{64,128},{128,192},{192,0},{1,65},{65,129},{129,193},{193,1... | collective-permute-start | bytes 196616 | tf_op jit(solution)/shard_map/ppermute | solution.py:610
  (126 shorter events, 102.6 us)
Async XLA Ops:
  3.0 11.2 %collective-permute-start.2 = (s32[1,64]{1,0:T(1,128)S(1)}, s32[1,64]{1,0:T(1,128)S(1)}, u32[]{:S(2)}, u32[]{:S(2)}) collective-permute-start(s32[1,64]{1,0:T(1,128)S(1)} %get-tuple-element.162), channel_id=1, source_target_pairs={{0,192},{64,0},{128,64},{192,128},{1,193},{65,1},{129,65},{193,129... | collective-permute-start | bytes 776 | tf_op jit(solution)/shard_map/ppermute | solution.py:546
  6.0 8.2 %collective-permute-start.1 = (s32[1,64]{1,0:T(1,128)S(1)}, s32[1,64]{1,0:T(1,128)S(1)}, u32[]{:S(2)}, u32[]{:S(2)}) collective-permute-start(s32[1,64]{1,0:T(1,128)S(1)} %get-tuple-element.162), channel_id=1, source_target_pairs={{0,128},{64,192},{128,0},{192,64},{1,129},{65,193},{129,1},{193,65... | collective-permute-start | bytes 776 | tf_op jit(solution)/shard_map/ppermute | solution.py:546
  6.6 7.6 %collective-permute-start = (s32[1,64]{1,0:T(1,128)S(1)}, s32[1,64]{1,0:T(1,128)S(1)}, u32[]{:S(2)}, u32[]{:S(2)}) collective-permute-start(s32[1,64]{1,0:T(1,128)S(1)} %get-tuple-element.162), channel_id=1, source_target_pairs={{0,64},{64,128},{128,192},{192,0},{1,65},{65,129},{129,193},{193,1... | collective-permute-start | bytes 776 | tf_op jit(solution)/shard_map/ppermute | solution.py:546
  9.1 7.6 %collective-permute-start.3 = (f32[8,512]{1,0:T(8,128)S(1)}, f32[8,512]{1,0:T(8,128)S(1)}, u32[]{:S(2)}, u32[]{:S(2)}) collective-permute-start(f32[8,512]{1,0:T(8,128)S(1)} %get-tuple-element.82), channel_id=1, source_target_pairs={{1,2},{3,4},{5,6},{7,8},{9,10},{11,12},{13,14},{15,16},{17,18},{19... | collective-permute-start | bytes 49160 | tf_op jit(solution)/shard_map/ppermute | solution.py:554
  71.5 6.1 %collective-permute-start.18 = (f32[8,512]{1,0:T(8,128)S(1)}, f32[8,512]{1,0:T(8,128)S(1)}, u32[]{:S(2)}, u32[]{:S(2)}) collective-permute-start(f32[8,512]{1,0:T(8,128)S(1)} %get-tuple-element.105), channel_id=1, source_target_pairs={{0,1},{1,0},{2,3},{3,2},{4,5},{5,4},{6,7},{7,6},{8,9},{9,8},{10,11... | collective-permute-start | bytes 49160 | tf_op jit(solution)/shard_map/ppermute | solution.py:555
  83.1 53.4 %all-to-all-start = ((f32[4,2,6,8,512]{4,3,2,1,0:T(8,128)}), f32[4,2,6,8,512]{4,3,2,1,0:T(8,128)}, u32[]{:S(2)}, u32[]{:S(2)}) async-start(f32[4,2,6,8,512]{4,3,2,1,0:T(8,128)} %pad_maximum_fusion), calls=%async_computation | async-start | bytes 1572864 | tf_op jit(solution)/shard_map/all_to_all | solution.py:575
  89.8 11.6 %collective-permute-start.19 = (f32[8,512]{1,0:T(8,128)S(1)}, f32[8,512]{1,0:T(8,128)S(1)}, u32[]{:S(2)}, u32[]{:S(2)}) collective-permute-start(f32[8,512]{1,0:T(8,128)S(1)} %get-tuple-element.109), channel_id=1, source_target_pairs={{1,2},{3,4},{5,6},{7,8},{9,10},{11,12},{13,14},{15,16},{17,18},{19... | collective-permute-start | bytes 49160 | tf_op jit(solution)/shard_map/ppermute | solution.py:554
  92.3 9.1 %collective-permute-start.20 = (f32[8,512]{1,0:T(8,128)S(1)}, f32[8,512]{1,0:T(8,128)S(1)}, u32[]{:S(2)}, u32[]{:S(2)}) collective-permute-start(f32[8,512]{1,0:T(8,128)S(1)} %get-tuple-element.110), channel_id=1, source_target_pairs={{0,1},{1,0},{2,3},{3,2},{4,5},{5,4},{6,7},{7,6},{8,9},{9,8},{10,11... | collective-permute-start | bytes 49160 | tf_op jit(solution)/shard_map/ppermute | solution.py:555
  102.3 8.0 %collective-permute-start.21 = (f32[8,512]{1,0:T(8,128)S(1)}, f32[8,512]{1,0:T(8,128)S(1)}, u32[]{:S(2)}, u32[]{:S(2)}) collective-permute-start(f32[8,512]{1,0:T(8,128)S(1)} %get-tuple-element.115), channel_id=1, source_target_pairs={{1,2},{3,4},{5,6},{7,8},{9,10},{11,12},{13,14},{15,16},{17,18},{19... | collective-permute-start | bytes 49160 | tf_op jit(solution)/shard_map/ppermute | solution.py:554
  104.3 6.0 %collective-permute-start.22 = (f32[8,512]{1,0:T(8,128)S(1)}, f32[8,512]{1,0:T(8,128)S(1)}, u32[]{:S(2)}, u32[]{:S(2)}) collective-permute-start(f32[8,512]{1,0:T(8,128)S(1)} %get-tuple-element.116), channel_id=1, source_target_pairs={{0,1},{1,0},{2,3},{3,2},{4,5},{5,4},{6,7},{7,6},{8,9},{9,8},{10,11... | collective-permute-start | bytes 49160 | tf_op jit(solution)/shard_map/ppermute | solution.py:555
  111.7 8.4 %collective-permute-start.23 = (f32[8,512]{1,0:T(8,128)S(1)}, f32[8,512]{1,0:T(8,128)S(1)}, u32[]{:S(2)}, u32[]{:S(2)}) collective-permute-start(f32[8,512]{1,0:T(8,128)S(1)} %get-tuple-element.121), channel_id=1, source_target_pairs={{1,2},{3,4},{5,6},{7,8},{9,10},{11,12},{13,14},{15,16},{17,18},{19... | collective-permute-start | bytes 49160 | tf_op jit(solution)/shard_map/ppermute | solution.py:554
  113.7 6.5 %collective-permute-start.24 = (f32[8,512]{1,0:T(8,128)S(1)}, f32[8,512]{1,0:T(8,128)S(1)}, u32[]{:S(2)}, u32[]{:S(2)}) collective-permute-start(f32[8,512]{1,0:T(8,128)S(1)} %get-tuple-element.122), channel_id=1, source_target_pairs={{0,1},{1,0},{2,3},{3,2},{4,5},{5,4},{6,7},{7,6},{8,9},{9,8},{10,11... | collective-permute-start | bytes 49160 | tf_op jit(solution)/shard_map/ppermute | solution.py:555
  121.1 9.0 %collective-permute-start.25 = (f32[8,512]{1,0:T(8,128)S(1)}, f32[8,512]{1,0:T(8,128)S(1)}, u32[]{:S(2)}, u32[]{:S(2)}) collective-permute-start(f32[8,512]{1,0:T(8,128)S(1)} %get-tuple-element.127), channel_id=1, source_target_pairs={{1,2},{3,4},{5,6},{7,8},{9,10},{11,12},{13,14},{15,16},{17,18},{19... | collective-permute-start | bytes 49160 | tf_op jit(solution)/shard_map/ppermute | solution.py:554
  123.0 7.0 %collective-permute-start.26 = (f32[8,512]{1,0:T(8,128)S(1)}, f32[8,512]{1,0:T(8,128)S(1)}, u32[]{:S(2)}, u32[]{:S(2)}) collective-permute-start(f32[8,512]{1,0:T(8,128)S(1)} %get-tuple-element.128), channel_id=1, source_target_pairs={{0,1},{1,0},{2,3},{3,2},{4,5},{5,4},{6,7},{7,6},{8,9},{9,8},{10,11... | collective-permute-start | bytes 49160 | tf_op jit(solution)/shard_map/ppermute | solution.py:555
  131.5 7.8 %collective-permute-start.27 = (f32[8,512]{1,0:T(8,128)S(1)}, f32[8,512]{1,0:T(8,128)S(1)}, u32[]{:S(2)}, u32[]{:S(2)}) collective-permute-start(f32[8,512]{1,0:T(8,128)S(1)} %get-tuple-element.135), channel_id=1, source_target_pairs={{1,2},{3,4},{5,6},{7,8},{9,10},{11,12},{13,14},{15,16},{17,18},{19... | collective-permute-start | bytes 49160 | tf_op jit(solution)/shard_map/ppermute | solution.py:554
  140.9 7.8 %collective-permute-start.29 = (f32[8,512]{1,0:T(8,128)S(1)}, f32[8,512]{1,0:T(8,128)S(1)}, u32[]{:S(2)}, u32[]{:S(2)}) collective-permute-start(f32[8,512]{1,0:T(8,128)S(1)} %get-tuple-element.141), channel_id=1, source_target_pairs={{1,2},{3,4},{5,6},{7,8},{9,10},{11,12},{13,14},{15,16},{17,18},{19... | collective-permute-start | bytes 49160 | tf_op jit(solution)/shard_map/ppermute | solution.py:554
  150.6 40.2 %all-to-all-start.1 = ((f32[4,2,6,8,512]{4,3,2,1,0:T(8,128)}), f32[4,2,6,8,512]{4,3,2,1,0:T(8,128)S(1)}, u32[]{:S(2)}, u32[]{:S(2)}) async-start(f32[4,2,6,8,512]{4,3,2,1,0:T(8,128)} %pad_maximum_fusion.1), calls=%async_computation.1 | async-start | bytes 1572864 | tf_op jit(solution)/shard_map/all_to_all | solution.py:605
  155.5 8.3 %collective-permute-start.31 = (f32[8,512]{1,0:T(8,128)S(1)}, f32[8,512]{1,0:T(8,128)S(1)}, u32[]{:S(2)}, u32[]{:S(2)}) collective-permute-start(f32[8,512]{1,0:T(8,128)S(1)} %get-tuple-element.150), channel_id=1, source_target_pairs={{1,2},{3,4},{5,6},{7,8},{9,10},{11,12},{13,14},{15,16},{17,18},{19... | collective-permute-start | bytes 49160 | tf_op jit(solution)/shard_map/ppermute | solution.py:554
  157.4 6.4 %collective-permute-start.32 = (f32[8,512]{1,0:T(8,128)S(1)}, f32[8,512]{1,0:T(8,128)S(1)}, u32[]{:S(2)}, u32[]{:S(2)}) collective-permute-start(f32[8,512]{1,0:T(8,128)S(1)} %get-tuple-element.151), channel_id=1, source_target_pairs={{0,1},{1,0},{2,3},{3,2},{4,5},{5,4},{6,7},{7,6},{8,9},{9,8},{10,11... | collective-permute-start | bytes 49160 | tf_op jit(solution)/shard_map/ppermute | solution.py:555
  167.4 23.4 %collective-permute-start.40 = (f32[2,6,8,512]{3,2,1,0:T(8,128)S(1)}, f32[2,6,8,512]{3,2,1,0:T(8,128)S(1)}, u32[]{:S(2)}, u32[]{:S(2)}) collective-permute-start(f32[2,6,8,512]{3,2,1,0:T(8,128)S(1)} %get-tuple-element.155.lam.refs_4_), channel_id=1, source_target_pairs={{192,0},{193,1},{194,2},{195,3},{196,4},{197,5},{198,6},{199,7},{2... | collective-permute-start | bytes 589832 | tf_op jit(solution)/shard_map/ppermute | solution.py:608
  168.7 22.1 %collective-permute-start.39 = (f32[2,6,8,512]{3,2,1,0:T(8,128)S(1)}, f32[2,6,8,512]{3,2,1,0:T(8,128)S(1)}, u32[]{:S(2)}, u32[]{:S(2)}) collective-permute-start(f32[2,6,8,512]{3,2,1,0:T(8,128)S(1)} %get-tuple-element.155.lam.refs_4_), channel_id=1, source_target_pairs={{128,0},{129,1},{130,2},{131,3},{132,4},{133,5},{134,6},{135,7},{1... | collective-permute-start | bytes 589832 | tf_op jit(solution)/shard_map/ppermute | solution.py:608
  170.0 20.8 %collective-permute-start.38 = (f32[2,6,8,512]{3,2,1,0:T(8,128)S(1)}, f32[2,6,8,512]{3,2,1,0:T(8,128)S(1)}, u32[]{:S(2)}, u32[]{:S(2)}) collective-permute-start(f32[2,6,8,512]{3,2,1,0:T(8,128)S(1)} %get-tuple-element.155.lam.refs_4_), channel_id=1, source_target_pairs={{64,0},{65,1},{66,2},{67,3},{68,4},{69,5},{70,6},{71,7},{72,8},{73... | collective-permute-start | bytes 589832 | tf_op jit(solution)/shard_map/ppermute | solution.py:608
  171.3 6.9 %collective-permute-start.33 = (f32[8,512]{1,0:T(8,128)S(1)}, f32[8,512]{1,0:T(8,128)S(1)}, u32[]{:S(2)}, u32[]{:S(2)}) collective-permute-start(f32[8,512]{1,0:T(8,128)S(1)} %get-tuple-element.156), channel_id=1, source_target_pairs={{1,2},{3,4},{5,6},{7,8},{9,10},{11,12},{13,14},{15,16},{17,18},{19... | collective-permute-start | bytes 49160 | tf_op jit(solution)/shard_map/ppermute | solution.py:554
  182.4 6.4 %collective-permute-start.36 = (f32[4,8,512]{2,1,0:T(8,128)S(1)}, f32[4,8,512]{2,1,0:T(8,128)S(1)}, u32[]{:S(2)}, u32[]{:S(2)}) collective-permute-start(f32[4,8,512]{2,1,0:T(8,128)S(1)} %shard_map.118.refs_0_), channel_id=1, source_target_pairs={{0,128},{64,192},{128,0},{192,64},{1,129},{65,193},{129,1},{193,65... | collective-permute-start | bytes 196616 | tf_op jit(solution)/shard_map/ppermute | solution.py:610
  (28 other events, 251.9 us)
